TPU v7x, 128 devices: a whole 4x4x4 slice. The times are simulated.
128 devices in a mesh: row: 8 (over z, core), col: 16 (over x, y).
Axes of the slice: x: 4, y: 4, z: 4, core: 2. Of those that a mesh axis runs over, the one named last changes fastest.
Arguments:
- tiles: bfloat16 [8, 16, 128, 128, 128], P('row', 'col'), may hold values from -6 to 6
- tile_row: int32 [8, 16, 128], P('row', 'col'), may hold values from 0 to 127, as said below
- tile_col: int32 [8, 16, 128], P('row', 'col'), may hold values from 0 to 63
- tile_count: int32 [8, 16], P('row', 'col'), may hold values from 16 to 128, as said below
- query_ids: int32 [128], replicated, may hold values from 0 to 131071
- damping: float32 [128], replicated, may hold values from 0.006629126 to 0.026516505
Outputs:
- scores: float32 [131072, 128], P(('row', 'col'))
Inputs may be any that keep to these rules, and one draw needn't show every extreme that they name: `tile_count`: some device holds exactly 128 live slots; slots at or past the count hold arbitrary finite values and are ignored. `tile_row`: positions may repeat within a device; such tiles add. For every device and every col index o, the live slots name at most 4 distinct values among o * 8 to o * 8 + 7, and every device reaches 4 for some o. `query_ids`: ids may repeat.
All inputs are finite; a program needn't handle non-finite values.
Results may differ from a plain program's by a relative error of at most 0.003.
Values may be sent and summed in bfloat16 or wider, within the bound.
No kernel may reach another device: no remote copies, remote signals or barrier semaphores. Data moves between devices by JAX's collectives and lax.ppermute only.
A program may use at most 128 MiB of HBM per device.

v0:
```python
import jax
import jax.numpy as jnp
from jax import lax
from jax.experimental import pallas as pl
from jax.experimental.pallas import tpu as pltpu
from jax.sharding import PartitionSpec as P


BPD = 8
TERMS = 4
TOUCH = 4
N_Z = 4
N_CORE = 2
STREAMS = 2
PLACES = 32
ID_ROWS = 16
UNROLL = 8
FIRST_UNROLL = 4
CHUNK = 32
VMEM_LIMIT = 14 * 1024 * 1024

VMEM = pl.BlockSpec(memory_space=pltpu.VMEM)
HBM = pl.BlockSpec(memory_space=pltpu.HBM)
SMEM = pl.BlockSpec(memory_space=pltpu.SMEM)
PARAMS = pltpu.CompilerParams(vmem_limit_bytes=VMEM_LIMIT)
F32 = jnp.float32
BF16 = jnp.bfloat16


def power(damping_ref, step):
    damping = damping_ref[...]
    coef = damping
    for _ in range(step - 1):
        coef = coef * damping
    return coef


def multiply_tiles(slot_ref, place_ref, count, tiles_ref, x_parts, turned, acc_ref, x_ref, tile_ref, sems):
    chunks = (count + CHUNK - 1) // CHUNK

    def chunk_copy(chunk):
        here = pl.ds(chunk * CHUNK, CHUNK)
        return pltpu.make_async_copy(tiles_ref.at[here], tile_ref.at[here], sems.at[chunk])

    def start(chunk, carry):
        chunk_copy(chunk).start()
        return carry

    lax.fori_loop(0, chunks, start, 0)
    each = x_ref.shape[0] // len(x_parts)
    for part, part_ref in enumerate(x_parts):
        x_ref[part * each : (part + 1) * each] = part_ref[...]
    acc_ref[...] = jnp.zeros(acc_ref.shape, F32)

    def group(base):
        prods = []
        for lane in range(UNROLL):
            prods.append(
                lax.dot_general(
                    x_ref[place_ref[base + lane]],
                    tile_ref[base + lane],
                    (((1,), (0 if turned else 1,)), ((), ())),
                    preferred_element_type=F32,
                )
            )
        for lane in range(UNROLL):
            slot = slot_ref[base + lane]
            acc_ref[slot] = acc_ref[slot] + prods[lane]

    def chunk_step(chunk, carry):
        chunk_copy(chunk).wait()
        for part in range(CHUNK // UNROLL):
            group(chunk * CHUNK + part * UNROLL)
        return carry

    lax.fori_loop(0, chunks, chunk_step, 0)


def tile_scratch(sent, blocks, width, tiles):
    tile = tiles.shape[1]
    return [
        pltpu.VMEM((sent + 1, width, tile), F32),
        pltpu.VMEM((blocks, width, tile), BF16),
        pltpu.VMEM(tiles.shape, tiles.dtype),
        pltpu.SemaphoreType.DMA((tiles.shape[0] // CHUNK,)),
    ]


def first_products(round_index, rows, cols, query_ids, count, col, tiles, n_col, n_row):
    slots, tile, _ = tiles.shape
    queries = query_ids.shape[0]
    col_blocks = n_row * BPD
    row_blocks = n_col * BPD
    spare = n_col * TOUCH
    sent_rows = TOUCH * PLACES
    tile_bits, col_bits, block_bits = (n.bit_length() - 1 for n in (tile, n_col, BPD))

    def body(info_ref, row_ref, col_ref, query_ref, tiles_ref, out_ref, *scratch):
        acc_ref, x_ref, tile_ref, id_rows_ref, asked_ref, has_ref, list_ref, mark_ref, slot_ref, id_ref, sems = scratch
        live, mine, first = info_ref[0], info_ref[1], info_ref[2] * PLACES

        def repeat(times, step, start=0, unroll=8):
            return lax.fori_loop(0, times, step, start, unroll=unroll)

        def clear(ref, value):
            def step(index, carry):
                ref[index] = value
                return carry

            repeat(ref.shape[0], step)

        def copy(index, lane):
            return pltpu.make_async_copy(tiles_ref.at[index], tile_ref.at[lane], sems.at[lane])

        def ask(query, found):
            node = query_ref[query]
            asked_ref[found] = node
            home = (node >> (tile_bits + block_bits)) & (n_col - 1)
            return found + (home == mine).astype(jnp.int32)

        asked = repeat(queries, ask)
        clear(has_ref, 0)
        x_ref[...] = jnp.zeros(x_ref.shape, BF16)
        place_of = lax.broadcasted_iota(jnp.int32, (PLACES, tile), 0)
        node_of = lax.broadcasted_iota(jnp.int32, (PLACES, tile), 1)

        def mark_query(place, carry):
            node = asked_ref[first + place]
            block = (node >> (tile_bits + block_bits + col_bits)) * BPD + ((node >> tile_bits) & (BPD - 1))
            here = (place_of == place) & (node_of == (node & (tile - 1)))
            x_ref[block] = jnp.where(here, 1.0, x_ref[block].astype(F32)).astype(BF16)
            has_ref[block] = 1
            return carry

        lax.fori_loop(0, jnp.clip(asked - first, 0, PLACES), mark_query, 0)

        def pick(index, found):
            list_ref[found] = index
            return found + jnp.where(index < live, has_ref[col_ref[index]], 0)

        found = repeat(slots, pick)

        def start(lane, carry):
            copy(list_ref[lane], lane).start()
            return carry

        lax.fori_loop(0, found, start, 0)
        clear(mark_ref, 0)

        def mark_row(index, carry):
            mark_ref[jnp.where(index < live, row_ref[index], row_blocks)] = 1
            return carry

        repeat(slots, mark_row)
        clear(id_ref, BPD)
        id_rows_ref[...] = jnp.full(id_rows_ref.shape, float(BPD), F32)

        def number_owner(owner, carry):
            rank = 0
            for block in range(BPD):
                marked = mark_ref[owner * BPD + block]
                slot_ref[owner * BPD + block] = owner * TOUCH + rank
                id_ref[owner * TOUCH + rank] = jnp.where(marked > 0, block, BPD)
                rank = rank + marked
            for place in range(TOUCH):
                number = id_ref[owner * TOUCH + place].astype(F32)
                id_rows_ref[owner, place : place + 1] = jnp.full((1, tile), number, F32)
            return carry

        repeat(n_col, number_owner, unroll=1)
        acc_ref[...] = jnp.zeros(acc_ref.shape, F32)

        def step(index, carry):
            prods, goes = [], []
            for lane in range(FIRST_UNROLL):
                at = index * FIRST_UNROLL + lane
                valid = at < found
                which = jnp.where(valid, list_ref[at], 0)

                @pl.when(valid)
                def _():
                    copy(which, at).wait()

                goes.append((at, which, valid))
            for at, which, valid in goes:
                prods.append(
                    lax.dot_general(
                        x_ref[col_ref[which]], tile_ref[at], (((1,), (1,)), ((), ())), preferred_element_type=F32
                    )
                )
            for (at, which, valid), prod in zip(goes, prods):
                slot = jnp.where(valid, slot_ref[row_ref[which]], spare)
                acc_ref[slot] = acc_ref[slot] + prod
            return carry

        lax.fori_loop(0, (found + FIRST_UNROLL - 1) // FIRST_UNROLL, step, 0)
        out_ref[:, :sent_rows] = acc_ref[:spare].astype(BF16).reshape(n_col, sent_rows, tile)
        out_ref[:, sent_rows:] = id_rows_ref[...].astype(BF16)

    info = jnp.stack([count, col, round_index]).astype(jnp.int32)
    return pl.pallas_call(
        body,
        out_shape=jax.ShapeDtypeStruct((n_col, sent_rows + ID_ROWS, tile), BF16),
        in_specs=[SMEM, SMEM, SMEM, SMEM, HBM],
        out_specs=VMEM,
        scratch_shapes=[
            pltpu.VMEM((spare + 1, PLACES, tile), F32),
            pltpu.VMEM((col_blocks, PLACES, tile), BF16),
            pltpu.VMEM(tiles.shape, tiles.dtype),
            pltpu.VMEM((n_col, ID_ROWS, tile), F32),
            pltpu.SMEM((queries,), jnp.int32),
            pltpu.SMEM((col_blocks,), jnp.int32),
            pltpu.SMEM((slots,), jnp.int32),
            pltpu.SMEM((row_blocks + 8,), jnp.int32),
            pltpu.SMEM((row_blocks,), jnp.int32),
            pltpu.SMEM((spare + 8,), jnp.int32),
            pltpu.SemaphoreType.DMA((slots,)),
        ],
        compiler_params=PARAMS,
        name="first_products",
    )(info, rows, cols, query_ids, pltpu.with_memory_space_constraint(tiles, pltpu.HBM))


def products(step, slots, places, count, turned, xparts, owners, damping, owned, scores):
    parts = len(xparts)
    each, width, tile = xparts[0].shape
    rows = TOUCH * width
    before = [] if step == 1 else [scores]

    def body(slot_ref, place_ref, count_ref, tiles_ref, *refs):
        x_refs, (damping_ref, owned_ref), refs = refs[:parts], refs[parts : parts + 2], refs[parts + 2 :]
        score_in, refs = refs[: len(before)], refs[len(before) :]
        out_ref, score_out, score_ref, score_sems, acc_ref, *scratch = refs
        for ref in score_in:
            pltpu.make_async_copy(ref, score_ref, score_sems.at[0]).start()
        multiply_tiles(slot_ref, place_ref, count_ref[0], tiles_ref, x_refs, True, acc_ref, *scratch)
        for ref in score_in:
            pltpu.make_async_copy(ref, score_ref, score_sems.at[0]).wait()
        if score_in:
            score_ref[...] = score_ref[...] + power(damping_ref, step - 1)[None] * owned_ref[...]
        else:
            score_ref[...] = owned_ref[...]
        leave = pltpu.make_async_copy(score_ref, score_out, score_sems.at[1])
        leave.start()
        out_ref[...] = acc_ref[: owners * TOUCH].astype(BF16).reshape(owners, rows, tile)
        leave.wait()

    return pl.pallas_call(
        body,
        out_shape=(
            jax.ShapeDtypeStruct((owners, rows, tile), BF16),
            pltpu.HBM((BPD, width, tile), F32),
        ),
        in_specs=[SMEM, SMEM, SMEM, HBM] + [VMEM] * (parts + 2) + [HBM] * len(before),
        out_specs=(VMEM, HBM),
        scratch_shapes=[
            pltpu.VMEM((BPD, width, tile), F32),
            pltpu.SemaphoreType.DMA((2,)),
            *tile_scratch(owners * TOUCH, parts * each, width, turned),
        ],
        compiler_params=PARAMS,
        name="products",
    )(
        slots,
        places,
        count,
        pltpu.with_memory_space_constraint(turned, pltpu.HBM),
        *xparts,
        damping,
        owned,
        *[pltpu.with_memory_space_constraint(part, pltpu.HBM) for part in before],
    )


def turned_tiles(count, tiles):
    def body(count_ref, tiles_ref, out_ref):
        def group(index, carry):
            for lane in range(UNROLL):
                out_ref[index * UNROLL + lane] = jnp.transpose(tiles_ref[index * UNROLL + lane])
            return carry

        lax.fori_loop(0, (count_ref[0] + UNROLL - 1) // UNROLL, group, 0)

    return pl.pallas_call(
        body,
        out_shape=jax.ShapeDtypeStruct(tiles.shape, tiles.dtype),
        in_specs=[SMEM, VMEM],
        out_specs=VMEM,
        compiler_params=PARAMS,
        name="turned",
    )(count, tiles)


def summed(id_ref, got_ref, acc_ref):
    width = acc_ref.shape[1]
    acc_ref[...] = jnp.zeros(acc_ref.shape, F32)
    for source in range(got_ref.shape[0]):
        for place in range(TOUCH):
            block = id_ref[source * TOUCH + place]
            part = got_ref[source, place * width : (place + 1) * width].astype(F32)
            acc_ref[block] = acc_ref[block] + part


def owned_sum(ids, got, damping):
    width, tile = damping.shape

    def body(id_ref, got_ref, x_ref, out_ref, acc_ref):
        summed(id_ref, got_ref, acc_ref)
        owned = acc_ref[:BPD]
        x_ref[...] = owned.astype(BF16)
        out_ref[...] = owned

    return pl.pallas_call(
        body,
        out_shape=(
            jax.ShapeDtypeStruct((BPD, width, tile), BF16),
            jax.ShapeDtypeStruct((BPD, width, tile), F32),
        ),
        in_specs=[SMEM, VMEM],
        out_specs=(VMEM, VMEM),
        scratch_shapes=[pltpu.VMEM((BPD + 1, width, tile), F32)],
        compiler_params=PARAMS,
        name="owned",
    )(ids, got)


def placed_sum(ids, got, spread, width, before=()):
    sources, _, tile = got.shape
    queries, columns = spread.shape
    streams = queries // width

    def body(id_ref, got_ref, spread_ref, *refs):
        whole_refs, refs = refs[: len(before)], refs[len(before) :]
        x_refs, out_refs, piece_ref = refs[:streams], refs[streams : 2 * streams], refs[-1]
        piece_ref[...] = jnp.zeros(piece_ref.shape, BF16)
        for source in range(sources):
            for place in range(TOUCH):
                block = id_ref[source * TOUCH + place]
                piece_ref[block, source * PLACES : (source + 1) * PLACES] = got_ref[
                    source, place * PLACES : (place + 1) * PLACES
                ]
        for block in range(BPD):
            owned = jnp.dot(spread_ref[...], piece_ref[block], preferred_element_type=F32)
            for stream in range(streams):
                mine = owned[stream * width : (stream + 1) * width]
                if whole_refs:
                    mine = mine + whole_refs[stream][block]
                x_refs[stream][block] = mine.astype(BF16)
                out_refs[stream][block] = mine

    shape = (BPD, width, tile)
    return pl.pallas_call(
        body,
        out_shape=[jax.ShapeDtypeStruct(shape, BF16)] * streams + [jax.ShapeDtypeStruct(shape, F32)] * streams,
        in_specs=[SMEM] + [VMEM] * (2 + len(before)),
        out_specs=[VMEM] * (2 * streams),
        scratch_shapes=[pltpu.VMEM((BPD + 1, columns, tile), BF16)],
        compiler_params=PARAMS,
        name="placed",
    )(ids, got, spread, *before)


def ended_sum(step, ids, got, damping, scores):
    width, tile = damping.shape

    def body(id_ref, got_ref, damping_ref, score_ref, out_ref, acc_ref):
        summed(id_ref, got_ref, acc_ref)
        out_ref[...] = score_ref[...] + power(damping_ref, step)[None] * acc_ref[:BPD]

    return pl.pallas_call(
        body,
        out_shape=jax.ShapeDtypeStruct((BPD, width, tile), F32),
        in_specs=[SMEM] + [VMEM] * 3,
        out_specs=VMEM,
        scratch_shapes=[pltpu.VMEM((BPD + 1, width, tile), F32)],
        compiler_params=PARAMS,
        name="ended",
    )(ids, got, damping, scores)


def last_sum(step, ids, got, damping, scores, *done):
    width, tile = damping.shape
    queries = sum(part.shape[1] for part in done) + width

    def body(id_ref, got_ref, damping_ref, score_ref, *refs):
        done_refs, (out_ref, acc_ref) = refs[:-2], refs[-2:]
        summed(id_ref, got_ref, acc_ref)
        coef = power(damping_ref, step)
        for block in range(BPD):
            mine = score_ref[block] + coef * acc_ref[block]
            rows = [part[block] for part in done_refs] + [mine]
            out_ref[block] = jnp.transpose(jnp.concatenate(rows, axis=0))

    return pl.pallas_call(
        body,
        out_shape=jax.ShapeDtypeStruct((BPD, tile, queries), F32),
        in_specs=[SMEM] + [VMEM] * (3 + len(done)),
        out_specs=VMEM,
        scratch_shapes=[pltpu.VMEM((BPD + 1, width, tile), F32)],
        compiler_params=PARAMS,
        name="last",
    )(ids, got, damping, scores, *done)


def row_shift(dz, dcore):
    return [
        (z * N_CORE + core, (z + dz) % N_Z * N_CORE + (core + dcore) % N_CORE)
        for z in range(N_Z)
        for core in range(N_CORE)
    ]


def column_parts(mine):
    same = [mine] + [lax.ppermute(mine, "row", row_shift(dz, 0)) for dz in range(1, N_Z)]
    other = [lax.ppermute(part, "row", row_shift(0, 1)) for part in same]
    return same + other


def after(value, *others):
    return lax.optimization_barrier((value, *others))[0]


def exchange(sent):
    return lax.all_to_all(sent, "col", split_axis=0, concat_axis=0, tiled=True)


def routes(rows, cols, count, n_col):
    slots = rows.shape[0]
    live = jnp.arange(slots, dtype=jnp.int32) < count
    blocks = jnp.arange(n_col * BPD, dtype=jnp.int32)
    hits = (rows[None, :] == blocks[:, None]) & live[None, :]
    marked = jnp.any(hits, axis=1).astype(jnp.int32).reshape(n_col, BPD)
    local = jnp.arange(BPD, dtype=jnp.int32)
    rank = jnp.sum(marked[:, None, :] * (local[None, None, :] < local[None, :, None]), axis=2)
    slot_of = (jnp.arange(n_col, dtype=jnp.int32)[:, None] * TOUCH + rank).reshape(-1)
    slot = jnp.sum(jnp.where(hits, slot_of[:, None], 0), axis=0)
    slot = jnp.where(live, slot, n_col * TOUCH)
    row = lax.axis_index("row")
    owner, block = cols // BPD, cols % BPD
    far = (row // N_CORE - owner // N_CORE) % N_Z
    place = ((row % N_CORE != owner % N_CORE).astype(jnp.int32) * N_Z + far) * BPD + block
    return slot, place


def shards(tiles, tile_row, tile_col, tile_count, query_ids, damping):
    tiles, rows, cols, count = tiles[0, 0], tile_row[0, 0], tile_col[0, 0], tile_count[0, 0]
    tile = tiles.shape[1]
    queries = query_ids.shape[0]
    width = queries // STREAMS
    n_row, n_col = lax.axis_size("row"), lax.axis_size("col")
    col = lax.axis_index("col")

    def first_sent(round_index):
        return first_products(round_index, rows, cols, query_ids, count, col, tiles, n_col, n_row)

    sent = first_sent(0)
    got = exchange(sent)

    later_ids = after(query_ids, sent)
    home = later_ids // (BPD * tile) % n_col
    number = jnp.arange(queries, dtype=jnp.int32)
    same_home = home[:, None] == home[None, :]
    rank = jnp.sum((same_home & (number[None, :] < number[:, None])).astype(jnp.int32), axis=1)
    rounds = jnp.max(rank) // PLACES + 1

    def spread(round_index):
        place = rank - round_index * PLACES
        column = jnp.where((place >= 0) & (place < PLACES), home * PLACES + place, -1)
        return (column[:, None] == jnp.arange(n_col * PLACES, dtype=jnp.int32)[None, :]).astype(BF16)

    slot, place = routes(after(rows, sent), cols, count, n_col)
    turned = turned_tiles(count.reshape(1), after(tiles, sent))
    first_spread = spread(0)
    got_ids = got[:, -ID_ROWS:, 0][:, :TOUCH].astype(jnp.int32).reshape(-1)
    sums = placed_sum(got_ids, after(got, turned, slot, place, first_spread), first_spread, width)

    def next_round(state):
        index, *sums = state
        got = exchange(first_sent(index))
        return index + 1, *placed_sum(got_ids, got, spread(index), width, sums[STREAMS:])

    _, *sums = lax.while_loop(lambda state: state[0] < rounds, next_round, (jnp.int32(1), *sums))
    count = count.reshape(1)
    dampings = [
        jnp.broadcast_to(damping[stream * width : (stream + 1) * width][:, None], (width, tile))
        for stream in range(STREAMS)
    ]
    xparts = [column_parts(sums[stream]) for stream in range(STREAMS)]
    owned, scores = sums[STREAMS:], [None] * STREAMS
    for step in range(1, TERMS):
        for stream in range(STREAMS):
            sent, scores[stream] = products(
                step,
                slot,
                place,
                count,
                turned,
                xparts[stream],
                n_col,
                dampings[stream],
                owned[stream],
                scores[stream],
            )
            got = exchange(sent)
            if step + 1 < TERMS:
                mine, owned[stream] = owned_sum(got_ids, got, dampings[stream])
                xparts[stream] = column_parts(mine)
            elif stream + 1 < STREAMS:
                scores[stream] = ended_sum(step, got_ids, got, dampings[stream], scores[stream])
            else:
                total = last_sum(step, got_ids, got, dampings[stream], scores[stream], *scores[:-1])
    return total.reshape(BPD * tile, -1)


def solution(mesh):
    in_specs = (
        P("row", "col", None, None, None),
        P("row", "col", None),
        P("row", "col", None),
        P("row", "col"),
        P(),
        P(),
    )
    out_specs = P(("row", "col"), None)
    return jax.shard_map(shards, mesh=mesh, in_specs=in_specs, out_specs=out_specs, check_vma=False)
```

profile of v0, /device:TPU:32, one launch (start us, length us, event | category | flops | bytes accessed | tf_op | source)
XLA Modules:
  0.0 201.5 jit_solution(503720209998592095)
XLA Ops:
  0.8 5.7 %first_products.2 = bf16[16,144,128]{2,1,0:T(8,128)(2,1)} custom-call(s32[3]{0:T(128)S(1)} %pad_add_fusion.1.info_ref, s32[128]{0:T(128)} %bitcast.32, s32[128]{0:T(128)} %bitcast.30, s32[128]{0:T(128)} %query_ref.1, bf16[128,128,128]{2,1,0:T(8,128)(2,1)} %bitcast.27), custom_call_target="tpu_custom_call" | custom-call | tf_op jit(solution)/shard_map/first_products/pallas_call | solution.py:201
  10.6 3.2 %turned.1.tiles_ref = bf16[128,128,128]{2,1,0:T(8,128)(2,1)S(1)} custom-call(s32[1]{0:T(128)} %bitcast.18.count_ref, bf16[128,128,128]{2,1,0:T(8,128)(2,1)} %bitcast.28), custom_call_target="tpu_custom_call" | custom-call | tf_op jit(solution)/shard_map/turned/pallas_call | solution.py:284
  13.8 2.0 copy-done
  15.8 8.0 %all-to-all-start.1 = ((bf16[16,144,128]{2,1,0:T(8,128)(2,1)}), bf16[16,144,128]{2,1,0:T(8,128)(2,1)S(1)}, u32[]{:S(2)}, u32[]{:S(2)}) async-start(bf16[16,144,128]{2,1,0:T(8,128)(2,1)} %first_products.2), calls=%async_computation.1 | async-start | bytes 1179648 | tf_op jit(solution)/shard_map/all_to_all | solution.py:424
  24.0 12.0 %all-to-all-done.1.got_ref = bf16[16,144,128]{2,1,0:T(8,128)(2,1)S(1)} async-done(((bf16[16,144,128]{2,1,0:T(8,128)(2,1)}), bf16[16,144,128]{2,1,0:T(8,128)(2,1)S(1)}, u32[]{:S(2)}, u32[]{:S(2)}) %all-to-all-start.1) | async-done | bytes 589856 | tf_op jit(solution)/shard_map/all_to_all | solution.py:424
  38.0 1.9 collective-permute-start.21
  44.0 2.7 %collective-permute-done.22.refs_2_ = bf16[8,64,128]{2,1,0:T(8,128)(2,1)S(1)} collective-permute-done((bf16[8,64,128]{2,1,0:T(8,128)(2,1)}, bf16[8,64,128]{2,1,0:T(8,128)(2,1)S(1)}, u32[]{:S(2)}, u32[]{:S(2)}) %collective-permute-start.22) | collective-permute-done | bytes 131104 | tf_op jit(solution)/shard_map/ppermute | solution.py:414
  49.3 4.8 %products.9 = (bf16[16,256,128]{2,1,0:T(8,128)(2,1)}, f32[8,64,128]{2,1,0:T(8,128)}) custom-call(s32[128]{0:T(128)S(1)} %get-tuple-element.183.slot_ref, s32[128]{0:T(128)S(1)} %get-tuple-element.182.place_ref, s32[1]{0:T(128)} %bitcast.22.count_ref, bf16[128,128,128]{2,1,0:T(8,128)(2,1)} %copy-done, bf16[8,64,128]{2,1,0:T(8,128)(2,1)} %get-tuple-element.136.refs_0_, ...), custom_call_target="tpu_custom_call" | custom-call | tf_op jit(solution)/shard_map/products/pallas_call | solution.py:248
  54.1 4.5 %all-to-all-start.5 = ((bf16[16,256,128]{2,1,0:T(8,128)(2,1)}), bf16[16,256,128]{2,1,0:T(8,128)(2,1)S(1)}, u32[]{:S(2)}, u32[]{:S(2)}) async-start(bf16[16,256,128]{2,1,0:T(8,128)(2,1)} %get-tuple-element.138), calls=%async_computation.5 | async-start | bytes 2097152 | tf_op jit(solution)/shard_map/all_to_all | solution.py:424
  60.7 2.5 %collective-permute-start.2 = (bf16[8,64,128]{2,1,0:T(8,128)(2,1)S(1)}, bf16[8,64,128]{2,1,0:T(8,128)(2,1)S(1)}, u32[]{:S(2)}, u32[]{:S(2)}) collective-permute-start(bf16[8,64,128]{2,1,0:T(8,128)(2,1)S(1)} %copy-done.3), channel_id=1, source_target_pairs={{0,96},{16,112},{32,0},{48,16},{64,32},{80,48},{96,64},{112,80},{1... | collective-permute-start | bytes 393224 | tf_op jit(solution)/shard_map/ppermute | solution.py:414
  64.2 2.7 %collective-permute-done.1.refs_2_ = bf16[8,64,128]{2,1,0:T(8,128)(2,1)S(1)} collective-permute-done((bf16[8,64,128]{2,1,0:T(8,128)(2,1)S(1)}, bf16[8,64,128]{2,1,0:T(8,128)(2,1)S(1)}, u32[]{:S(2)}, u32[]{:S(2)}) %collective-permute-start.1) | collective-permute-done | bytes 131104 | tf_op jit(solution)/shard_map/ppermute | solution.py:414
  70.2 4.4 %products.6 = (bf16[16,256,128]{2,1,0:T(8,128)(2,1)}, f32[8,64,128]{2,1,0:T(8,128)}) custom-call(s32[128]{0:T(128)S(1)} %get-tuple-element.183.slot_ref, s32[128]{0:T(128)S(1)} %get-tuple-element.182.place_ref, s32[1]{0:T(128)} %bitcast.19.count_ref, bf16[128,128,128]{2,1,0:T(8,128)(2,1)} %copy-done, bf16[8,64,128]{2,1,0:T(8,128)(2,1)S(1)} %copy-done.3, ...), custom_call_target="tpu_custom_call" | custom-call | tf_op jit(solution)/shard_map/products/pallas_call | solution.py:248
  74.6 2.1 %all-to-all-done.5.got_ref = bf16[16,256,128]{2,1,0:T(8,128)(2,1)S(1)} async-done(((bf16[16,256,128]{2,1,0:T(8,128)(2,1)}), bf16[16,256,128]{2,1,0:T(8,128)(2,1)S(1)}, u32[]{:S(2)}, u32[]{:S(2)}) %all-to-all-start.5) | async-done | bytes 1048608 | tf_op jit(solution)/shard_map/all_to_all | solution.py:424
  76.7 5.6 %all-to-all-start.2 = ((bf16[16,256,128]{2,1,0:T(8,128)(2,1)}), bf16[16,256,128]{2,1,0:T(8,128)(2,1)S(1)}, u32[]{:S(2)}, u32[]{:S(2)}) async-start(bf16[16,256,128]{2,1,0:T(8,128)(2,1)} %get-tuple-element.126), calls=%async_computation.2 | async-start | bytes 2097152 | tf_op jit(solution)/shard_map/all_to_all | solution.py:424
  85.3 2.5 %collective-permute-start.30 = (bf16[8,64,128]{2,1,0:T(8,128)(2,1)S(1)}, bf16[8,64,128]{2,1,0:T(8,128)(2,1)S(1)}, u32[]{:S(2)}, u32[]{:S(2)}) collective-permute-start(bf16[8,64,128]{2,1,0:T(8,128)(2,1)S(1)} %get-tuple-element.139.refs_0_), channel_id=1, source_target_pairs={{0,96},{16,112},{32,0},{48,16},{64,32},{80,48},{96,64},{112,80},{1... | collective-permute-start | bytes 393224 | tf_op jit(solution)/shard_map/ppermute | solution.py:414
  87.8 1.9 collective-permute-done.28.refs_1_
  89.7 2.0 collective-permute-done.29.refs_2_
  94.8 4.5 %products.10 = (bf16[16,256,128]{2,1,0:T(8,128)(2,1)}, f32[8,64,128]{2,1,0:T(8,128)}) custom-call(s32[128]{0:T(128)S(1)} %get-tuple-element.183.slot_ref, s32[128]{0:T(128)S(1)} %get-tuple-element.182.place_ref, s32[1]{0:T(128)} %bitcast.23.count_ref, bf16[128,128,128]{2,1,0:T(8,128)(2,1)} %copy-done, bf16[8,64,128]{2,1,0:T(8,128)(2,1)S(1)} %get-tuple-element.139.refs_0_, ...), custom_call_target="tpu_custom_call" | custom-call | tf_op jit(solution)/shard_map/products/pallas_call | solution.py:248
  100.4 6.6 %all-to-all-start.6 = ((bf16[16,256,128]{2,1,0:T(8,128)(2,1)}), bf16[16,256,128]{2,1,0:T(8,128)(2,1)S(1)}, u32[]{:S(2)}, u32[]{:S(2)}) async-start(bf16[16,256,128]{2,1,0:T(8,128)(2,1)} %get-tuple-element.142), calls=%async_computation.6 | async-start | bytes 2097152 | tf_op jit(solution)/shard_map/all_to_all | solution.py:424
  108.4 2.0 %collective-permute-start.8 = (bf16[8,64,128]{2,1,0:T(8,128)(2,1)S(1)}, bf16[8,64,128]{2,1,0:T(8,128)(2,1)S(1)}, u32[]{:S(2)}, u32[]{:S(2)}) collective-permute-start(bf16[8,64,128]{2,1,0:T(8,128)(2,1)S(1)} %get-tuple-element.127.refs_0_), channel_id=1, source_target_pairs={{0,64},{16,80},{32,96},{48,112},{64,0},{80,16},{96,32},{112,48},{1... | collective-permute-start | bytes 393224 | tf_op jit(solution)/shard_map/ppermute | solution.py:414
  110.4 2.5 %collective-permute-start.9 = (bf16[8,64,128]{2,1,0:T(8,128)(2,1)S(1)}, bf16[8,64,128]{2,1,0:T(8,128)(2,1)S(1)}, u32[]{:S(2)}, u32[]{:S(2)}) collective-permute-start(bf16[8,64,128]{2,1,0:T(8,128)(2,1)S(1)} %get-tuple-element.127.refs_0_), channel_id=1, source_target_pairs={{0,96},{16,112},{32,0},{48,16},{64,32},{80,48},{96,64},{112,80},{1... | collective-permute-start | bytes 393224 | tf_op jit(solution)/shard_map/ppermute | solution.py:414
  119.3 4.5 %products.7 = (bf16[16,256,128]{2,1,0:T(8,128)(2,1)}, f32[8,64,128]{2,1,0:T(8,128)}) custom-call(s32[128]{0:T(128)S(1)} %get-tuple-element.183.slot_ref, s32[128]{0:T(128)S(1)} %get-tuple-element.182.place_ref, s32[1]{0:T(128)} %bitcast.20.count_ref, bf16[128,128,128]{2,1,0:T(8,128)(2,1)} %copy-done, bf16[8,64,128]{2,1,0:T(8,128)(2,1)S(1)} %get-tuple-element.127.refs_0_, ...), custom_call_target="tpu_custom_call" | custom-call | tf_op jit(solution)/shard_map/products/pallas_call | solution.py:248
  125.2 6.4 %all-to-all-start.3 = ((bf16[16,256,128]{2,1,0:T(8,128)(2,1)}), bf16[16,256,128]{2,1,0:T(8,128)(2,1)S(1)}, u32[]{:S(2)}, u32[]{:S(2)}) async-start(bf16[16,256,128]{2,1,0:T(8,128)(2,1)} %get-tuple-element.130), calls=%async_computation.3 | async-start | bytes 2097152 | tf_op jit(solution)/shard_map/all_to_all | solution.py:424
  134.7 2.5 %collective-permute-start.37 = (bf16[8,64,128]{2,1,0:T(8,128)(2,1)S(1)}, bf16[8,64,128]{2,1,0:T(8,128)(2,1)S(1)}, u32[]{:S(2)}, u32[]{:S(2)}) collective-permute-start(bf16[8,64,128]{2,1,0:T(8,128)(2,1)S(1)} %get-tuple-element.143.refs_0_), channel_id=1, source_target_pairs={{0,96},{16,112},{32,0},{48,16},{64,32},{80,48},{96,64},{112,80},{1... | collective-permute-start | bytes 393224 | tf_op jit(solution)/shard_map/ppermute | solution.py:414
  143.8 4.5 %products.11 = (bf16[16,256,128]{2,1,0:T(8,128)(2,1)}, f32[8,64,128]{2,1,0:T(8,128)}) custom-call(s32[128]{0:T(128)S(1)} %get-tuple-element.183.slot_ref, s32[128]{0:T(128)S(1)} %get-tuple-element.182.place_ref, s32[1]{0:T(128)} %bitcast.24.count_ref, bf16[128,128,128]{2,1,0:T(8,128)(2,1)} %copy-done, bf16[8,64,128]{2,1,0:T(8,128)(2,1)S(1)} %get-tuple-element.143.refs_0_, ...), custom_call_target="tpu_custom_call" | custom-call | tf_op jit(solution)/shard_map/products/pallas_call | solution.py:248
  149.7 6.4 %all-to-all-start.7 = ((bf16[16,256,128]{2,1,0:T(8,128)(2,1)}), bf16[16,256,128]{2,1,0:T(8,128)(2,1)S(1)}, u32[]{:S(2)}, u32[]{:S(2)}) async-start(bf16[16,256,128]{2,1,0:T(8,128)(2,1)} %get-tuple-element.146), calls=%async_computation.7 | async-start | bytes 2097152 | tf_op jit(solution)/shard_map/all_to_all | solution.py:424
  159.0 2.5 %collective-permute-start.16 = (bf16[8,64,128]{2,1,0:T(8,128)(2,1)S(1)}, bf16[8,64,128]{2,1,0:T(8,128)(2,1)S(1)}, u32[]{:S(2)}, u32[]{:S(2)}) collective-permute-start(bf16[8,64,128]{2,1,0:T(8,128)(2,1)S(1)} %get-tuple-element.131.refs_0_), channel_id=1, source_target_pairs={{0,96},{16,112},{32,0},{48,16},{64,32},{80,48},{96,64},{112,80},{1... | collective-permute-start | bytes 393224 | tf_op jit(solution)/shard_map/ppermute | solution.py:414
  161.5 1.9 collective-permute-done.14.refs_1_
  163.5 1.9 collective-permute-done.15.refs_2_
  168.3 4.5 %products.8 = (bf16[16,256,128]{2,1,0:T(8,128)(2,1)}, f32[8,64,128]{2,1,0:T(8,128)}) custom-call(s32[128]{0:T(128)S(1)} %get-tuple-element.183.slot_ref, s32[128]{0:T(128)S(1)} %get-tuple-element.182.place_ref, s32[1]{0:T(128)} %bitcast.21.count_ref, bf16[128,128,128]{2,1,0:T(8,128)(2,1)} %copy-done, bf16[8,64,128]{2,1,0:T(8,128)(2,1)S(1)} %get-tuple-element.131.refs_0_, ...), custom_call_target="tpu_custom_call" | custom-call | tf_op jit(solution)/shard_map/products/pallas_call | solution.py:248
  174.2 6.4 %all-to-all-start.4 = ((bf16[16,256,128]{2,1,0:T(8,128)(2,1)}), bf16[16,256,128]{2,1,0:T(8,128)(2,1)S(1)}, u32[]{:S(2)}, u32[]{:S(2)}) async-start(bf16[16,256,128]{2,1,0:T(8,128)(2,1)} %get-tuple-element.134), calls=%async_computation.4 | async-start | bytes 2097152 | tf_op jit(solution)/shard_map/all_to_all | solution.py:424
  181.5 17.2 %all-to-all-done.4.got_ref = bf16[16,256,128]{2,1,0:T(8,128)(2,1)S(1)} async-done(((bf16[16,256,128]{2,1,0:T(8,128)(2,1)}), bf16[16,256,128]{2,1,0:T(8,128)(2,1)S(1)}, u32[]{:S(2)}, u32[]{:S(2)}) %all-to-all-start.4) | async-done | bytes 1048608 | tf_op jit(solution)/shard_map/all_to_all | solution.py:424
  (122 shorter events, 54.9 us)
Async XLA Ops:
  15.8 20.2 %all-to-all-start.1 = ((bf16[16,144,128]{2,1,0:T(8,128)(2,1)}), bf16[16,144,128]{2,1,0:T(8,128)(2,1)S(1)}, u32[]{:S(2)}, u32[]{:S(2)}) async-start(bf16[16,144,128]{2,1,0:T(8,128)(2,1)} %first_products.2), calls=%async_computation.1 | async-start | bytes 1179648 | tf_op jit(solution)/shard_map/all_to_all | solution.py:424
  38.0 6.0 %collective-permute-start.21 = (bf16[8,64,128]{2,1,0:T(8,128)(2,1)}, bf16[8,64,128]{2,1,0:T(8,128)(2,1)S(1)}, u32[]{:S(2)}, u32[]{:S(2)}) collective-permute-start(bf16[8,64,128]{2,1,0:T(8,128)(2,1)} %get-tuple-element.136.refs_0_), channel_id=1, source_target_pairs={{0,32},{16,48},{32,64},{48,80},{64,96},{80,112},{96,0},{112,16},{1... | collective-permute-start | bytes 393224 | tf_op jit(solution)/shard_map/ppermute | solution.py:414
  39.9 6.8 %collective-permute-start.22 = (bf16[8,64,128]{2,1,0:T(8,128)(2,1)}, bf16[8,64,128]{2,1,0:T(8,128)(2,1)S(1)}, u32[]{:S(2)}, u32[]{:S(2)}) collective-permute-start(bf16[8,64,128]{2,1,0:T(8,128)(2,1)} %get-tuple-element.136.refs_0_), channel_id=1, source_target_pairs={{0,64},{16,80},{32,96},{48,112},{64,0},{80,16},{96,32},{112,48},{1... | collective-permute-start | bytes 393224 | tf_op jit(solution)/shard_map/ppermute | solution.py:414
  40.2 7.7 %collective-permute-start.23 = (bf16[8,64,128]{2,1,0:T(8,128)(2,1)}, bf16[8,64,128]{2,1,0:T(8,128)(2,1)S(1)}, u32[]{:S(2)}, u32[]{:S(2)}) collective-permute-start(bf16[8,64,128]{2,1,0:T(8,128)(2,1)} %get-tuple-element.136.refs_0_), channel_id=1, source_target_pairs={{0,96},{16,112},{32,0},{48,16},{64,32},{80,48},{96,64},{112,80},{1... | collective-permute-start | bytes 393224 | tf_op jit(solution)/shard_map/ppermute | solution.py:414
  42.1 5.9 %collective-permute-start.24 = (bf16[8,64,128]{2,1,0:T(8,128)(2,1)}, bf16[8,64,128]{2,1,0:T(8,128)(2,1)S(1)}, u32[]{:S(2)}, u32[]{:S(2)}) collective-permute-start(bf16[8,64,128]{2,1,0:T(8,128)(2,1)} %get-tuple-element.136.refs_0_), channel_id=1, source_target_pairs={{0,16},{16,0},{32,48},{48,32},{64,80},{80,64},{96,112},{112,96},{1... | collective-permute-start | bytes 393224 | tf_op jit(solution)/shard_map/ppermute | solution.py:415
  54.1 22.6 %all-to-all-start.5 = ((bf16[16,256,128]{2,1,0:T(8,128)(2,1)}), bf16[16,256,128]{2,1,0:T(8,128)(2,1)S(1)}, u32[]{:S(2)}, u32[]{:S(2)}) async-start(bf16[16,256,128]{2,1,0:T(8,128)(2,1)} %get-tuple-element.138), calls=%async_computation.5 | async-start | bytes 2097152 | tf_op jit(solution)/shard_map/all_to_all | solution.py:424
  58.6 5.6 %collective-permute-start = (bf16[8,64,128]{2,1,0:T(8,128)(2,1)S(1)}, bf16[8,64,128]{2,1,0:T(8,128)(2,1)S(1)}, u32[]{:S(2)}, u32[]{:S(2)}) collective-permute-start(bf16[8,64,128]{2,1,0:T(8,128)(2,1)S(1)} %copy-done.3), channel_id=1, source_target_pairs={{0,32},{16,48},{32,64},{48,80},{64,96},{80,112},{96,0},{112,16},{1... | collective-permute-start | bytes 393224 | tf_op jit(solution)/shard_map/ppermute | solution.py:414
  59.0 7.9 %collective-permute-start.1 = (bf16[8,64,128]{2,1,0:T(8,128)(2,1)S(1)}, bf16[8,64,128]{2,1,0:T(8,128)(2,1)S(1)}, u32[]{:S(2)}, u32[]{:S(2)}) collective-permute-start(bf16[8,64,128]{2,1,0:T(8,128)(2,1)S(1)} %copy-done.3), channel_id=1, source_target_pairs={{0,64},{16,80},{32,96},{48,112},{64,0},{80,16},{96,32},{112,48},{1... | collective-permute-start | bytes 393224 | tf_op jit(solution)/shard_map/ppermute | solution.py:414
  60.7 8.1 %collective-permute-start.2 = (bf16[8,64,128]{2,1,0:T(8,128)(2,1)S(1)}, bf16[8,64,128]{2,1,0:T(8,128)(2,1)S(1)}, u32[]{:S(2)}, u32[]{:S(2)}) collective-permute-start(bf16[8,64,128]{2,1,0:T(8,128)(2,1)S(1)} %copy-done.3), channel_id=1, source_target_pairs={{0,96},{16,112},{32,0},{48,16},{64,32},{80,48},{96,64},{112,80},{1... | collective-permute-start | bytes 393224 | tf_op jit(solution)/shard_map/ppermute | solution.py:414
  63.2 5.5 %collective-permute-start.3 = (bf16[8,64,128]{2,1,0:T(8,128)(2,1)S(1)}, bf16[8,64,128]{2,1,0:T(8,128)(2,1)S(1)}, u32[]{:S(2)}, u32[]{:S(2)}) collective-permute-start(bf16[8,64,128]{2,1,0:T(8,128)(2,1)S(1)} %copy-done.3), channel_id=1, source_target_pairs={{0,16},{16,0},{32,48},{48,32},{64,80},{80,64},{96,112},{112,96},{1... | collective-permute-start | bytes 393224 | tf_op jit(solution)/shard_map/ppermute | solution.py:415
  64.2 4.6 %collective-permute-start.4 = (bf16[8,64,128]{2,1,0:T(8,128)(2,1)S(1)}, bf16[8,64,128]{2,1,0:T(8,128)(2,1)S(1)}, u32[]{:S(2)}, u32[]{:S(2)}) collective-permute-start(bf16[8,64,128]{2,1,0:T(8,128)(2,1)S(1)} %collective-permute-done.refs_1_), channel_id=1, source_target_pairs={{0,16},{16,0},{32,48},{48,32},{64,80},{80,64},{96,112},{112,96},{1... | collective-permute-start | bytes 393224 | tf_op jit(solution)/shard_map/ppermute | solution.py:415
  76.7 23.7 %all-to-all-start.2 = ((bf16[16,256,128]{2,1,0:T(8,128)(2,1)}), bf16[16,256,128]{2,1,0:T(8,128)(2,1)S(1)}, u32[]{:S(2)}, u32[]{:S(2)}) async-start(bf16[16,256,128]{2,1,0:T(8,128)(2,1)} %get-tuple-element.126), calls=%async_computation.2 | async-start | bytes 2097152 | tf_op jit(solution)/shard_map/all_to_all | solution.py:424
  83.3 6.4 %collective-permute-start.28 = (bf16[8,64,128]{2,1,0:T(8,128)(2,1)S(1)}, bf16[8,64,128]{2,1,0:T(8,128)(2,1)S(1)}, u32[]{:S(2)}, u32[]{:S(2)}) collective-permute-start(bf16[8,64,128]{2,1,0:T(8,128)(2,1)S(1)} %get-tuple-element.139.refs_0_), channel_id=1, source_target_pairs={{0,32},{16,48},{32,64},{48,80},{64,96},{80,112},{96,0},{112,16},{1... | collective-permute-start | bytes 393224 | tf_op jit(solution)/shard_map/ppermute | solution.py:414
  83.8 7.9 %collective-permute-start.29 = (bf16[8,64,128]{2,1,0:T(8,128)(2,1)S(1)}, bf16[8,64,128]{2,1,0:T(8,128)(2,1)S(1)}, u32[]{:S(2)}, u32[]{:S(2)}) collective-permute-start(bf16[8,64,128]{2,1,0:T(8,128)(2,1)S(1)} %get-tuple-element.139.refs_0_), channel_id=1, source_target_pairs={{0,64},{16,80},{32,96},{48,112},{64,0},{80,16},{96,32},{112,48},{1... | collective-permute-start | bytes 393224 | tf_op jit(solution)/shard_map/ppermute | solution.py:414
  85.3 8.1 %collective-permute-start.30 = (bf16[8,64,128]{2,1,0:T(8,128)(2,1)S(1)}, bf16[8,64,128]{2,1,0:T(8,128)(2,1)S(1)}, u32[]{:S(2)}, u32[]{:S(2)}) collective-permute-start(bf16[8,64,128]{2,1,0:T(8,128)(2,1)S(1)} %get-tuple-element.139.refs_0_), channel_id=1, source_target_pairs={{0,96},{16,112},{32,0},{48,16},{64,32},{80,48},{96,64},{112,80},{1... | collective-permute-start | bytes 393224 | tf_op jit(solution)/shard_map/ppermute | solution.py:414
  87.8 5.7 %collective-permute-start.31 = (bf16[8,64,128]{2,1,0:T(8,128)(2,1)S(1)}, bf16[8,64,128]{2,1,0:T(8,128)(2,1)S(1)}, u32[]{:S(2)}, u32[]{:S(2)}) collective-permute-start(bf16[8,64,128]{2,1,0:T(8,128)(2,1)S(1)} %get-tuple-element.139.refs_0_), channel_id=1, source_target_pairs={{0,16},{16,0},{32,48},{48,32},{64,80},{80,64},{96,112},{112,96},{1... | collective-permute-start | bytes 393224 | tf_op jit(solution)/shard_map/ppermute | solution.py:415
  100.4 24.7 %all-to-all-start.6 = ((bf16[16,256,128]{2,1,0:T(8,128)(2,1)}), bf16[16,256,128]{2,1,0:T(8,128)(2,1)S(1)}, u32[]{:S(2)}, u32[]{:S(2)}) async-start(bf16[16,256,128]{2,1,0:T(8,128)(2,1)} %get-tuple-element.142), calls=%async_computation.6 | async-start | bytes 2097152 | tf_op jit(solution)/shard_map/all_to_all | solution.py:424
  108.0 6.4 %collective-permute-start.7 = (bf16[8,64,128]{2,1,0:T(8,128)(2,1)S(1)}, bf16[8,64,128]{2,1,0:T(8,128)(2,1)S(1)}, u32[]{:S(2)}, u32[]{:S(2)}) collective-permute-start(bf16[8,64,128]{2,1,0:T(8,128)(2,1)S(1)} %get-tuple-element.127.refs_0_), channel_id=1, source_target_pairs={{0,32},{16,48},{32,64},{48,80},{64,96},{80,112},{96,0},{112,16},{1... | collective-permute-start | bytes 393224 | tf_op jit(solution)/shard_map/ppermute | solution.py:414
  108.4 7.9 %collective-permute-start.8 = (bf16[8,64,128]{2,1,0:T(8,128)(2,1)S(1)}, bf16[8,64,128]{2,1,0:T(8,128)(2,1)S(1)}, u32[]{:S(2)}, u32[]{:S(2)}) collective-permute-start(bf16[8,64,128]{2,1,0:T(8,128)(2,1)S(1)} %get-tuple-element.127.refs_0_), channel_id=1, source_target_pairs={{0,64},{16,80},{32,96},{48,112},{64,0},{80,16},{96,32},{112,48},{1... | collective-permute-start | bytes 393224 | tf_op jit(solution)/shard_map/ppermute | solution.py:414
  110.4 7.6 %collective-permute-start.9 = (bf16[8,64,128]{2,1,0:T(8,128)(2,1)S(1)}, bf16[8,64,128]{2,1,0:T(8,128)(2,1)S(1)}, u32[]{:S(2)}, u32[]{:S(2)}) collective-permute-start(bf16[8,64,128]{2,1,0:T(8,128)(2,1)S(1)} %get-tuple-element.127.refs_0_), channel_id=1, source_target_pairs={{0,96},{16,112},{32,0},{48,16},{64,32},{80,48},{96,64},{112,80},{1... | collective-permute-start | bytes 393224 | tf_op jit(solution)/shard_map/ppermute | solution.py:414
  112.9 5.0 %collective-permute-start.10 = (bf16[8,64,128]{2,1,0:T(8,128)(2,1)S(1)}, bf16[8,64,128]{2,1,0:T(8,128)(2,1)S(1)}, u32[]{:S(2)}, u32[]{:S(2)}) collective-permute-start(bf16[8,64,128]{2,1,0:T(8,128)(2,1)S(1)} %get-tuple-element.127.refs_0_), channel_id=1, source_target_pairs={{0,16},{16,0},{32,48},{48,32},{64,80},{80,64},{96,112},{112,96},{1... | collective-permute-start | bytes 393224 | tf_op jit(solution)/shard_map/ppermute | solution.py:415
  125.2 24.5 %all-to-all-start.3 = ((bf16[16,256,128]{2,1,0:T(8,128)(2,1)}), bf16[16,256,128]{2,1,0:T(8,128)(2,1)S(1)}, u32[]{:S(2)}, u32[]{:S(2)}) async-start(bf16[16,256,128]{2,1,0:T(8,128)(2,1)} %get-tuple-element.130), calls=%async_computation.3 | async-start | bytes 2097152 | tf_op jit(solution)/shard_map/all_to_all | solution.py:424
  132.6 6.4 %collective-permute-start.35 = (bf16[8,64,128]{2,1,0:T(8,128)(2,1)S(1)}, bf16[8,64,128]{2,1,0:T(8,128)(2,1)S(1)}, u32[]{:S(2)}, u32[]{:S(2)}) collective-permute-start(bf16[8,64,128]{2,1,0:T(8,128)(2,1)S(1)} %get-tuple-element.143.refs_0_), channel_id=1, source_target_pairs={{0,32},{16,48},{32,64},{48,80},{64,96},{80,112},{96,0},{112,16},{1... | collective-permute-start | bytes 393224 | tf_op jit(solution)/shard_map/ppermute | solution.py:414
  132.9 7.9 %collective-permute-start.36 = (bf16[8,64,128]{2,1,0:T(8,128)(2,1)S(1)}, bf16[8,64,128]{2,1,0:T(8,128)(2,1)S(1)}, u32[]{:S(2)}, u32[]{:S(2)}) collective-permute-start(bf16[8,64,128]{2,1,0:T(8,128)(2,1)S(1)} %get-tuple-element.143.refs_0_), channel_id=1, source_target_pairs={{0,64},{16,80},{32,96},{48,112},{64,0},{80,16},{96,32},{112,48},{1... | collective-permute-start | bytes 393224 | tf_op jit(solution)/shard_map/ppermute | solution.py:414
  134.7 7.7 %collective-permute-start.37 = (bf16[8,64,128]{2,1,0:T(8,128)(2,1)S(1)}, bf16[8,64,128]{2,1,0:T(8,128)(2,1)S(1)}, u32[]{:S(2)}, u32[]{:S(2)}) collective-permute-start(bf16[8,64,128]{2,1,0:T(8,128)(2,1)S(1)} %get-tuple-element.143.refs_0_), channel_id=1, source_target_pairs={{0,96},{16,112},{32,0},{48,16},{64,32},{80,48},{96,64},{112,80},{1... | collective-permute-start | bytes 393224 | tf_op jit(solution)/shard_map/ppermute | solution.py:414
  137.2 5.2 %collective-permute-start.38 = (bf16[8,64,128]{2,1,0:T(8,128)(2,1)S(1)}, bf16[8,64,128]{2,1,0:T(8,128)(2,1)S(1)}, u32[]{:S(2)}, u32[]{:S(2)}) collective-permute-start(bf16[8,64,128]{2,1,0:T(8,128)(2,1)S(1)} %get-tuple-element.143.refs_0_), channel_id=1, source_target_pairs={{0,16},{16,0},{32,48},{48,32},{64,80},{80,64},{96,112},{112,96},{1... | collective-permute-start | bytes 393224 | tf_op jit(solution)/shard_map/ppermute | solution.py:415
  149.7 24.5 %all-to-all-start.7 = ((bf16[16,256,128]{2,1,0:T(8,128)(2,1)}), bf16[16,256,128]{2,1,0:T(8,128)(2,1)S(1)}, u32[]{:S(2)}, u32[]{:S(2)}) async-start(bf16[16,256,128]{2,1,0:T(8,128)(2,1)} %get-tuple-element.146), calls=%async_computation.7 | async-start | bytes 2097152 | tf_op jit(solution)/shard_map/all_to_all | solution.py:424
  157.0 6.4 %collective-permute-start.14 = (bf16[8,64,128]{2,1,0:T(8,128)(2,1)S(1)}, bf16[8,64,128]{2,1,0:T(8,128)(2,1)S(1)}, u32[]{:S(2)}, u32[]{:S(2)}) collective-permute-start(bf16[8,64,128]{2,1,0:T(8,128)(2,1)S(1)} %get-tuple-element.131.refs_0_), channel_id=1, source_target_pairs={{0,32},{16,48},{32,64},{48,80},{64,96},{80,112},{96,0},{112,16},{1... | collective-permute-start | bytes 393224 | tf_op jit(solution)/shard_map/ppermute | solution.py:414
  157.5 7.9 %collective-permute-start.15 = (bf16[8,64,128]{2,1,0:T(8,128)(2,1)S(1)}, bf16[8,64,128]{2,1,0:T(8,128)(2,1)S(1)}, u32[]{:S(2)}, u32[]{:S(2)}) collective-permute-start(bf16[8,64,128]{2,1,0:T(8,128)(2,1)S(1)} %get-tuple-element.131.refs_0_), channel_id=1, source_target_pairs={{0,64},{16,80},{32,96},{48,112},{64,0},{80,16},{96,32},{112,48},{1... | collective-permute-start | bytes 393224 | tf_op jit(solution)/shard_map/ppermute | solution.py:414
  159.0 7.9 %collective-permute-start.16 = (bf16[8,64,128]{2,1,0:T(8,128)(2,1)S(1)}, bf16[8,64,128]{2,1,0:T(8,128)(2,1)S(1)}, u32[]{:S(2)}, u32[]{:S(2)}) collective-permute-start(bf16[8,64,128]{2,1,0:T(8,128)(2,1)S(1)} %get-tuple-element.131.refs_0_), channel_id=1, source_target_pairs={{0,96},{16,112},{32,0},{48,16},{64,32},{80,48},{96,64},{112,80},{1... | collective-permute-start | bytes 393224 | tf_op jit(solution)/shard_map/ppermute | solution.py:414
  161.5 5.4 %collective-permute-start.17 = (bf16[8,64,128]{2,1,0:T(8,128)(2,1)S(1)}, bf16[8,64,128]{2,1,0:T(8,128)(2,1)S(1)}, u32[]{:S(2)}, u32[]{:S(2)}) collective-permute-start(bf16[8,64,128]{2,1,0:T(8,128)(2,1)S(1)} %get-tuple-element.131.refs_0_), channel_id=1, source_target_pairs={{0,16},{16,0},{32,48},{48,32},{64,80},{80,64},{96,112},{112,96},{1... | collective-permute-start | bytes 393224 | tf_op jit(solution)/shard_map/ppermute | solution.py:415
  174.2 24.5 %all-to-all-start.4 = ((bf16[16,256,128]{2,1,0:T(8,128)(2,1)}), bf16[16,256,128]{2,1,0:T(8,128)(2,1)S(1)}, u32[]{:S(2)}, u32[]{:S(2)}) async-start(bf16[16,256,128]{2,1,0:T(8,128)(2,1)} %get-tuple-element.134), calls=%async_computation.4 | async-start | bytes 2097152 | tf_op jit(solution)/shard_map/all_to_all | solution.py:424
  (25 other events, 123.0 us)
where the time goes:
time: 204 us; the launch traced here: 201 us
  waiting for transfers between devices  77 us (38%)
  starting transfers between devices  71.3 us (35%)
  Pallas kernels  44.4 us (22%)
  between operations  3.7 us (2%)
  local copies, waits for them, and re-layouts  3.69 us (2%)
    all_to_all x7, starting transfers between devices, exchange(): return lax.all_to_all(sent, 'col', split_axis=0, concat_axis=0, tiled=True)  43.9 us
    all_to_all x7, waiting for transfers between devices, exchange(): return lax.all_to_all(sent, 'col', split_axis=0, concat_axis=0, tiled=True)  36.6 us
    ppermute x18, waiting for transfers between devices, column_parts(): lax.ppermute(mine, 'row', row_shift(dz, 0))  32.5 us
    ppermute x18, starting transfers between devices, column_parts(): lax.ppermute(mine, 'row', row_shift(dz, 0))  27.3 us
    pallas_call x6, Pallas kernels, products(): pl.pallas_call(body, out_shape=(jax.ShapeDtypeStruct((owners, rows, tile)...  27.1 us
    ppermute x24, waiting for transfers between devices, column_parts(): other = [lax.ppermute(part, 'row', row_shift(0, 1)) for part in same]  7.88 us
    pallas_call x1, Pallas kernels, first_products(): pl.pallas_call(body, out_shape=jax.ShapeDtypeStruct((n_col, sent_rows + I...  5.72 us
  transfers between devices with their start and end apart: 49, of which 32 were waited for; matrix products, arithmetic and copies ran while one was open for 0% of the time, Pallas kernels for 13%

commit v1 on v0

--- a/solution.py
+++ b/solution.py
@@ -23,6 +23,7 @@
 HBM = pl.BlockSpec(memory_space=pltpu.HBM)
 SMEM = pl.BlockSpec(memory_space=pltpu.SMEM)
 PARAMS = pltpu.CompilerParams(vmem_limit_bytes=VMEM_LIMIT)
+COVER = pl.CostEstimate(flops=int(8e9), bytes_accessed=int(40e6), transcendentals=0)
 F32 = jnp.float32
 BF16 = jnp.bfloat16
 
@@ -35,18 +36,7 @@
     return coef
 
 
-def multiply_tiles(slot_ref, place_ref, count, tiles_ref, x_parts, turned, acc_ref, x_ref, tile_ref, sems):
-    chunks = (count + CHUNK - 1) // CHUNK
-
-    def chunk_copy(chunk):
-        here = pl.ds(chunk * CHUNK, CHUNK)
-        return pltpu.make_async_copy(tiles_ref.at[here], tile_ref.at[here], sems.at[chunk])
-
-    def start(chunk, carry):
-        chunk_copy(chunk).start()
-        return carry
-
-    lax.fori_loop(0, chunks, start, 0)
+def multiply_tiles(slot_ref, place_ref, count, tile_ref, x_parts, acc_ref, x_ref):
     each = x_ref.shape[0] // len(x_parts)
     for part, part_ref in enumerate(x_parts):
         x_ref[part * each : (part + 1) * each] = part_ref[...]
@@ -56,34 +46,18 @@
         prods = []
         for lane in range(UNROLL):
             prods.append(
-                lax.dot_general(
-                    x_ref[place_ref[base + lane]],
-                    tile_ref[base + lane],
-                    (((1,), (0 if turned else 1,)), ((), ())),
-                    preferred_element_type=F32,
-                )
+                jnp.dot(x_ref[place_ref[base + lane]], tile_ref[base + lane], preferred_element_type=F32)
             )
         for lane in range(UNROLL):
             slot = slot_ref[base + lane]
             acc_ref[slot] = acc_ref[slot] + prods[lane]
 
     def chunk_step(chunk, carry):
-        chunk_copy(chunk).wait()
         for part in range(CHUNK // UNROLL):
             group(chunk * CHUNK + part * UNROLL)
         return carry
 
-    lax.fori_loop(0, chunks, chunk_step, 0)
-
-
-def tile_scratch(sent, blocks, width, tiles):
-    tile = tiles.shape[1]
-    return [
-        pltpu.VMEM((sent + 1, width, tile), F32),
-        pltpu.VMEM((blocks, width, tile), BF16),
-        pltpu.VMEM(tiles.shape, tiles.dtype),
-        pltpu.SemaphoreType.DMA((tiles.shape[0] // CHUNK,)),
-    ]
+    lax.fori_loop(0, (count + CHUNK - 1) // CHUNK, chunk_step, 0)
 
 
 def first_products(round_index, rows, cols, query_ids, count, col, tiles, n_col, n_row):
@@ -233,7 +207,7 @@
         out_ref, score_out, score_ref, score_sems, acc_ref, *scratch = refs
         for ref in score_in:
             pltpu.make_async_copy(ref, score_ref, score_sems.at[0]).start()
-        multiply_tiles(slot_ref, place_ref, count_ref[0], tiles_ref, x_refs, True, acc_ref, *scratch)
+        multiply_tiles(slot_ref, place_ref, count_ref[0], tiles_ref, x_refs, acc_ref, *scratch)
         for ref in score_in:
             pltpu.make_async_copy(ref, score_ref, score_sems.at[0]).wait()
         if score_in:
@@ -251,12 +225,13 @@
             jax.ShapeDtypeStruct((owners, rows, tile), BF16),
             pltpu.HBM((BPD, width, tile), F32),
         ),
-        in_specs=[SMEM, SMEM, SMEM, HBM] + [VMEM] * (parts + 2) + [HBM] * len(before),
+        in_specs=[SMEM, SMEM, SMEM, VMEM] + [VMEM] * (parts + 2) + [HBM] * len(before),
         out_specs=(VMEM, HBM),
         scratch_shapes=[
             pltpu.VMEM((BPD, width, tile), F32),
             pltpu.SemaphoreType.DMA((2,)),
-            *tile_scratch(owners * TOUCH, parts * each, width, turned),
+            pltpu.VMEM((owners * TOUCH + 1, width, tile), F32),
+            pltpu.VMEM((parts * each, width, tile), BF16),
         ],
         compiler_params=PARAMS,
         name="products",
@@ -264,7 +239,7 @@
         slots,
         places,
         count,
-        pltpu.with_memory_space_constraint(turned, pltpu.HBM),
+        turned,
         *xparts,
         damping,
         owned,
@@ -320,6 +295,7 @@
         out_specs=(VMEM, VMEM),
         scratch_shapes=[pltpu.VMEM((BPD + 1, width, tile), F32)],
         compiler_params=PARAMS,
+        cost_estimate=COVER,
         name="owned",
     )(ids, got)
 
@@ -330,8 +306,7 @@
     streams = queries // width
 
     def body(id_ref, got_ref, spread_ref, *refs):
-        whole_refs, refs = refs[: len(before)], refs[len(before) :]
-        x_refs, out_refs, piece_ref = refs[:streams], refs[streams : 2 * streams], refs[-1]
+        whole_refs, out_refs, piece_ref = refs[: len(before)], refs[len(before) : -1], refs[-1]
         piece_ref[...] = jnp.zeros(piece_ref.shape, BF16)
         for source in range(sources):
             for place in range(TOUCH):
@@ -345,19 +320,34 @@
                 mine = owned[stream * width : (stream + 1) * width]
                 if whole_refs:
                     mine = mine + whole_refs[stream][block]
-                x_refs[stream][block] = mine.astype(BF16)
                 out_refs[stream][block] = mine
 
     shape = (BPD, width, tile)
     return pl.pallas_call(
         body,
-        out_shape=[jax.ShapeDtypeStruct(shape, BF16)] * streams + [jax.ShapeDtypeStruct(shape, F32)] * streams,
+        out_shape=[jax.ShapeDtypeStruct(shape, F32)] * streams,
         in_specs=[SMEM] + [VMEM] * (2 + len(before)),
-        out_specs=[VMEM] * (2 * streams),
+        out_specs=[VMEM] * streams,
         scratch_shapes=[pltpu.VMEM((BPD + 1, columns, tile), BF16)],
         compiler_params=PARAMS,
         name="placed",
     )(ids, got, spread, *before)
+
+
+def rounded(wholes):
+    def body(*refs):
+        for whole_ref, out_ref in zip(refs[: len(wholes)], refs[len(wholes) :]):
+            out_ref[...] = whole_ref[...].astype(BF16)
+
+    return pl.pallas_call(
+        body,
+        out_shape=[jax.ShapeDtypeStruct(whole.shape, BF16) for whole in wholes],
+        in_specs=[VMEM] * len(wholes),
+        out_specs=[VMEM] * len(wholes),
+        compiler_params=PARAMS,
+        cost_estimate=COVER,
+        name="rounded",
+    )(*wholes)
 
 
 def ended_sum(step, ids, got, damping, scores):
@@ -477,7 +467,7 @@
     def next_round(state):
         index, *sums = state
         got = exchange(first_sent(index))
-        return index + 1, *placed_sum(got_ids, got, spread(index), width, sums[STREAMS:])
+        return index + 1, *placed_sum(got_ids, got, spread(index), width, sums)
 
     _, *sums = lax.while_loop(lambda state: state[0] < rounds, next_round, (jnp.int32(1), *sums))
     count = count.reshape(1)
@@ -485,8 +475,8 @@
         jnp.broadcast_to(damping[stream * width : (stream + 1) * width][:, None], (width, tile))
         for stream in range(STREAMS)
     ]
-    xparts = [column_parts(sums[stream]) for stream in range(STREAMS)]
-    owned, scores = sums[STREAMS:], [None] * STREAMS
+    xparts = [column_parts(mine) for mine in rounded(sums)]
+    owned, scores = sums, [None] * STREAMS
     for step in range(1, TERMS):
         for stream in range(STREAMS):
             sent, scores[stream] = products(

time: 204 us -> 198 us (0.971)
  Pallas kernels: 44.4 us -> 36.7 us
  starting transfers between devices: 71.3 us -> 67.9 us
  waiting for transfers between devices: 77 us -> 80.2 us
  local copies, waits for them, and re-layouts: 3.69 us -> 5.9 us
    pallas_call x6, Pallas kernels: 27.1 us -> 20 us  [products(): pl.pallas_call(body, out_shape=(jax.ShapeDtypeStruct((owners, rows, tile)...]
    all_to_all x7, starting transfers between devices: 43.9 us -> 40.4 us  [exchange(): return lax.all_to_all(sent, 'col', split_axis=0, concat_axis=0, tiled=True)]
    all_to_all x7, waiting for transfers between devices: 36.6 us -> 40 us  [exchange(): return lax.all_to_all(sent, 'col', split_axis=0, concat_axis=0, tiled=True)]
    unnamed x16 -> x26, local copies, waits for them, and re-layouts: 2.96 us -> 5.18 us
  transfers between devices with their start and end apart: 49 -> 49, of which waited for: 32 -> 32; matrix products, arithmetic and copies ran while one was open for 0% -> 0% of each run, Pallas kernels for 13% -> 11%
where the time goes in v1:
time: 198 us; the launch traced here: 196 us
  waiting for transfers between devices  80.2 us (41%)
  starting transfers between devices  67.9 us (34%)
  Pallas kernels  36.7 us (19%)
  local copies, waits for them, and re-layouts  5.9 us (3%)
  between operations  3.94 us (2%)
    all_to_all x7, starting transfers between devices, exchange(): return lax.all_to_all(sent, 'col', split_axis=0, concat_axis=0, tiled=True)  40.4 us
    all_to_all x7, waiting for transfers between devices, exchange(): return lax.all_to_all(sent, 'col', split_axis=0, concat_axis=0, tiled=True)  40 us
    ppermute x18, waiting for transfers between devices, column_parts(): lax.ppermute(mine, 'row', row_shift(dz, 0))  32.3 us
    ppermute x18, starting transfers between devices, column_parts(): lax.ppermute(mine, 'row', row_shift(dz, 0))  27.3 us
    pallas_call x6, Pallas kernels, products(): pl.pallas_call(body, out_shape=(jax.ShapeDtypeStruct((owners, rows, tile)...  20 us
    ppermute x24, waiting for transfers between devices, column_parts(): other = [lax.ppermute(part, 'row', row_shift(0, 1)) for part in same]  7.88 us
    pallas_call x1, Pallas kernels, first_products(): pl.pallas_call(body, out_shape=jax.ShapeDtypeStruct((n_col, sent_rows + I...  5.74 us
    unnamed x26, local copies, waits for them, and re-layouts  5.18 us
  transfers between devices with their start and end apart: 49, of which 32 were waited for; matrix products, arithmetic and copies ran while one was open for 0% of the time, Pallas kernels for 11%

profile of v1, /device:TPU:32, one launch (start us, length us, event | category | flops | bytes accessed | tf_op | source)
XLA Modules:
  0.0 196.1 jit_solution(18406028366692516767)
XLA Ops:
  0.8 5.7 %first_products.2 = bf16[16,144,128]{2,1,0:T(8,128)(2,1)} custom-call(s32[3]{0:T(128)S(1)} %pad_add_fusion.1.info_ref, s32[128]{0:T(128)} %bitcast.32, s32[128]{0:T(128)} %bitcast.30, s32[128]{0:T(128)} %query_ref.1, bf16[128,128,128]{2,1,0:T(8,128)(2,1)} %bitcast.27), custom_call_target="tpu_custom_call" | custom-call | tf_op jit(solution)/shard_map/first_products/pallas_call | solution.py:175
  10.9 3.2 %turned.1.tiles_ref = bf16[128,128,128]{2,1,0:T(8,128)(2,1)S(1)} custom-call(s32[1]{0:T(128)} %bitcast.18.count_ref, bf16[128,128,128]{2,1,0:T(8,128)(2,1)} %bitcast.28), custom_call_target="tpu_custom_call" | custom-call | tf_op jit(solution)/shard_map/turned/pallas_call | solution.py:259
  14.1 2.0 %copy-done = bf16[128,128,128]{2,1,0:T(8,128)(2,1)} copy-done((bf16[128,128,128]{2,1,0:T(8,128)(2,1)}, bf16[128,128,128]{2,1,0:T(8,128)(2,1)S(1)}, u32[]{:S(2)}) %copy-start) | copy-done | bytes 4194328
  16.0 8.0 %all-to-all-start.1 = ((bf16[16,144,128]{2,1,0:T(8,128)(2,1)}), bf16[16,144,128]{2,1,0:T(8,128)(2,1)S(1)}, u32[]{:S(2)}, u32[]{:S(2)}) async-start(bf16[16,144,128]{2,1,0:T(8,128)(2,1)} %first_products.2), calls=%async_computation.1 | async-start | bytes 1179648 | tf_op jit(solution)/shard_map/all_to_all | solution.py:414
  24.3 12.0 %all-to-all-done.1.got_ref = bf16[16,144,128]{2,1,0:T(8,128)(2,1)S(1)} async-done(((bf16[16,144,128]{2,1,0:T(8,128)(2,1)}), bf16[16,144,128]{2,1,0:T(8,128)(2,1)S(1)}, u32[]{:S(2)}, u32[]{:S(2)}) %all-to-all-start.1) | async-done | bytes 589856 | tf_op jit(solution)/shard_map/all_to_all | solution.py:414
  43.5 2.7 %collective-permute-done.22.refs_2_ = bf16[8,64,128]{2,1,0:T(8,128)(2,1)S(1)} collective-permute-done((bf16[8,64,128]{2,1,0:T(8,128)(2,1)S(1)}, bf16[8,64,128]{2,1,0:T(8,128)(2,1)S(1)}, u32[]{:S(2)}, u32[]{:S(2)}) %collective-permute-start.22) | collective-permute-done | bytes 131104 | tf_op jit(solution)/shard_map/ppermute | solution.py:404
  48.8 3.3 %products.9 = (bf16[16,256,128]{2,1,0:T(8,128)(2,1)}, f32[8,64,128]{2,1,0:T(8,128)}) custom-call(s32[128]{0:T(128)S(1)} %get-tuple-element.165.slot_ref, s32[128]{0:T(128)S(1)} %get-tuple-element.164.place_ref, s32[1]{0:T(128)} %bitcast.22.count_ref, bf16[128,128,128]{2,1,0:T(8,128)(2,1)S(1)} %copy-done.1, ...), custom_call_target="tpu_custom_call" | custom-call | tf_op jit(solution)/shard_map/products/pallas_call | solution.py:222
  52.1 4.5 %all-to-all-start.5 = ((bf16[16,256,128]{2,1,0:T(8,128)(2,1)}), bf16[16,256,128]{2,1,0:T(8,128)(2,1)S(1)}, u32[]{:S(2)}, u32[]{:S(2)}) async-start(bf16[16,256,128]{2,1,0:T(8,128)(2,1)} %get-tuple-element.124), calls=%async_computation.5 | async-start | bytes 2097152 | tf_op jit(solution)/shard_map/all_to_all | solution.py:414
  58.8 2.5 %collective-permute-start.2 = (bf16[8,64,128]{2,1,0:T(8,128)(2,1)S(1)}, bf16[8,64,128]{2,1,0:T(8,128)(2,1)S(1)}, u32[]{:S(2)}, u32[]{:S(2)}) collective-permute-start(bf16[8,64,128]{2,1,0:T(8,128)(2,1)S(1)} %get-tuple-element.112.refs_0_), channel_id=1, source_target_pairs={{0,96},{16,112},{32,0},{48,16},{64,32},{80,48},{96,64},{112,80},{1... | collective-permute-start | bytes 393224 | tf_op jit(solution)/shard_map/ppermute | solution.py:404
  62.3 2.7 %collective-permute-done.1.refs_2_ = bf16[8,64,128]{2,1,0:T(8,128)(2,1)S(1)} collective-permute-done((bf16[8,64,128]{2,1,0:T(8,128)(2,1)S(1)}, bf16[8,64,128]{2,1,0:T(8,128)(2,1)S(1)}, u32[]{:S(2)}, u32[]{:S(2)}) %collective-permute-start.1) | collective-permute-done | bytes 131104 | tf_op jit(solution)/shard_map/ppermute | solution.py:404
  68.3 2.2 %copy-done.2 = bf16[128,128,128]{2,1,0:T(8,128)(2,1)S(1)} copy-done((bf16[128,128,128]{2,1,0:T(8,128)(2,1)S(1)}, bf16[128,128,128]{2,1,0:T(8,128)(2,1)}, u32[]{:S(2)}) %copy-start.2) | copy-done | bytes 4194328
  70.5 3.3 %products.6 = (bf16[16,256,128]{2,1,0:T(8,128)(2,1)}, f32[8,64,128]{2,1,0:T(8,128)}) custom-call(s32[128]{0:T(128)S(1)} %get-tuple-element.165.slot_ref, s32[128]{0:T(128)S(1)} %get-tuple-element.164.place_ref, s32[1]{0:T(128)} %bitcast.19.count_ref, bf16[128,128,128]{2,1,0:T(8,128)(2,1)S(1)} %copy-done.2, ...), custom_call_target="tpu_custom_call" | custom-call | tf_op jit(solution)/shard_map/products/pallas_call | solution.py:222
  74.8 6.6 %all-to-all-start.2 = ((bf16[16,256,128]{2,1,0:T(8,128)(2,1)}), bf16[16,256,128]{2,1,0:T(8,128)(2,1)S(1)}, u32[]{:S(2)}, u32[]{:S(2)}) async-start(bf16[16,256,128]{2,1,0:T(8,128)(2,1)} %get-tuple-element.113), calls=%async_computation.2 | async-start | bytes 2097152 | tf_op jit(solution)/shard_map/all_to_all | solution.py:414
  84.5 2.5 %collective-permute-start.30 = (bf16[8,64,128]{2,1,0:T(8,128)(2,1)S(1)}, bf16[8,64,128]{2,1,0:T(8,128)(2,1)S(1)}, u32[]{:S(2)}, u32[]{:S(2)}) collective-permute-start(bf16[8,64,128]{2,1,0:T(8,128)(2,1)S(1)} %get-tuple-element.125.refs_0_), channel_id=1, source_target_pairs={{0,96},{16,112},{32,0},{48,16},{64,32},{80,48},{96,64},{112,80},{1... | collective-permute-start | bytes 393224 | tf_op jit(solution)/shard_map/ppermute | solution.py:404
  88.9 2.0 %collective-permute-done.29.refs_2_ = bf16[8,64,128]{2,1,0:T(8,128)(2,1)S(1)} collective-permute-done((bf16[8,64,128]{2,1,0:T(8,128)(2,1)S(1)}, bf16[8,64,128]{2,1,0:T(8,128)(2,1)S(1)}, u32[]{:S(2)}, u32[]{:S(2)}) %collective-permute-start.29) | collective-permute-done | bytes 131104 | tf_op jit(solution)/shard_map/ppermute | solution.py:404
  93.9 3.3 %products.10 = (bf16[16,256,128]{2,1,0:T(8,128)(2,1)}, f32[8,64,128]{2,1,0:T(8,128)}) custom-call(s32[128]{0:T(128)S(1)} %get-tuple-element.165.slot_ref, s32[128]{0:T(128)S(1)} %get-tuple-element.164.place_ref, s32[1]{0:T(128)} %bitcast.23.count_ref, bf16[128,128,128]{2,1,0:T(8,128)(2,1)S(1)} %copy-done.3, ...), custom_call_target="tpu_custom_call" | custom-call | tf_op jit(solution)/shard_map/products/pallas_call | solution.py:222
  97.3 2.3 %all-to-all-done.2.got_ref = bf16[16,256,128]{2,1,0:T(8,128)(2,1)S(1)} async-done(((bf16[16,256,128]{2,1,0:T(8,128)(2,1)}), bf16[16,256,128]{2,1,0:T(8,128)(2,1)S(1)}, u32[]{:S(2)}, u32[]{:S(2)}) %all-to-all-start.2) | async-done | bytes 1048608 | tf_op jit(solution)/shard_map/all_to_all | solution.py:414
  99.5 5.5 %all-to-all-start.6 = ((bf16[16,256,128]{2,1,0:T(8,128)(2,1)}), bf16[16,256,128]{2,1,0:T(8,128)(2,1)S(1)}, u32[]{:S(2)}, u32[]{:S(2)}) async-start(bf16[16,256,128]{2,1,0:T(8,128)(2,1)} %get-tuple-element.128), calls=%async_computation.6 | async-start | bytes 2097152 | tf_op jit(solution)/shard_map/all_to_all | solution.py:414
  106.4 2.0 %collective-permute-start.8 = (bf16[8,64,128]{2,1,0:T(8,128)(2,1)S(1)}, bf16[8,64,128]{2,1,0:T(8,128)(2,1)S(1)}, u32[]{:S(2)}, u32[]{:S(2)}) collective-permute-start(bf16[8,64,128]{2,1,0:T(8,128)(2,1)S(1)} %get-tuple-element.114.refs_0_), channel_id=1, source_target_pairs={{0,64},{16,80},{32,96},{48,112},{64,0},{80,16},{96,32},{112,48},{1... | collective-permute-start | bytes 393224 | tf_op jit(solution)/shard_map/ppermute | solution.py:404
  108.4 2.5 %collective-permute-start.9 = (bf16[8,64,128]{2,1,0:T(8,128)(2,1)S(1)}, bf16[8,64,128]{2,1,0:T(8,128)(2,1)S(1)}, u32[]{:S(2)}, u32[]{:S(2)}) collective-permute-start(bf16[8,64,128]{2,1,0:T(8,128)(2,1)S(1)} %get-tuple-element.114.refs_0_), channel_id=1, source_target_pairs={{0,96},{16,112},{32,0},{48,16},{64,32},{80,48},{96,64},{112,80},{1... | collective-permute-start | bytes 393224 | tf_op jit(solution)/shard_map/ppermute | solution.py:404
  117.3 3.3 %products.7 = (bf16[16,256,128]{2,1,0:T(8,128)(2,1)}, f32[8,64,128]{2,1,0:T(8,128)}) custom-call(s32[128]{0:T(128)S(1)} %get-tuple-element.165.slot_ref, s32[128]{0:T(128)S(1)} %get-tuple-element.164.place_ref, s32[1]{0:T(128)} %bitcast.20.count_ref, bf16[128,128,128]{2,1,0:T(8,128)(2,1)S(1)} %copy-done.4, ...), custom_call_target="tpu_custom_call" | custom-call | tf_op jit(solution)/shard_map/products/pallas_call | solution.py:222
  120.7 2.5 %all-to-all-done.6.got_ref = bf16[16,256,128]{2,1,0:T(8,128)(2,1)S(1)} async-done(((bf16[16,256,128]{2,1,0:T(8,128)(2,1)}), bf16[16,256,128]{2,1,0:T(8,128)(2,1)S(1)}, u32[]{:S(2)}, u32[]{:S(2)}) %all-to-all-start.6) | async-done | bytes 1048608 | tf_op jit(solution)/shard_map/all_to_all | solution.py:414
  123.2 5.3 %all-to-all-start.3 = ((bf16[16,256,128]{2,1,0:T(8,128)(2,1)}), bf16[16,256,128]{2,1,0:T(8,128)(2,1)S(1)}, u32[]{:S(2)}, u32[]{:S(2)}) async-start(bf16[16,256,128]{2,1,0:T(8,128)(2,1)} %get-tuple-element.117), calls=%async_computation.3 | async-start | bytes 2097152 | tf_op jit(solution)/shard_map/all_to_all | solution.py:414
  131.5 2.5 %collective-permute-start.37 = (bf16[8,64,128]{2,1,0:T(8,128)(2,1)S(1)}, bf16[8,64,128]{2,1,0:T(8,128)(2,1)S(1)}, u32[]{:S(2)}, u32[]{:S(2)}) collective-permute-start(bf16[8,64,128]{2,1,0:T(8,128)(2,1)S(1)} %get-tuple-element.129.refs_0_), channel_id=1, source_target_pairs={{0,96},{16,112},{32,0},{48,16},{64,32},{80,48},{96,64},{112,80},{1... | collective-permute-start | bytes 393224 | tf_op jit(solution)/shard_map/ppermute | solution.py:404
  140.7 3.3 %products.11 = (bf16[16,256,128]{2,1,0:T(8,128)(2,1)}, f32[8,64,128]{2,1,0:T(8,128)}) custom-call(s32[128]{0:T(128)S(1)} %get-tuple-element.165.slot_ref, s32[128]{0:T(128)S(1)} %get-tuple-element.164.place_ref, s32[1]{0:T(128)} %bitcast.24.count_ref, bf16[128,128,128]{2,1,0:T(8,128)(2,1)S(1)} %copy-done.5, ...), custom_call_target="tpu_custom_call" | custom-call | tf_op jit(solution)/shard_map/products/pallas_call | solution.py:222
  144.0 2.5 %all-to-all-done.3.got_ref = bf16[16,256,128]{2,1,0:T(8,128)(2,1)S(1)} async-done(((bf16[16,256,128]{2,1,0:T(8,128)(2,1)}), bf16[16,256,128]{2,1,0:T(8,128)(2,1)S(1)}, u32[]{:S(2)}, u32[]{:S(2)}) %all-to-all-start.3) | async-done | bytes 1048608 | tf_op jit(solution)/shard_map/all_to_all | solution.py:414
  146.6 5.2 %all-to-all-start.7 = ((bf16[16,256,128]{2,1,0:T(8,128)(2,1)}), bf16[16,256,128]{2,1,0:T(8,128)(2,1)S(1)}, u32[]{:S(2)}, u32[]{:S(2)}) async-start(bf16[16,256,128]{2,1,0:T(8,128)(2,1)} %get-tuple-element.132), calls=%async_computation.7 | async-start | bytes 2097152 | tf_op jit(solution)/shard_map/all_to_all | solution.py:414
  154.8 2.5 %collective-permute-start.16 = (bf16[8,64,128]{2,1,0:T(8,128)(2,1)S(1)}, bf16[8,64,128]{2,1,0:T(8,128)(2,1)S(1)}, u32[]{:S(2)}, u32[]{:S(2)}) collective-permute-start(bf16[8,64,128]{2,1,0:T(8,128)(2,1)S(1)} %get-tuple-element.118.refs_0_), channel_id=1, source_target_pairs={{0,96},{16,112},{32,0},{48,16},{64,32},{80,48},{96,64},{112,80},{1... | collective-permute-start | bytes 393224 | tf_op jit(solution)/shard_map/ppermute | solution.py:404
  164.0 3.4 %products.8 = (bf16[16,256,128]{2,1,0:T(8,128)(2,1)}, f32[8,64,128]{2,1,0:T(8,128)}) custom-call(s32[128]{0:T(128)S(1)} %get-tuple-element.165.slot_ref, s32[128]{0:T(128)S(1)} %get-tuple-element.164.place_ref, s32[1]{0:T(128)} %bitcast.21.count_ref, bf16[128,128,128]{2,1,0:T(8,128)(2,1)S(1)} %copy-done.6, ...), custom_call_target="tpu_custom_call" | custom-call | tf_op jit(solution)/shard_map/products/pallas_call | solution.py:222
  167.4 2.5 %all-to-all-done.7.got_ref = bf16[16,256,128]{2,1,0:T(8,128)(2,1)S(1)} async-done(((bf16[16,256,128]{2,1,0:T(8,128)(2,1)}), bf16[16,256,128]{2,1,0:T(8,128)(2,1)S(1)}, u32[]{:S(2)}, u32[]{:S(2)}) %all-to-all-start.7) | async-done | bytes 1048608 | tf_op jit(solution)/shard_map/all_to_all | solution.py:414
  169.9 5.2 %all-to-all-start.4 = ((bf16[16,256,128]{2,1,0:T(8,128)(2,1)}), bf16[16,256,128]{2,1,0:T(8,128)(2,1)S(1)}, u32[]{:S(2)}, u32[]{:S(2)}) async-start(bf16[16,256,128]{2,1,0:T(8,128)(2,1)} %get-tuple-element.121), calls=%async_computation.4 | async-start | bytes 2097152 | tf_op jit(solution)/shard_map/all_to_all | solution.py:414
  176.1 17.2 %all-to-all-done.4.got_ref = bf16[16,256,128]{2,1,0:T(8,128)(2,1)S(1)} async-done(((bf16[16,256,128]{2,1,0:T(8,128)(2,1)}), bf16[16,256,128]{2,1,0:T(8,128)(2,1)S(1)}, u32[]{:S(2)}, u32[]{:S(2)}) %all-to-all-start.4) | async-done | bytes 1048608 | tf_op jit(solution)/shard_map/all_to_all | solution.py:414
  (133 shorter events, 57.6 us)
Async XLA Ops:
  16.0 20.2 %all-to-all-start.1 = ((bf16[16,144,128]{2,1,0:T(8,128)(2,1)}), bf16[16,144,128]{2,1,0:T(8,128)(2,1)S(1)}, u32[]{:S(2)}, u32[]{:S(2)}) async-start(bf16[16,144,128]{2,1,0:T(8,128)(2,1)} %first_products.2), calls=%async_computation.1 | async-start | bytes 1179648 | tf_op jit(solution)/shard_map/all_to_all | solution.py:414
  37.7 5.8 %collective-permute-start.21 = (bf16[8,64,128]{2,1,0:T(8,128)(2,1)S(1)}, bf16[8,64,128]{2,1,0:T(8,128)(2,1)S(1)}, u32[]{:S(2)}, u32[]{:S(2)}) collective-permute-start(bf16[8,64,128]{2,1,0:T(8,128)(2,1)S(1)} %get-tuple-element.123.refs_0_), channel_id=1, source_target_pairs={{0,32},{16,48},{32,64},{48,80},{64,96},{80,112},{96,0},{112,16},{1... | collective-permute-start | bytes 393224 | tf_op jit(solution)/shard_map/ppermute | solution.py:404
  39.7 6.6 %collective-permute-start.22 = (bf16[8,64,128]{2,1,0:T(8,128)(2,1)S(1)}, bf16[8,64,128]{2,1,0:T(8,128)(2,1)S(1)}, u32[]{:S(2)}, u32[]{:S(2)}) collective-permute-start(bf16[8,64,128]{2,1,0:T(8,128)(2,1)S(1)} %get-tuple-element.123.refs_0_), channel_id=1, source_target_pairs={{0,64},{16,80},{32,96},{48,112},{64,0},{80,16},{96,32},{112,48},{1... | collective-permute-start | bytes 393224 | tf_op jit(solution)/shard_map/ppermute | solution.py:404
  40.0 7.4 %collective-permute-start.23 = (bf16[8,64,128]{2,1,0:T(8,128)(2,1)S(1)}, bf16[8,64,128]{2,1,0:T(8,128)(2,1)S(1)}, u32[]{:S(2)}, u32[]{:S(2)}) collective-permute-start(bf16[8,64,128]{2,1,0:T(8,128)(2,1)S(1)} %get-tuple-element.123.refs_0_), channel_id=1, source_target_pairs={{0,96},{16,112},{32,0},{48,16},{64,32},{80,48},{96,64},{112,80},{1... | collective-permute-start | bytes 393224 | tf_op jit(solution)/shard_map/ppermute | solution.py:404
  41.8 5.7 %collective-permute-start.24 = (bf16[8,64,128]{2,1,0:T(8,128)(2,1)S(1)}, bf16[8,64,128]{2,1,0:T(8,128)(2,1)S(1)}, u32[]{:S(2)}, u32[]{:S(2)}) collective-permute-start(bf16[8,64,128]{2,1,0:T(8,128)(2,1)S(1)} %get-tuple-element.123.refs_0_), channel_id=1, source_target_pairs={{0,16},{16,0},{32,48},{48,32},{64,80},{80,64},{96,112},{112,96},{1... | collective-permute-start | bytes 393224 | tf_op jit(solution)/shard_map/ppermute | solution.py:405
  52.1 22.7 %all-to-all-start.5 = ((bf16[16,256,128]{2,1,0:T(8,128)(2,1)}), bf16[16,256,128]{2,1,0:T(8,128)(2,1)S(1)}, u32[]{:S(2)}, u32[]{:S(2)}) async-start(bf16[16,256,128]{2,1,0:T(8,128)(2,1)} %get-tuple-element.124), calls=%async_computation.5 | async-start | bytes 2097152 | tf_op jit(solution)/shard_map/all_to_all | solution.py:414
  56.7 5.6 %collective-permute-start = (bf16[8,64,128]{2,1,0:T(8,128)(2,1)S(1)}, bf16[8,64,128]{2,1,0:T(8,128)(2,1)S(1)}, u32[]{:S(2)}, u32[]{:S(2)}) collective-permute-start(bf16[8,64,128]{2,1,0:T(8,128)(2,1)S(1)} %get-tuple-element.112.refs_0_), channel_id=1, source_target_pairs={{0,32},{16,48},{32,64},{48,80},{64,96},{80,112},{96,0},{112,16},{1... | collective-permute-start | bytes 393224 | tf_op jit(solution)/shard_map/ppermute | solution.py:404
  57.1 7.9 %collective-permute-start.1 = (bf16[8,64,128]{2,1,0:T(8,128)(2,1)S(1)}, bf16[8,64,128]{2,1,0:T(8,128)(2,1)S(1)}, u32[]{:S(2)}, u32[]{:S(2)}) collective-permute-start(bf16[8,64,128]{2,1,0:T(8,128)(2,1)S(1)} %get-tuple-element.112.refs_0_), channel_id=1, source_target_pairs={{0,64},{16,80},{32,96},{48,112},{64,0},{80,16},{96,32},{112,48},{1... | collective-permute-start | bytes 393224 | tf_op jit(solution)/shard_map/ppermute | solution.py:404
  58.8 8.1 %collective-permute-start.2 = (bf16[8,64,128]{2,1,0:T(8,128)(2,1)S(1)}, bf16[8,64,128]{2,1,0:T(8,128)(2,1)S(1)}, u32[]{:S(2)}, u32[]{:S(2)}) collective-permute-start(bf16[8,64,128]{2,1,0:T(8,128)(2,1)S(1)} %get-tuple-element.112.refs_0_), channel_id=1, source_target_pairs={{0,96},{16,112},{32,0},{48,16},{64,32},{80,48},{96,64},{112,80},{1... | collective-permute-start | bytes 393224 | tf_op jit(solution)/shard_map/ppermute | solution.py:404
  61.3 5.5 %collective-permute-start.3 = (bf16[8,64,128]{2,1,0:T(8,128)(2,1)S(1)}, bf16[8,64,128]{2,1,0:T(8,128)(2,1)S(1)}, u32[]{:S(2)}, u32[]{:S(2)}) collective-permute-start(bf16[8,64,128]{2,1,0:T(8,128)(2,1)S(1)} %get-tuple-element.112.refs_0_), channel_id=1, source_target_pairs={{0,16},{16,0},{32,48},{48,32},{64,80},{80,64},{96,112},{112,96},{1... | collective-permute-start | bytes 393224 | tf_op jit(solution)/shard_map/ppermute | solution.py:405
  62.3 4.6 %collective-permute-start.4 = (bf16[8,64,128]{2,1,0:T(8,128)(2,1)S(1)}, bf16[8,64,128]{2,1,0:T(8,128)(2,1)S(1)}, u32[]{:S(2)}, u32[]{:S(2)}) collective-permute-start(bf16[8,64,128]{2,1,0:T(8,128)(2,1)S(1)} %collective-permute-done.refs_1_), channel_id=1, source_target_pairs={{0,16},{16,0},{32,48},{48,32},{64,80},{80,64},{96,112},{112,96},{1... | collective-permute-start | bytes 393224 | tf_op jit(solution)/shard_map/ppermute | solution.py:405
  74.8 24.8 %all-to-all-start.2 = ((bf16[16,256,128]{2,1,0:T(8,128)(2,1)}), bf16[16,256,128]{2,1,0:T(8,128)(2,1)S(1)}, u32[]{:S(2)}, u32[]{:S(2)}) async-start(bf16[16,256,128]{2,1,0:T(8,128)(2,1)} %get-tuple-element.113), calls=%async_computation.2 | async-start | bytes 2097152 | tf_op jit(solution)/shard_map/all_to_all | solution.py:414
  82.4 6.4 %collective-permute-start.28 = (bf16[8,64,128]{2,1,0:T(8,128)(2,1)S(1)}, bf16[8,64,128]{2,1,0:T(8,128)(2,1)S(1)}, u32[]{:S(2)}, u32[]{:S(2)}) collective-permute-start(bf16[8,64,128]{2,1,0:T(8,128)(2,1)S(1)} %get-tuple-element.125.refs_0_), channel_id=1, source_target_pairs={{0,32},{16,48},{32,64},{48,80},{64,96},{80,112},{96,0},{112,16},{1... | collective-permute-start | bytes 393224 | tf_op jit(solution)/shard_map/ppermute | solution.py:404
  83.0 7.9 %collective-permute-start.29 = (bf16[8,64,128]{2,1,0:T(8,128)(2,1)S(1)}, bf16[8,64,128]{2,1,0:T(8,128)(2,1)S(1)}, u32[]{:S(2)}, u32[]{:S(2)}) collective-permute-start(bf16[8,64,128]{2,1,0:T(8,128)(2,1)S(1)} %get-tuple-element.125.refs_0_), channel_id=1, source_target_pairs={{0,64},{16,80},{32,96},{48,112},{64,0},{80,16},{96,32},{112,48},{1... | collective-permute-start | bytes 393224 | tf_op jit(solution)/shard_map/ppermute | solution.py:404
  84.5 8.1 %collective-permute-start.30 = (bf16[8,64,128]{2,1,0:T(8,128)(2,1)S(1)}, bf16[8,64,128]{2,1,0:T(8,128)(2,1)S(1)}, u32[]{:S(2)}, u32[]{:S(2)}) collective-permute-start(bf16[8,64,128]{2,1,0:T(8,128)(2,1)S(1)} %get-tuple-element.125.refs_0_), channel_id=1, source_target_pairs={{0,96},{16,112},{32,0},{48,16},{64,32},{80,48},{96,64},{112,80},{1... | collective-permute-start | bytes 393224 | tf_op jit(solution)/shard_map/ppermute | solution.py:404
  86.9 5.7 %collective-permute-start.31 = (bf16[8,64,128]{2,1,0:T(8,128)(2,1)S(1)}, bf16[8,64,128]{2,1,0:T(8,128)(2,1)S(1)}, u32[]{:S(2)}, u32[]{:S(2)}) collective-permute-start(bf16[8,64,128]{2,1,0:T(8,128)(2,1)S(1)} %get-tuple-element.125.refs_0_), channel_id=1, source_target_pairs={{0,16},{16,0},{32,48},{48,32},{64,80},{80,64},{96,112},{112,96},{1... | collective-permute-start | bytes 393224 | tf_op jit(solution)/shard_map/ppermute | solution.py:405
  99.5 23.6 %all-to-all-start.6 = ((bf16[16,256,128]{2,1,0:T(8,128)(2,1)}), bf16[16,256,128]{2,1,0:T(8,128)(2,1)S(1)}, u32[]{:S(2)}, u32[]{:S(2)}) async-start(bf16[16,256,128]{2,1,0:T(8,128)(2,1)} %get-tuple-element.128), calls=%async_computation.6 | async-start | bytes 2097152 | tf_op jit(solution)/shard_map/all_to_all | solution.py:414
  106.0 6.4 %collective-permute-start.7 = (bf16[8,64,128]{2,1,0:T(8,128)(2,1)S(1)}, bf16[8,64,128]{2,1,0:T(8,128)(2,1)S(1)}, u32[]{:S(2)}, u32[]{:S(2)}) collective-permute-start(bf16[8,64,128]{2,1,0:T(8,128)(2,1)S(1)} %get-tuple-element.114.refs_0_), channel_id=1, source_target_pairs={{0,32},{16,48},{32,64},{48,80},{64,96},{80,112},{96,0},{112,16},{1... | collective-permute-start | bytes 393224 | tf_op jit(solution)/shard_map/ppermute | solution.py:404
  106.4 7.9 %collective-permute-start.8 = (bf16[8,64,128]{2,1,0:T(8,128)(2,1)S(1)}, bf16[8,64,128]{2,1,0:T(8,128)(2,1)S(1)}, u32[]{:S(2)}, u32[]{:S(2)}) collective-permute-start(bf16[8,64,128]{2,1,0:T(8,128)(2,1)S(1)} %get-tuple-element.114.refs_0_), channel_id=1, source_target_pairs={{0,64},{16,80},{32,96},{48,112},{64,0},{80,16},{96,32},{112,48},{1... | collective-permute-start | bytes 393224 | tf_op jit(solution)/shard_map/ppermute | solution.py:404
  108.4 7.6 %collective-permute-start.9 = (bf16[8,64,128]{2,1,0:T(8,128)(2,1)S(1)}, bf16[8,64,128]{2,1,0:T(8,128)(2,1)S(1)}, u32[]{:S(2)}, u32[]{:S(2)}) collective-permute-start(bf16[8,64,128]{2,1,0:T(8,128)(2,1)S(1)} %get-tuple-element.114.refs_0_), channel_id=1, source_target_pairs={{0,96},{16,112},{32,0},{48,16},{64,32},{80,48},{96,64},{112,80},{1... | collective-permute-start | bytes 393224 | tf_op jit(solution)/shard_map/ppermute | solution.py:404
  110.9 5.0 %collective-permute-start.10 = (bf16[8,64,128]{2,1,0:T(8,128)(2,1)S(1)}, bf16[8,64,128]{2,1,0:T(8,128)(2,1)S(1)}, u32[]{:S(2)}, u32[]{:S(2)}) collective-permute-start(bf16[8,64,128]{2,1,0:T(8,128)(2,1)S(1)} %get-tuple-element.114.refs_0_), channel_id=1, source_target_pairs={{0,16},{16,0},{32,48},{48,32},{64,80},{80,64},{96,112},{112,96},{1... | collective-permute-start | bytes 393224 | tf_op jit(solution)/shard_map/ppermute | solution.py:405
  123.2 23.4 %all-to-all-start.3 = ((bf16[16,256,128]{2,1,0:T(8,128)(2,1)}), bf16[16,256,128]{2,1,0:T(8,128)(2,1)S(1)}, u32[]{:S(2)}, u32[]{:S(2)}) async-start(bf16[16,256,128]{2,1,0:T(8,128)(2,1)} %get-tuple-element.117), calls=%async_computation.3 | async-start | bytes 2097152 | tf_op jit(solution)/shard_map/all_to_all | solution.py:414
  129.4 6.4 %collective-permute-start.35 = (bf16[8,64,128]{2,1,0:T(8,128)(2,1)S(1)}, bf16[8,64,128]{2,1,0:T(8,128)(2,1)S(1)}, u32[]{:S(2)}, u32[]{:S(2)}) collective-permute-start(bf16[8,64,128]{2,1,0:T(8,128)(2,1)S(1)} %get-tuple-element.129.refs_0_), channel_id=1, source_target_pairs={{0,32},{16,48},{32,64},{48,80},{64,96},{80,112},{96,0},{112,16},{1... | collective-permute-start | bytes 393224 | tf_op jit(solution)/shard_map/ppermute | solution.py:404
  129.8 7.9 %collective-permute-start.36 = (bf16[8,64,128]{2,1,0:T(8,128)(2,1)S(1)}, bf16[8,64,128]{2,1,0:T(8,128)(2,1)S(1)}, u32[]{:S(2)}, u32[]{:S(2)}) collective-permute-start(bf16[8,64,128]{2,1,0:T(8,128)(2,1)S(1)} %get-tuple-element.129.refs_0_), channel_id=1, source_target_pairs={{0,64},{16,80},{32,96},{48,112},{64,0},{80,16},{96,32},{112,48},{1... | collective-permute-start | bytes 393224 | tf_op jit(solution)/shard_map/ppermute | solution.py:404
  131.5 7.8 %collective-permute-start.37 = (bf16[8,64,128]{2,1,0:T(8,128)(2,1)S(1)}, bf16[8,64,128]{2,1,0:T(8,128)(2,1)S(1)}, u32[]{:S(2)}, u32[]{:S(2)}) collective-permute-start(bf16[8,64,128]{2,1,0:T(8,128)(2,1)S(1)} %get-tuple-element.129.refs_0_), channel_id=1, source_target_pairs={{0,96},{16,112},{32,0},{48,16},{64,32},{80,48},{96,64},{112,80},{1... | collective-permute-start | bytes 393224 | tf_op jit(solution)/shard_map/ppermute | solution.py:404
  134.1 5.3 %collective-permute-start.38 = (bf16[8,64,128]{2,1,0:T(8,128)(2,1)S(1)}, bf16[8,64,128]{2,1,0:T(8,128)(2,1)S(1)}, u32[]{:S(2)}, u32[]{:S(2)}) collective-permute-start(bf16[8,64,128]{2,1,0:T(8,128)(2,1)S(1)} %get-tuple-element.129.refs_0_), channel_id=1, source_target_pairs={{0,16},{16,0},{32,48},{48,32},{64,80},{80,64},{96,112},{112,96},{1... | collective-permute-start | bytes 393224 | tf_op jit(solution)/shard_map/ppermute | solution.py:405
  146.6 23.4 %all-to-all-start.7 = ((bf16[16,256,128]{2,1,0:T(8,128)(2,1)}), bf16[16,256,128]{2,1,0:T(8,128)(2,1)S(1)}, u32[]{:S(2)}, u32[]{:S(2)}) async-start(bf16[16,256,128]{2,1,0:T(8,128)(2,1)} %get-tuple-element.132), calls=%async_computation.7 | async-start | bytes 2097152 | tf_op jit(solution)/shard_map/all_to_all | solution.py:414
  152.8 6.4 %collective-permute-start.14 = (bf16[8,64,128]{2,1,0:T(8,128)(2,1)S(1)}, bf16[8,64,128]{2,1,0:T(8,128)(2,1)S(1)}, u32[]{:S(2)}, u32[]{:S(2)}) collective-permute-start(bf16[8,64,128]{2,1,0:T(8,128)(2,1)S(1)} %get-tuple-element.118.refs_0_), channel_id=1, source_target_pairs={{0,32},{16,48},{32,64},{48,80},{64,96},{80,112},{96,0},{112,16},{1... | collective-permute-start | bytes 393224 | tf_op jit(solution)/shard_map/ppermute | solution.py:404
  153.2 7.9 %collective-permute-start.15 = (bf16[8,64,128]{2,1,0:T(8,128)(2,1)S(1)}, bf16[8,64,128]{2,1,0:T(8,128)(2,1)S(1)}, u32[]{:S(2)}, u32[]{:S(2)}) collective-permute-start(bf16[8,64,128]{2,1,0:T(8,128)(2,1)S(1)} %get-tuple-element.118.refs_0_), channel_id=1, source_target_pairs={{0,64},{16,80},{32,96},{48,112},{64,0},{80,16},{96,32},{112,48},{1... | collective-permute-start | bytes 393224 | tf_op jit(solution)/shard_map/ppermute | solution.py:404
  154.8 7.9 %collective-permute-start.16 = (bf16[8,64,128]{2,1,0:T(8,128)(2,1)S(1)}, bf16[8,64,128]{2,1,0:T(8,128)(2,1)S(1)}, u32[]{:S(2)}, u32[]{:S(2)}) collective-permute-start(bf16[8,64,128]{2,1,0:T(8,128)(2,1)S(1)} %get-tuple-element.118.refs_0_), channel_id=1, source_target_pairs={{0,96},{16,112},{32,0},{48,16},{64,32},{80,48},{96,64},{112,80},{1... | collective-permute-start | bytes 393224 | tf_op jit(solution)/shard_map/ppermute | solution.py:404
  157.3 5.4 %collective-permute-start.17 = (bf16[8,64,128]{2,1,0:T(8,128)(2,1)S(1)}, bf16[8,64,128]{2,1,0:T(8,128)(2,1)S(1)}, u32[]{:S(2)}, u32[]{:S(2)}) collective-permute-start(bf16[8,64,128]{2,1,0:T(8,128)(2,1)S(1)} %get-tuple-element.118.refs_0_), channel_id=1, source_target_pairs={{0,16},{16,0},{32,48},{48,32},{64,80},{80,64},{96,112},{112,96},{1... | collective-permute-start | bytes 393224 | tf_op jit(solution)/shard_map/ppermute | solution.py:405
  169.9 23.4 %all-to-all-start.4 = ((bf16[16,256,128]{2,1,0:T(8,128)(2,1)}), bf16[16,256,128]{2,1,0:T(8,128)(2,1)S(1)}, u32[]{:S(2)}, u32[]{:S(2)}) async-start(bf16[16,256,128]{2,1,0:T(8,128)(2,1)} %get-tuple-element.121), calls=%async_computation.4 | async-start | bytes 2097152 | tf_op jit(solution)/shard_map/all_to_all | solution.py:414
  (30 other events, 164.0 us)

commit v2 on v1

--- a/solution.py
+++ b/solution.py
@@ -334,20 +334,19 @@
     )(ids, got, spread, *before)
 
 
-def rounded(wholes):
-    def body(*refs):
-        for whole_ref, out_ref in zip(refs[: len(wholes)], refs[len(wholes) :]):
-            out_ref[...] = whole_ref[...].astype(BF16)
-
-    return pl.pallas_call(
-        body,
-        out_shape=[jax.ShapeDtypeStruct(whole.shape, BF16) for whole in wholes],
-        in_specs=[VMEM] * len(wholes),
-        out_specs=[VMEM] * len(wholes),
+def rounded(whole):
+    def body(whole_ref, out_ref):
+        out_ref[...] = whole_ref[...].astype(BF16)
+
+    return pl.pallas_call(
+        body,
+        out_shape=jax.ShapeDtypeStruct(whole.shape, BF16),
+        in_specs=[VMEM],
+        out_specs=VMEM,
         compiler_params=PARAMS,
         cost_estimate=COVER,
         name="rounded",
-    )(*wholes)
+    )(whole)
 
 
 def ended_sum(step, ids, got, damping, scores):
@@ -475,10 +474,13 @@
         jnp.broadcast_to(damping[stream * width : (stream + 1) * width][:, None], (width, tile))
         for stream in range(STREAMS)
     ]
-    xparts = [column_parts(mine) for mine in rounded(sums)]
+    xparts = [None] * STREAMS
     owned, scores = sums, [None] * STREAMS
     for step in range(1, TERMS):
         for stream in range(STREAMS):
+            if step == 1:
+                mine = rounded(after(owned[stream], sent) if stream else owned[stream])
+                xparts[stream] = column_parts(mine)
             sent, scores[stream] = products(
                 step,
                 slot,

time: 198 us -> 195 us (0.985)
  starting transfers between devices: 67.9 us -> 65.7 us
  waiting for transfers between devices: 80.2 us -> 82.4 us
  local copies, waits for them, and re-layouts: 5.9 us -> 3.7 us
    unnamed x26, local copies, waits for them, and re-layouts: 5.18 us -> 2.97 us
    all_to_all x7, waiting for transfers between devices: 40 us -> 42.2 us  [exchange(): return lax.all_to_all(sent, 'col', split_axis=0, concat_axis=0, tiled=True)]
    all_to_all x7, starting transfers between devices: 40.4 us -> 38.3 us  [exchange(): return lax.all_to_all(sent, 'col', split_axis=0, concat_axis=0, tiled=True)]
where the time goes in v2:
time: 195 us; the launch traced here: 194 us
  waiting for transfers between devices  82.4 us (42%)
  starting transfers between devices  65.7 us (34%)
  Pallas kernels  36.7 us (19%)
  between operations  3.72 us (2%)
  local copies, waits for them, and re-layouts  3.7 us (2%)
    all_to_all x7, waiting for transfers between devices, exchange(): return lax.all_to_all(sent, 'col', split_axis=0, concat_axis=0, tiled=True)  42.2 us
    all_to_all x7, starting transfers between devices, exchange(): return lax.all_to_all(sent, 'col', split_axis=0, concat_axis=0, tiled=True)  38.3 us
    ppermute x18, waiting for transfers between devices, column_parts(): lax.ppermute(mine, 'row', row_shift(dz, 0))  32.3 us
    ppermute x18, starting transfers between devices, column_parts(): lax.ppermute(mine, 'row', row_shift(dz, 0))  27.3 us
    pallas_call x6, Pallas kernels, products(): pl.pallas_call(body, out_shape=(jax.ShapeDtypeStruct((owners, rows, tile)...  20 us
    ppermute x24, waiting for transfers between devices, column_parts(): other = [lax.ppermute(part, 'row', row_shift(0, 1)) for part in same]  7.89 us
    pallas_call x1, Pallas kernels, first_products(): pl.pallas_call(body, out_shape=jax.ShapeDtypeStruct((n_col, sent_rows + I...  5.72 us
  transfers between devices with their start and end apart: 49, of which 32 were waited for; matrix products, arithmetic and copies ran while one was open for 0% of the time, Pallas kernels for 11%

profile of v2, /device:TPU:32, one launch (start us, length us, event | category | flops | bytes accessed | tf_op | source)
XLA Modules:
  0.0 193.7 jit_solution(10637960903059232238)
XLA Ops:
  0.8 5.7 %first_products.2 = bf16[16,144,128]{2,1,0:T(8,128)(2,1)} custom-call(s32[3]{0:T(128)S(1)} %pad_add_fusion.1.info_ref, s32[128]{0:T(128)} %bitcast.32, s32[128]{0:T(128)} %bitcast.30, s32[128]{0:T(128)} %query_ref.1, bf16[128,128,128]{2,1,0:T(8,128)(2,1)} %bitcast.27), custom_call_target="tpu_custom_call" | custom-call | tf_op jit(solution)/shard_map/first_products/pallas_call | solution.py:175
  10.6 3.2 %turned.1.tiles_ref = bf16[128,128,128]{2,1,0:T(8,128)(2,1)S(1)} custom-call(s32[1]{0:T(128)} %bitcast.18.count_ref, bf16[128,128,128]{2,1,0:T(8,128)(2,1)} %bitcast.28), custom_call_target="tpu_custom_call" | custom-call | tf_op jit(solution)/shard_map/turned/pallas_call | solution.py:259
  15.7 8.0 %all-to-all-start.1 = ((bf16[16,144,128]{2,1,0:T(8,128)(2,1)}), bf16[16,144,128]{2,1,0:T(8,128)(2,1)S(1)}, u32[]{:S(2)}, u32[]{:S(2)}) async-start(bf16[16,144,128]{2,1,0:T(8,128)(2,1)} %first_products.2), calls=%async_computation.1 | async-start | bytes 1179648 | tf_op jit(solution)/shard_map/all_to_all | solution.py:413
  23.9 12.0 %all-to-all-done.1.got_ref = bf16[16,144,128]{2,1,0:T(8,128)(2,1)S(1)} async-done(((bf16[16,144,128]{2,1,0:T(8,128)(2,1)}), bf16[16,144,128]{2,1,0:T(8,128)(2,1)S(1)}, u32[]{:S(2)}, u32[]{:S(2)}) %all-to-all-start.1) | async-done | bytes 589856 | tf_op jit(solution)/shard_map/all_to_all | solution.py:413
  37.3 2.0 %collective-permute-start = (bf16[8,64,128]{2,1,0:T(8,128)(2,1)S(1)}, bf16[8,64,128]{2,1,0:T(8,128)(2,1)S(1)}, u32[]{:S(2)}, u32[]{:S(2)}) collective-permute-start(bf16[8,64,128]{2,1,0:T(8,128)(2,1)S(1)} %rounded.2.refs_0_), channel_id=1, source_target_pairs={{0,32},{16,48},{32,64},{48,80},{64,96},{80,112},{96,0},{112,16},{1... | collective-permute-start | bytes 393224 | tf_op jit(solution)/shard_map/ppermute | solution.py:403
  43.2 2.7 %collective-permute-done.1.refs_2_ = bf16[8,64,128]{2,1,0:T(8,128)(2,1)S(1)} collective-permute-done((bf16[8,64,128]{2,1,0:T(8,128)(2,1)S(1)}, bf16[8,64,128]{2,1,0:T(8,128)(2,1)S(1)}, u32[]{:S(2)}, u32[]{:S(2)}) %collective-permute-start.1) | collective-permute-done | bytes 131104 | tf_op jit(solution)/shard_map/ppermute | solution.py:403
  48.5 3.3 %products.6 = (bf16[16,256,128]{2,1,0:T(8,128)(2,1)}, f32[8,64,128]{2,1,0:T(8,128)}) custom-call(s32[128]{0:T(128)S(1)} %get-tuple-element.163.slot_ref, s32[128]{0:T(128)S(1)} %get-tuple-element.162.place_ref, s32[1]{0:T(128)} %bitcast.19.count_ref, bf16[128,128,128]{2,1,0:T(8,128)(2,1)S(1)} %copy-done.1, bf16[8,64,128]{2,1,0:T(8,128)(2,1)S(1)} %rounded.2.refs_0_, ...), custom_call_target="tpu_custom_call" | custom-call | tf_op jit(solution)/shard_map/products/pallas_call | solution.py:222
  51.8 4.5 %all-to-all-start.5 = ((bf16[16,256,128]{2,1,0:T(8,128)(2,1)}), bf16[16,256,128]{2,1,0:T(8,128)(2,1)S(1)}, u32[]{:S(2)}, u32[]{:S(2)}) async-start(bf16[16,256,128]{2,1,0:T(8,128)(2,1)} %get-tuple-element.111), calls=%async_computation.5 | async-start | bytes 2097152 | tf_op jit(solution)/shard_map/all_to_all | solution.py:413
  58.5 2.5 %collective-permute-start.9 = (bf16[8,64,128]{2,1,0:T(8,128)(2,1)S(1)}, bf16[8,64,128]{2,1,0:T(8,128)(2,1)S(1)}, u32[]{:S(2)}, u32[]{:S(2)}) collective-permute-start(bf16[8,64,128]{2,1,0:T(8,128)(2,1)S(1)} %rounded.3.refs_0_), channel_id=1, source_target_pairs={{0,96},{16,112},{32,0},{48,16},{64,32},{80,48},{96,64},{112,80},{1... | collective-permute-start | bytes 393224 | tf_op jit(solution)/shard_map/ppermute | solution.py:403
  62.0 2.7 %collective-permute-done.8.refs_2_ = bf16[8,64,128]{2,1,0:T(8,128)(2,1)S(1)} collective-permute-done((bf16[8,64,128]{2,1,0:T(8,128)(2,1)S(1)}, bf16[8,64,128]{2,1,0:T(8,128)(2,1)S(1)}, u32[]{:S(2)}, u32[]{:S(2)}) %collective-permute-start.8) | collective-permute-done | bytes 131104 | tf_op jit(solution)/shard_map/ppermute | solution.py:403
  68.0 3.3 %products.7 = (bf16[16,256,128]{2,1,0:T(8,128)(2,1)}, f32[8,64,128]{2,1,0:T(8,128)}) custom-call(s32[128]{0:T(128)S(1)} %get-tuple-element.163.slot_ref, s32[128]{0:T(128)S(1)} %get-tuple-element.162.place_ref, s32[1]{0:T(128)} %bitcast.20.count_ref, bf16[128,128,128]{2,1,0:T(8,128)(2,1)S(1)} %copy-done.2, bf16[8,64,128]{2,1,0:T(8,128)(2,1)S(1)} %rounded.3.refs_0_, ...), custom_call_target="tpu_custom_call" | custom-call | tf_op jit(solution)/shard_map/products/pallas_call | solution.py:222
  71.3 3.2 %all-to-all-done.5.got_ref = bf16[16,256,128]{2,1,0:T(8,128)(2,1)S(1)} async-done(((bf16[16,256,128]{2,1,0:T(8,128)(2,1)}), bf16[16,256,128]{2,1,0:T(8,128)(2,1)S(1)}, u32[]{:S(2)}, u32[]{:S(2)}) %all-to-all-start.5) | async-done | bytes 1048608 | tf_op jit(solution)/shard_map/all_to_all | solution.py:413
  74.5 4.6 %all-to-all-start.2 = ((bf16[16,256,128]{2,1,0:T(8,128)(2,1)}), bf16[16,256,128]{2,1,0:T(8,128)(2,1)S(1)}, u32[]{:S(2)}, u32[]{:S(2)}) async-start(bf16[16,256,128]{2,1,0:T(8,128)(2,1)} %get-tuple-element.113), calls=%async_computation.2 | async-start | bytes 2097152 | tf_op jit(solution)/shard_map/all_to_all | solution.py:413
  82.0 2.5 %collective-permute-start.30 = (bf16[8,64,128]{2,1,0:T(8,128)(2,1)S(1)}, bf16[8,64,128]{2,1,0:T(8,128)(2,1)S(1)}, u32[]{:S(2)}, u32[]{:S(2)}) collective-permute-start(bf16[8,64,128]{2,1,0:T(8,128)(2,1)S(1)} %get-tuple-element.123.refs_0_), channel_id=1, source_target_pairs={{0,96},{16,112},{32,0},{48,16},{64,32},{80,48},{96,64},{112,80},{1... | collective-permute-start | bytes 393224 | tf_op jit(solution)/shard_map/ppermute | solution.py:403
  86.4 2.0 %collective-permute-done.29.refs_2_ = bf16[8,64,128]{2,1,0:T(8,128)(2,1)S(1)} collective-permute-done((bf16[8,64,128]{2,1,0:T(8,128)(2,1)S(1)}, bf16[8,64,128]{2,1,0:T(8,128)(2,1)S(1)}, u32[]{:S(2)}, u32[]{:S(2)}) %collective-permute-start.29) | collective-permute-done | bytes 131104 | tf_op jit(solution)/shard_map/ppermute | solution.py:403
  91.5 3.3 %products.10 = (bf16[16,256,128]{2,1,0:T(8,128)(2,1)}, f32[8,64,128]{2,1,0:T(8,128)}) custom-call(s32[128]{0:T(128)S(1)} %get-tuple-element.163.slot_ref, s32[128]{0:T(128)S(1)} %get-tuple-element.162.place_ref, s32[1]{0:T(128)} %bitcast.23.count_ref, bf16[128,128,128]{2,1,0:T(8,128)(2,1)S(1)} %copy-done.3, ...), custom_call_target="tpu_custom_call" | custom-call | tf_op jit(solution)/shard_map/products/pallas_call | solution.py:222
  94.8 2.3 %all-to-all-done.2.got_ref = bf16[16,256,128]{2,1,0:T(8,128)(2,1)S(1)} async-done(((bf16[16,256,128]{2,1,0:T(8,128)(2,1)}), bf16[16,256,128]{2,1,0:T(8,128)(2,1)S(1)}, u32[]{:S(2)}, u32[]{:S(2)}) %all-to-all-start.2) | async-done | bytes 1048608 | tf_op jit(solution)/shard_map/all_to_all | solution.py:413
  97.1 5.5 %all-to-all-start.6 = ((bf16[16,256,128]{2,1,0:T(8,128)(2,1)}), bf16[16,256,128]{2,1,0:T(8,128)(2,1)S(1)}, u32[]{:S(2)}, u32[]{:S(2)}) async-start(bf16[16,256,128]{2,1,0:T(8,128)(2,1)} %get-tuple-element.126), calls=%async_computation.6 | async-start | bytes 2097152 | tf_op jit(solution)/shard_map/all_to_all | solution.py:413
  103.9 2.0 %collective-permute-start.15 = (bf16[8,64,128]{2,1,0:T(8,128)(2,1)S(1)}, bf16[8,64,128]{2,1,0:T(8,128)(2,1)S(1)}, u32[]{:S(2)}, u32[]{:S(2)}) collective-permute-start(bf16[8,64,128]{2,1,0:T(8,128)(2,1)S(1)} %get-tuple-element.114.refs_0_), channel_id=1, source_target_pairs={{0,64},{16,80},{32,96},{48,112},{64,0},{80,16},{96,32},{112,48},{1... | collective-permute-start | bytes 393224 | tf_op jit(solution)/shard_map/ppermute | solution.py:403
  106.0 2.5 %collective-permute-start.16 = (bf16[8,64,128]{2,1,0:T(8,128)(2,1)S(1)}, bf16[8,64,128]{2,1,0:T(8,128)(2,1)S(1)}, u32[]{:S(2)}, u32[]{:S(2)}) collective-permute-start(bf16[8,64,128]{2,1,0:T(8,128)(2,1)S(1)} %get-tuple-element.114.refs_0_), channel_id=1, source_target_pairs={{0,96},{16,112},{32,0},{48,16},{64,32},{80,48},{96,64},{112,80},{1... | collective-permute-start | bytes 393224 | tf_op jit(solution)/shard_map/ppermute | solution.py:403
  114.9 3.3 %products.8 = (bf16[16,256,128]{2,1,0:T(8,128)(2,1)}, f32[8,64,128]{2,1,0:T(8,128)}) custom-call(s32[128]{0:T(128)S(1)} %get-tuple-element.163.slot_ref, s32[128]{0:T(128)S(1)} %get-tuple-element.162.place_ref, s32[1]{0:T(128)} %bitcast.21.count_ref, bf16[128,128,128]{2,1,0:T(8,128)(2,1)S(1)} %copy-done.4, ...), custom_call_target="tpu_custom_call" | custom-call | tf_op jit(solution)/shard_map/products/pallas_call | solution.py:222
  118.2 2.5 %all-to-all-done.6.got_ref = bf16[16,256,128]{2,1,0:T(8,128)(2,1)S(1)} async-done(((bf16[16,256,128]{2,1,0:T(8,128)(2,1)}), bf16[16,256,128]{2,1,0:T(8,128)(2,1)S(1)}, u32[]{:S(2)}, u32[]{:S(2)}) %all-to-all-start.6) | async-done | bytes 1048608 | tf_op jit(solution)/shard_map/all_to_all | solution.py:413
  120.7 5.3 %all-to-all-start.3 = ((bf16[16,256,128]{2,1,0:T(8,128)(2,1)}), bf16[16,256,128]{2,1,0:T(8,128)(2,1)S(1)}, u32[]{:S(2)}, u32[]{:S(2)}) async-start(bf16[16,256,128]{2,1,0:T(8,128)(2,1)} %get-tuple-element.117), calls=%async_computation.3 | async-start | bytes 2097152 | tf_op jit(solution)/shard_map/all_to_all | solution.py:413
  129.1 2.5 %collective-permute-start.37 = (bf16[8,64,128]{2,1,0:T(8,128)(2,1)S(1)}, bf16[8,64,128]{2,1,0:T(8,128)(2,1)S(1)}, u32[]{:S(2)}, u32[]{:S(2)}) collective-permute-start(bf16[8,64,128]{2,1,0:T(8,128)(2,1)S(1)} %get-tuple-element.127.refs_0_), channel_id=1, source_target_pairs={{0,96},{16,112},{32,0},{48,16},{64,32},{80,48},{96,64},{112,80},{1... | collective-permute-start | bytes 393224 | tf_op jit(solution)/shard_map/ppermute | solution.py:403
  138.2 3.4 %products.11 = (bf16[16,256,128]{2,1,0:T(8,128)(2,1)}, f32[8,64,128]{2,1,0:T(8,128)}) custom-call(s32[128]{0:T(128)S(1)} %get-tuple-element.163.slot_ref, s32[128]{0:T(128)S(1)} %get-tuple-element.162.place_ref, s32[1]{0:T(128)} %bitcast.24.count_ref, bf16[128,128,128]{2,1,0:T(8,128)(2,1)S(1)} %copy-done.5, ...), custom_call_target="tpu_custom_call" | custom-call | tf_op jit(solution)/shard_map/products/pallas_call | solution.py:222
  141.6 2.5 %all-to-all-done.3.got_ref = bf16[16,256,128]{2,1,0:T(8,128)(2,1)S(1)} async-done(((bf16[16,256,128]{2,1,0:T(8,128)(2,1)}), bf16[16,256,128]{2,1,0:T(8,128)(2,1)S(1)}, u32[]{:S(2)}, u32[]{:S(2)}) %all-to-all-start.3) | async-done | bytes 1048608 | tf_op jit(solution)/shard_map/all_to_all | solution.py:413
  144.1 5.2 %all-to-all-start.7 = ((bf16[16,256,128]{2,1,0:T(8,128)(2,1)}), bf16[16,256,128]{2,1,0:T(8,128)(2,1)S(1)}, u32[]{:S(2)}, u32[]{:S(2)}) async-start(bf16[16,256,128]{2,1,0:T(8,128)(2,1)} %get-tuple-element.130), calls=%async_computation.7 | async-start | bytes 2097152 | tf_op jit(solution)/shard_map/all_to_all | solution.py:413
  152.3 2.5 %collective-permute-start.23 = (bf16[8,64,128]{2,1,0:T(8,128)(2,1)S(1)}, bf16[8,64,128]{2,1,0:T(8,128)(2,1)S(1)}, u32[]{:S(2)}, u32[]{:S(2)}) collective-permute-start(bf16[8,64,128]{2,1,0:T(8,128)(2,1)S(1)} %get-tuple-element.118.refs_0_), channel_id=1, source_target_pairs={{0,96},{16,112},{32,0},{48,16},{64,32},{80,48},{96,64},{112,80},{1... | collective-permute-start | bytes 393224 | tf_op jit(solution)/shard_map/ppermute | solution.py:403
  161.6 3.4 %products.9 = (bf16[16,256,128]{2,1,0:T(8,128)(2,1)}, f32[8,64,128]{2,1,0:T(8,128)}) custom-call(s32[128]{0:T(128)S(1)} %get-tuple-element.163.slot_ref, s32[128]{0:T(128)S(1)} %get-tuple-element.162.place_ref, s32[1]{0:T(128)} %bitcast.22.count_ref, bf16[128,128,128]{2,1,0:T(8,128)(2,1)S(1)} %copy-done.6, ...), custom_call_target="tpu_custom_call" | custom-call | tf_op jit(solution)/shard_map/products/pallas_call | solution.py:222
  165.0 2.5 %all-to-all-done.7.got_ref = bf16[16,256,128]{2,1,0:T(8,128)(2,1)S(1)} async-done(((bf16[16,256,128]{2,1,0:T(8,128)(2,1)}), bf16[16,256,128]{2,1,0:T(8,128)(2,1)S(1)}, u32[]{:S(2)}, u32[]{:S(2)}) %all-to-all-start.7) | async-done | bytes 1048608 | tf_op jit(solution)/shard_map/all_to_all | solution.py:413
  167.5 5.2 %all-to-all-start.4 = ((bf16[16,256,128]{2,1,0:T(8,128)(2,1)}), bf16[16,256,128]{2,1,0:T(8,128)(2,1)S(1)}, u32[]{:S(2)}, u32[]{:S(2)}) async-start(bf16[16,256,128]{2,1,0:T(8,128)(2,1)} %get-tuple-element.121), calls=%async_computation.4 | async-start | bytes 2097152 | tf_op jit(solution)/shard_map/all_to_all | solution.py:413
  173.7 17.2 %all-to-all-done.4.got_ref = bf16[16,256,128]{2,1,0:T(8,128)(2,1)S(1)} async-done(((bf16[16,256,128]{2,1,0:T(8,128)(2,1)}), bf16[16,256,128]{2,1,0:T(8,128)(2,1)S(1)}, u32[]{:S(2)}, u32[]{:S(2)}) %all-to-all-start.4) | async-done | bytes 1048608 | tf_op jit(solution)/shard_map/all_to_all | solution.py:413
  (134 shorter events, 56.5 us)
Async XLA Ops:
  15.7 20.2 %all-to-all-start.1 = ((bf16[16,144,128]{2,1,0:T(8,128)(2,1)}), bf16[16,144,128]{2,1,0:T(8,128)(2,1)S(1)}, u32[]{:S(2)}, u32[]{:S(2)}) async-start(bf16[16,144,128]{2,1,0:T(8,128)(2,1)} %first_products.2), calls=%async_computation.1 | async-start | bytes 1179648 | tf_op jit(solution)/shard_map/all_to_all | solution.py:413
  37.3 5.8 %collective-permute-start = (bf16[8,64,128]{2,1,0:T(8,128)(2,1)S(1)}, bf16[8,64,128]{2,1,0:T(8,128)(2,1)S(1)}, u32[]{:S(2)}, u32[]{:S(2)}) collective-permute-start(bf16[8,64,128]{2,1,0:T(8,128)(2,1)S(1)} %rounded.2.refs_0_), channel_id=1, source_target_pairs={{0,32},{16,48},{32,64},{48,80},{64,96},{80,112},{96,0},{112,16},{1... | collective-permute-start | bytes 393224 | tf_op jit(solution)/shard_map/ppermute | solution.py:403
  39.3 6.6 %collective-permute-start.1 = (bf16[8,64,128]{2,1,0:T(8,128)(2,1)S(1)}, bf16[8,64,128]{2,1,0:T(8,128)(2,1)S(1)}, u32[]{:S(2)}, u32[]{:S(2)}) collective-permute-start(bf16[8,64,128]{2,1,0:T(8,128)(2,1)S(1)} %rounded.2.refs_0_), channel_id=1, source_target_pairs={{0,64},{16,80},{32,96},{48,112},{64,0},{80,16},{96,32},{112,48},{1... | collective-permute-start | bytes 393224 | tf_op jit(solution)/shard_map/ppermute | solution.py:403
  39.6 7.4 %collective-permute-start.2 = (bf16[8,64,128]{2,1,0:T(8,128)(2,1)S(1)}, bf16[8,64,128]{2,1,0:T(8,128)(2,1)S(1)}, u32[]{:S(2)}, u32[]{:S(2)}) collective-permute-start(bf16[8,64,128]{2,1,0:T(8,128)(2,1)S(1)} %rounded.2.refs_0_), channel_id=1, source_target_pairs={{0,96},{16,112},{32,0},{48,16},{64,32},{80,48},{96,64},{112,80},{1... | collective-permute-start | bytes 393224 | tf_op jit(solution)/shard_map/ppermute | solution.py:403
  41.5 5.7 %collective-permute-start.3 = (bf16[8,64,128]{2,1,0:T(8,128)(2,1)S(1)}, bf16[8,64,128]{2,1,0:T(8,128)(2,1)S(1)}, u32[]{:S(2)}, u32[]{:S(2)}) collective-permute-start(bf16[8,64,128]{2,1,0:T(8,128)(2,1)S(1)} %rounded.2.refs_0_), channel_id=1, source_target_pairs={{0,16},{16,0},{32,48},{48,32},{64,80},{80,64},{96,112},{112,96},{1... | collective-permute-start | bytes 393224 | tf_op jit(solution)/shard_map/ppermute | solution.py:404
  51.8 22.6 %all-to-all-start.5 = ((bf16[16,256,128]{2,1,0:T(8,128)(2,1)}), bf16[16,256,128]{2,1,0:T(8,128)(2,1)S(1)}, u32[]{:S(2)}, u32[]{:S(2)}) async-start(bf16[16,256,128]{2,1,0:T(8,128)(2,1)} %get-tuple-element.111), calls=%async_computation.5 | async-start | bytes 2097152 | tf_op jit(solution)/shard_map/all_to_all | solution.py:413
  56.4 5.6 %collective-permute-start.7 = (bf16[8,64,128]{2,1,0:T(8,128)(2,1)S(1)}, bf16[8,64,128]{2,1,0:T(8,128)(2,1)S(1)}, u32[]{:S(2)}, u32[]{:S(2)}) collective-permute-start(bf16[8,64,128]{2,1,0:T(8,128)(2,1)S(1)} %rounded.3.refs_0_), channel_id=1, source_target_pairs={{0,32},{16,48},{32,64},{48,80},{64,96},{80,112},{96,0},{112,16},{1... | collective-permute-start | bytes 393224 | tf_op jit(solution)/shard_map/ppermute | solution.py:403
  56.8 7.9 %collective-permute-start.8 = (bf16[8,64,128]{2,1,0:T(8,128)(2,1)S(1)}, bf16[8,64,128]{2,1,0:T(8,128)(2,1)S(1)}, u32[]{:S(2)}, u32[]{:S(2)}) collective-permute-start(bf16[8,64,128]{2,1,0:T(8,128)(2,1)S(1)} %rounded.3.refs_0_), channel_id=1, source_target_pairs={{0,64},{16,80},{32,96},{48,112},{64,0},{80,16},{96,32},{112,48},{1... | collective-permute-start | bytes 393224 | tf_op jit(solution)/shard_map/ppermute | solution.py:403
  58.5 8.1 %collective-permute-start.9 = (bf16[8,64,128]{2,1,0:T(8,128)(2,1)S(1)}, bf16[8,64,128]{2,1,0:T(8,128)(2,1)S(1)}, u32[]{:S(2)}, u32[]{:S(2)}) collective-permute-start(bf16[8,64,128]{2,1,0:T(8,128)(2,1)S(1)} %rounded.3.refs_0_), channel_id=1, source_target_pairs={{0,96},{16,112},{32,0},{48,16},{64,32},{80,48},{96,64},{112,80},{1... | collective-permute-start | bytes 393224 | tf_op jit(solution)/shard_map/ppermute | solution.py:403
  61.0 5.5 %collective-permute-start.10 = (bf16[8,64,128]{2,1,0:T(8,128)(2,1)S(1)}, bf16[8,64,128]{2,1,0:T(8,128)(2,1)S(1)}, u32[]{:S(2)}, u32[]{:S(2)}) collective-permute-start(bf16[8,64,128]{2,1,0:T(8,128)(2,1)S(1)} %rounded.3.refs_0_), channel_id=1, source_target_pairs={{0,16},{16,0},{32,48},{48,32},{64,80},{80,64},{96,112},{112,96},{1... | collective-permute-start | bytes 393224 | tf_op jit(solution)/shard_map/ppermute | solution.py:404
  62.0 4.6 %collective-permute-start.11 = (bf16[8,64,128]{2,1,0:T(8,128)(2,1)S(1)}, bf16[8,64,128]{2,1,0:T(8,128)(2,1)S(1)}, u32[]{:S(2)}, u32[]{:S(2)}) collective-permute-start(bf16[8,64,128]{2,1,0:T(8,128)(2,1)S(1)} %collective-permute-done.7.refs_1_), channel_id=1, source_target_pairs={{0,16},{16,0},{32,48},{48,32},{64,80},{80,64},{96,112},{112,96},{1... | collective-permute-start | bytes 393224 | tf_op jit(solution)/shard_map/ppermute | solution.py:404
  74.5 22.7 %all-to-all-start.2 = ((bf16[16,256,128]{2,1,0:T(8,128)(2,1)}), bf16[16,256,128]{2,1,0:T(8,128)(2,1)S(1)}, u32[]{:S(2)}, u32[]{:S(2)}) async-start(bf16[16,256,128]{2,1,0:T(8,128)(2,1)} %get-tuple-element.113), calls=%async_computation.2 | async-start | bytes 2097152 | tf_op jit(solution)/shard_map/all_to_all | solution.py:413
  80.0 6.4 %collective-permute-start.28 = (bf16[8,64,128]{2,1,0:T(8,128)(2,1)S(1)}, bf16[8,64,128]{2,1,0:T(8,128)(2,1)S(1)}, u32[]{:S(2)}, u32[]{:S(2)}) collective-permute-start(bf16[8,64,128]{2,1,0:T(8,128)(2,1)S(1)} %get-tuple-element.123.refs_0_), channel_id=1, source_target_pairs={{0,32},{16,48},{32,64},{48,80},{64,96},{80,112},{96,0},{112,16},{1... | collective-permute-start | bytes 393224 | tf_op jit(solution)/shard_map/ppermute | solution.py:403
  80.5 7.9 %collective-permute-start.29 = (bf16[8,64,128]{2,1,0:T(8,128)(2,1)S(1)}, bf16[8,64,128]{2,1,0:T(8,128)(2,1)S(1)}, u32[]{:S(2)}, u32[]{:S(2)}) collective-permute-start(bf16[8,64,128]{2,1,0:T(8,128)(2,1)S(1)} %get-tuple-element.123.refs_0_), channel_id=1, source_target_pairs={{0,64},{16,80},{32,96},{48,112},{64,0},{80,16},{96,32},{112,48},{1... | collective-permute-start | bytes 393224 | tf_op jit(solution)/shard_map/ppermute | solution.py:403
  82.0 8.1 %collective-permute-start.30 = (bf16[8,64,128]{2,1,0:T(8,128)(2,1)S(1)}, bf16[8,64,128]{2,1,0:T(8,128)(2,1)S(1)}, u32[]{:S(2)}, u32[]{:S(2)}) collective-permute-start(bf16[8,64,128]{2,1,0:T(8,128)(2,1)S(1)} %get-tuple-element.123.refs_0_), channel_id=1, source_target_pairs={{0,96},{16,112},{32,0},{48,16},{64,32},{80,48},{96,64},{112,80},{1... | collective-permute-start | bytes 393224 | tf_op jit(solution)/shard_map/ppermute | solution.py:403
  84.5 5.7 %collective-permute-start.31 = (bf16[8,64,128]{2,1,0:T(8,128)(2,1)S(1)}, bf16[8,64,128]{2,1,0:T(8,128)(2,1)S(1)}, u32[]{:S(2)}, u32[]{:S(2)}) collective-permute-start(bf16[8,64,128]{2,1,0:T(8,128)(2,1)S(1)} %get-tuple-element.123.refs_0_), channel_id=1, source_target_pairs={{0,16},{16,0},{32,48},{48,32},{64,80},{80,64},{96,112},{112,96},{1... | collective-permute-start | bytes 393224 | tf_op jit(solution)/shard_map/ppermute | solution.py:404
  97.1 23.6 %all-to-all-start.6 = ((bf16[16,256,128]{2,1,0:T(8,128)(2,1)}), bf16[16,256,128]{2,1,0:T(8,128)(2,1)S(1)}, u32[]{:S(2)}, u32[]{:S(2)}) async-start(bf16[16,256,128]{2,1,0:T(8,128)(2,1)} %get-tuple-element.126), calls=%async_computation.6 | async-start | bytes 2097152 | tf_op jit(solution)/shard_map/all_to_all | solution.py:413
  103.6 6.4 %collective-permute-start.14 = (bf16[8,64,128]{2,1,0:T(8,128)(2,1)S(1)}, bf16[8,64,128]{2,1,0:T(8,128)(2,1)S(1)}, u32[]{:S(2)}, u32[]{:S(2)}) collective-permute-start(bf16[8,64,128]{2,1,0:T(8,128)(2,1)S(1)} %get-tuple-element.114.refs_0_), channel_id=1, source_target_pairs={{0,32},{16,48},{32,64},{48,80},{64,96},{80,112},{96,0},{112,16},{1... | collective-permute-start | bytes 393224 | tf_op jit(solution)/shard_map/ppermute | solution.py:403
  103.9 7.9 %collective-permute-start.15 = (bf16[8,64,128]{2,1,0:T(8,128)(2,1)S(1)}, bf16[8,64,128]{2,1,0:T(8,128)(2,1)S(1)}, u32[]{:S(2)}, u32[]{:S(2)}) collective-permute-start(bf16[8,64,128]{2,1,0:T(8,128)(2,1)S(1)} %get-tuple-element.114.refs_0_), channel_id=1, source_target_pairs={{0,64},{16,80},{32,96},{48,112},{64,0},{80,16},{96,32},{112,48},{1... | collective-permute-start | bytes 393224 | tf_op jit(solution)/shard_map/ppermute | solution.py:403
  106.0 7.6 %collective-permute-start.16 = (bf16[8,64,128]{2,1,0:T(8,128)(2,1)S(1)}, bf16[8,64,128]{2,1,0:T(8,128)(2,1)S(1)}, u32[]{:S(2)}, u32[]{:S(2)}) collective-permute-start(bf16[8,64,128]{2,1,0:T(8,128)(2,1)S(1)} %get-tuple-element.114.refs_0_), channel_id=1, source_target_pairs={{0,96},{16,112},{32,0},{48,16},{64,32},{80,48},{96,64},{112,80},{1... | collective-permute-start | bytes 393224 | tf_op jit(solution)/shard_map/ppermute | solution.py:403
  108.5 5.0 %collective-permute-start.17 = (bf16[8,64,128]{2,1,0:T(8,128)(2,1)S(1)}, bf16[8,64,128]{2,1,0:T(8,128)(2,1)S(1)}, u32[]{:S(2)}, u32[]{:S(2)}) collective-permute-start(bf16[8,64,128]{2,1,0:T(8,128)(2,1)S(1)} %get-tuple-element.114.refs_0_), channel_id=1, source_target_pairs={{0,16},{16,0},{32,48},{48,32},{64,80},{80,64},{96,112},{112,96},{1... | collective-permute-start | bytes 393224 | tf_op jit(solution)/shard_map/ppermute | solution.py:404
  120.7 23.4 %all-to-all-start.3 = ((bf16[16,256,128]{2,1,0:T(8,128)(2,1)}), bf16[16,256,128]{2,1,0:T(8,128)(2,1)S(1)}, u32[]{:S(2)}, u32[]{:S(2)}) async-start(bf16[16,256,128]{2,1,0:T(8,128)(2,1)} %get-tuple-element.117), calls=%async_computation.3 | async-start | bytes 2097152 | tf_op jit(solution)/shard_map/all_to_all | solution.py:413
  127.0 6.4 %collective-permute-start.35 = (bf16[8,64,128]{2,1,0:T(8,128)(2,1)S(1)}, bf16[8,64,128]{2,1,0:T(8,128)(2,1)S(1)}, u32[]{:S(2)}, u32[]{:S(2)}) collective-permute-start(bf16[8,64,128]{2,1,0:T(8,128)(2,1)S(1)} %get-tuple-element.127.refs_0_), channel_id=1, source_target_pairs={{0,32},{16,48},{32,64},{48,80},{64,96},{80,112},{96,0},{112,16},{1... | collective-permute-start | bytes 393224 | tf_op jit(solution)/shard_map/ppermute | solution.py:403
  127.3 7.9 %collective-permute-start.36 = (bf16[8,64,128]{2,1,0:T(8,128)(2,1)S(1)}, bf16[8,64,128]{2,1,0:T(8,128)(2,1)S(1)}, u32[]{:S(2)}, u32[]{:S(2)}) collective-permute-start(bf16[8,64,128]{2,1,0:T(8,128)(2,1)S(1)} %get-tuple-element.127.refs_0_), channel_id=1, source_target_pairs={{0,64},{16,80},{32,96},{48,112},{64,0},{80,16},{96,32},{112,48},{1... | collective-permute-start | bytes 393224 | tf_op jit(solution)/shard_map/ppermute | solution.py:403
  129.1 7.8 %collective-permute-start.37 = (bf16[8,64,128]{2,1,0:T(8,128)(2,1)S(1)}, bf16[8,64,128]{2,1,0:T(8,128)(2,1)S(1)}, u32[]{:S(2)}, u32[]{:S(2)}) collective-permute-start(bf16[8,64,128]{2,1,0:T(8,128)(2,1)S(1)} %get-tuple-element.127.refs_0_), channel_id=1, source_target_pairs={{0,96},{16,112},{32,0},{48,16},{64,32},{80,48},{96,64},{112,80},{1... | collective-permute-start | bytes 393224 | tf_op jit(solution)/shard_map/ppermute | solution.py:403
  131.6 5.2 %collective-permute-start.38 = (bf16[8,64,128]{2,1,0:T(8,128)(2,1)S(1)}, bf16[8,64,128]{2,1,0:T(8,128)(2,1)S(1)}, u32[]{:S(2)}, u32[]{:S(2)}) collective-permute-start(bf16[8,64,128]{2,1,0:T(8,128)(2,1)S(1)} %get-tuple-element.127.refs_0_), channel_id=1, source_target_pairs={{0,16},{16,0},{32,48},{48,32},{64,80},{80,64},{96,112},{112,96},{1... | collective-permute-start | bytes 393224 | tf_op jit(solution)/shard_map/ppermute | solution.py:404
  144.1 23.4 %all-to-all-start.7 = ((bf16[16,256,128]{2,1,0:T(8,128)(2,1)}), bf16[16,256,128]{2,1,0:T(8,128)(2,1)S(1)}, u32[]{:S(2)}, u32[]{:S(2)}) async-start(bf16[16,256,128]{2,1,0:T(8,128)(2,1)} %get-tuple-element.130), calls=%async_computation.7 | async-start | bytes 2097152 | tf_op jit(solution)/shard_map/all_to_all | solution.py:413
  150.4 6.4 %collective-permute-start.21 = (bf16[8,64,128]{2,1,0:T(8,128)(2,1)S(1)}, bf16[8,64,128]{2,1,0:T(8,128)(2,1)S(1)}, u32[]{:S(2)}, u32[]{:S(2)}) collective-permute-start(bf16[8,64,128]{2,1,0:T(8,128)(2,1)S(1)} %get-tuple-element.118.refs_0_), channel_id=1, source_target_pairs={{0,32},{16,48},{32,64},{48,80},{64,96},{80,112},{96,0},{112,16},{1... | collective-permute-start | bytes 393224 | tf_op jit(solution)/shard_map/ppermute | solution.py:403
  150.8 7.9 %collective-permute-start.22 = (bf16[8,64,128]{2,1,0:T(8,128)(2,1)S(1)}, bf16[8,64,128]{2,1,0:T(8,128)(2,1)S(1)}, u32[]{:S(2)}, u32[]{:S(2)}) collective-permute-start(bf16[8,64,128]{2,1,0:T(8,128)(2,1)S(1)} %get-tuple-element.118.refs_0_), channel_id=1, source_target_pairs={{0,64},{16,80},{32,96},{48,112},{64,0},{80,16},{96,32},{112,48},{1... | collective-permute-start | bytes 393224 | tf_op jit(solution)/shard_map/ppermute | solution.py:403
  152.3 7.9 %collective-permute-start.23 = (bf16[8,64,128]{2,1,0:T(8,128)(2,1)S(1)}, bf16[8,64,128]{2,1,0:T(8,128)(2,1)S(1)}, u32[]{:S(2)}, u32[]{:S(2)}) collective-permute-start(bf16[8,64,128]{2,1,0:T(8,128)(2,1)S(1)} %get-tuple-element.118.refs_0_), channel_id=1, source_target_pairs={{0,96},{16,112},{32,0},{48,16},{64,32},{80,48},{96,64},{112,80},{1... | collective-permute-start | bytes 393224 | tf_op jit(solution)/shard_map/ppermute | solution.py:403
  154.9 5.4 %collective-permute-start.24 = (bf16[8,64,128]{2,1,0:T(8,128)(2,1)S(1)}, bf16[8,64,128]{2,1,0:T(8,128)(2,1)S(1)}, u32[]{:S(2)}, u32[]{:S(2)}) collective-permute-start(bf16[8,64,128]{2,1,0:T(8,128)(2,1)S(1)} %get-tuple-element.118.refs_0_), channel_id=1, source_target_pairs={{0,16},{16,0},{32,48},{48,32},{64,80},{80,64},{96,112},{112,96},{1... | collective-permute-start | bytes 393224 | tf_op jit(solution)/shard_map/ppermute | solution.py:404
  167.5 23.4 %all-to-all-start.4 = ((bf16[16,256,128]{2,1,0:T(8,128)(2,1)}), bf16[16,256,128]{2,1,0:T(8,128)(2,1)S(1)}, u32[]{:S(2)}, u32[]{:S(2)}) async-start(bf16[16,256,128]{2,1,0:T(8,128)(2,1)} %get-tuple-element.121), calls=%async_computation.4 | async-start | bytes 2097152 | tf_op jit(solution)/shard_map/all_to_all | solution.py:413
  (30 other events, 173.1 us)

commit v3 on v2

--- a/solution.py
+++ b/solution.py
@@ -11,11 +11,12 @@
 TOUCH = 4
 N_Z = 4
 N_CORE = 2
+N_X = 4
 STREAMS = 2
-PLACES = 32
+PLACES = 24
 ID_ROWS = 16
 UNROLL = 8
-FIRST_UNROLL = 4
+FIRST_UNROLL = 8
 CHUNK = 32
 VMEM_LIMIT = 14 * 1024 * 1024
 
@@ -129,19 +130,19 @@
         clear(id_ref, BPD)
         id_rows_ref[...] = jnp.full(id_rows_ref.shape, float(BPD), F32)
 
-        def number_owner(owner, carry):
+        def number_owner(owner, sent_to):
             rank = 0
             for block in range(BPD):
                 marked = mark_ref[owner * BPD + block]
-                slot_ref[owner * BPD + block] = owner * TOUCH + rank
-                id_ref[owner * TOUCH + rank] = jnp.where(marked > 0, block, BPD)
+                slot_ref[owner * BPD + block] = sent_to * TOUCH + rank
+                id_ref[sent_to * TOUCH + rank] = jnp.where(marked > 0, block, BPD)
                 rank = rank + marked
             for place in range(TOUCH):
-                number = id_ref[owner * TOUCH + place].astype(F32)
-                id_rows_ref[owner, place : place + 1] = jnp.full((1, tile), number, F32)
-            return carry
-
-        repeat(n_col, number_owner, unroll=1)
+                number = id_ref[sent_to * TOUCH + place].astype(F32)
+                id_rows_ref[sent_to, place : place + 1] = jnp.full((1, tile), number, F32)
+
+        for sent_to, owner in enumerate(exchange_order(n_col)):
+            number_owner(owner, sent_to)
         acc_ref[...] = jnp.zeros(acc_ref.shape, F32)
 
         def step(index, carry):
@@ -168,7 +169,7 @@
             return carry
 
         lax.fori_loop(0, (found + FIRST_UNROLL - 1) // FIRST_UNROLL, step, 0)
-        out_ref[:, :sent_rows] = acc_ref[:spare].astype(BF16).reshape(n_col, sent_rows, tile)
+        out_ref[:, :sent_rows] = acc_ref[:spare].reshape(n_col, sent_rows, tile).astype(BF16)
         out_ref[:, sent_rows:] = id_rows_ref[...].astype(BF16)
 
     info = jnp.stack([count, col, round_index]).astype(jnp.int32)
@@ -307,15 +308,16 @@
 
     def body(id_ref, got_ref, spread_ref, *refs):
         whole_refs, out_refs, piece_ref = refs[: len(before)], refs[len(before) : -1], refs[-1]
-        piece_ref[...] = jnp.zeros(piece_ref.shape, BF16)
+        piece_ref[...] = jnp.zeros(piece_ref.shape, F32)
         for source in range(sources):
+            part = got_ref[source].astype(F32)
             for place in range(TOUCH):
                 block = id_ref[source * TOUCH + place]
-                piece_ref[block, source * PLACES : (source + 1) * PLACES] = got_ref[
-                    source, place * PLACES : (place + 1) * PLACES
+                piece_ref[block, source * PLACES : (source + 1) * PLACES] = part[
+                    place * PLACES : (place + 1) * PLACES
                 ]
         for block in range(BPD):
-            owned = jnp.dot(spread_ref[...], piece_ref[block], preferred_element_type=F32)
+            owned = jnp.dot(spread_ref[...], piece_ref[block].astype(BF16), preferred_element_type=F32)
             for stream in range(streams):
                 mine = owned[stream * width : (stream + 1) * width]
                 if whole_refs:
@@ -328,7 +330,7 @@
         out_shape=[jax.ShapeDtypeStruct(shape, F32)] * streams,
         in_specs=[SMEM] + [VMEM] * (2 + len(before)),
         out_specs=[VMEM] * streams,
-        scratch_shapes=[pltpu.VMEM((BPD + 1, columns, tile), BF16)],
+        scratch_shapes=[pltpu.VMEM((BPD + 1, columns, tile), F32)],
         compiler_params=PARAMS,
         name="placed",
     )(ids, got, spread, *before)
@@ -409,8 +411,21 @@
     return lax.optimization_barrier((value, *others))[0]
 
 
+def exchange_order(n_col):
+    n_y = n_col // N_X
+    return [x * n_y + (y if x % 2 == 0 else n_y - 1 - y) for x in range(N_X) for y in range(n_y)]
+
+
+def position_of(device, n_col):
+    n_y = n_col // N_X
+    x, y = device // n_y, device % n_y
+    return x * n_y + jnp.where(x % 2 == 0, y, n_y - 1 - y)
+
+
 def exchange(sent):
-    return lax.all_to_all(sent, "col", split_axis=0, concat_axis=0, tiled=True)
+    return lax.all_to_all(
+        sent, "col", split_axis=0, concat_axis=0, tiled=True, axis_index_groups=[exchange_order(sent.shape[0])]
+    )
 
 
 def routes(rows, cols, count, n_col):
@@ -421,7 +436,7 @@
     marked = jnp.any(hits, axis=1).astype(jnp.int32).reshape(n_col, BPD)
     local = jnp.arange(BPD, dtype=jnp.int32)
     rank = jnp.sum(marked[:, None, :] * (local[None, None, :] < local[None, :, None]), axis=2)
-    slot_of = (jnp.arange(n_col, dtype=jnp.int32)[:, None] * TOUCH + rank).reshape(-1)
+    slot_of = (position_of(jnp.arange(n_col, dtype=jnp.int32), n_col)[:, None] * TOUCH + rank).reshape(-1)
     slot = jnp.sum(jnp.where(hits, slot_of[:, None], 0), axis=0)
     slot = jnp.where(live, slot, n_col * TOUCH)
     row = lax.axis_index("row")
@@ -454,7 +469,7 @@
 
     def spread(round_index):
         place = rank - round_index * PLACES
-        column = jnp.where((place >= 0) & (place < PLACES), home * PLACES + place, -1)
+        column = jnp.where((place >= 0) & (place < PLACES), position_of(home, n_col) * PLACES + place, -1)
         return (column[:, None] == jnp.arange(n_col * PLACES, dtype=jnp.int32)[None, :]).astype(BF16)
 
     slot, place = routes(after(rows, sent), cols, count, n_col)

time: 195 us -> 190 us (0.974)
  waiting for transfers between devices: 82.4 us -> 68.7 us
  starting transfers between devices: 65.7 us -> 75.8 us
    all_to_all x7, waiting for transfers between devices: 42.2 us -> 28.9 us  [exchange(): lax.all_to_all(sent, 'col', split_axis=0, concat_axis=0, tiled=True, axis...]
    all_to_all x7, starting transfers between devices: 38.3 us -> 48 us  [exchange(): lax.all_to_all(sent, 'col', split_axis=0, concat_axis=0, tiled=True, axis...]
  transfers between devices with their start and end apart: 49 -> 49, of which waited for: 32 -> 33; matrix products, arithmetic and copies ran while one was open for 0% -> 0% of each run, Pallas kernels for 11% -> 11%
where the time goes in v3:
time: 190 us; the launch traced here: 189 us
  starting transfers between devices  75.8 us (40%)
  waiting for transfers between devices  68.7 us (36%)
  Pallas kernels  36.1 us (19%)
  local copies, waits for them, and re-layouts  3.72 us (2%)
  between operations  2.88 us (2%)
    all_to_all x7, starting transfers between devices, exchange(): lax.all_to_all(sent, 'col', split_axis=0, concat_axis=0, tiled=True, axis...  48 us
    ppermute x18, waiting for transfers between devices, column_parts(): lax.ppermute(mine, 'row', row_shift(dz, 0))  32 us
    all_to_all x7, waiting for transfers between devices, exchange(): lax.all_to_all(sent, 'col', split_axis=0, concat_axis=0, tiled=True, axis...  28.9 us
    ppermute x18, starting transfers between devices, column_parts(): lax.ppermute(mine, 'row', row_shift(dz, 0))  27.7 us
    pallas_call x6, Pallas kernels, products(): pl.pallas_call(body, out_shape=(jax.ShapeDtypeStruct((owners, rows, tile)...  20 us
    ppermute x24, waiting for transfers between devices, column_parts(): other = [lax.ppermute(part, 'row', row_shift(0, 1)) for part in same]  7.89 us
    pallas_call x1, Pallas kernels, first_products(): pl.pallas_call(body, out_shape=jax.ShapeDtypeStruct((n_col, sent_rows + I...  5.17 us
    pallas_call x4, Pallas kernels, owned_sum(): pl.pallas_call(body, out_shape=(jax.ShapeDtypeStruct((BPD, width, tile),...  3.87 us
  transfers between devices with their start and end apart: 49, of which 33 were waited for; matrix products, arithmetic and copies ran while one was open for 0% of the time, Pallas kernels for 11%

profile of v3, /device:TPU:32, one launch (start us, length us, event | category | flops | bytes accessed | tf_op | source)
XLA Modules:
  0.0 188.6 jit_solution(13566176627478943697)
XLA Ops:
  0.8 5.2 %first_products.7 = bf16[16,112,128]{2,1,0:T(8,128)(2,1)} custom-call(s32[3]{0:T(128)S(1)} %pad_add_fusion.1.info_ref, s32[128]{0:T(128)} %bitcast.52, s32[128]{0:T(128)} %bitcast.50, s32[128]{0:T(128)} %query_ref.1, bf16[128,128,128]{2,1,0:T(8,128)(2,1)} %bitcast.47), custom_call_target="tpu_custom_call" | custom-call | tf_op jit(solution)/shard_map/first_products/pallas_call | solution.py:176
  9.3 3.2 %turned.1.tiles_ref = bf16[128,128,128]{2,1,0:T(8,128)(2,1)S(1)} custom-call(s32[1]{0:T(128)} %bitcast.38.count_ref, bf16[128,128,128]{2,1,0:T(8,128)(2,1)} %bitcast.48), custom_call_target="tpu_custom_call" | custom-call | tf_op jit(solution)/shard_map/turned/pallas_call | solution.py:260
  12.5 2.0 %copy-done = bf16[128,128,128]{2,1,0:T(8,128)(2,1)} copy-done((bf16[128,128,128]{2,1,0:T(8,128)(2,1)}, bf16[128,128,128]{2,1,0:T(8,128)(2,1)S(1)}, u32[]{:S(2)}) %copy-start) | copy-done | bytes 4194328
  14.4 8.0 %all-to-all-start.1 = ((bf16[16,112,128]{2,1,0:T(8,128)(2,1)}), bf16[16,112,128]{2,1,0:T(8,128)(2,1)S(1)}, u32[]{:S(2)}, u32[]{:S(2)}) async-start(bf16[16,112,128]{2,1,0:T(8,128)(2,1)} %first_products.7), calls=%async_computation.1 | async-start | bytes 917504 | tf_op jit(solution)/shard_map/all_to_all | solution.py:426
  22.6 10.1 %all-to-all-done.1.got_ref = bf16[16,112,128]{2,1,0:T(8,128)(2,1)S(1)} async-done(((bf16[16,112,128]{2,1,0:T(8,128)(2,1)}), bf16[16,112,128]{2,1,0:T(8,128)(2,1)S(1)}, u32[]{:S(2)}, u32[]{:S(2)}) %all-to-all-start.1) | async-done | bytes 458784 | tf_op jit(solution)/shard_map/all_to_all | solution.py:426
  34.0 2.1 %collective-permute-start = (bf16[8,64,128]{2,1,0:T(8,128)(2,1)S(1)}, bf16[8,64,128]{2,1,0:T(8,128)(2,1)S(1)}, u32[]{:S(2)}, u32[]{:S(2)}) collective-permute-start(bf16[8,64,128]{2,1,0:T(8,128)(2,1)S(1)} %rounded.2.refs_0_), channel_id=1, source_target_pairs={{0,32},{16,48},{32,64},{48,80},{64,96},{80,112},{96,0},{112,16},{1... | collective-permute-start | bytes 393224 | tf_op jit(solution)/shard_map/ppermute | solution.py:405
  36.3 2.4 %collective-permute-start.2 = (bf16[8,64,128]{2,1,0:T(8,128)(2,1)S(1)}, bf16[8,64,128]{2,1,0:T(8,128)(2,1)S(1)}, u32[]{:S(2)}, u32[]{:S(2)}) collective-permute-start(bf16[8,64,128]{2,1,0:T(8,128)(2,1)S(1)} %rounded.2.refs_0_), channel_id=1, source_target_pairs={{0,96},{16,112},{32,0},{48,16},{64,32},{80,48},{96,64},{112,80},{1... | collective-permute-start | bytes 393224 | tf_op jit(solution)/shard_map/ppermute | solution.py:405
  39.8 2.8 %collective-permute-done.1.refs_2_ = bf16[8,64,128]{2,1,0:T(8,128)(2,1)S(1)} collective-permute-done((bf16[8,64,128]{2,1,0:T(8,128)(2,1)S(1)}, bf16[8,64,128]{2,1,0:T(8,128)(2,1)S(1)}, u32[]{:S(2)}, u32[]{:S(2)}) %collective-permute-start.1) | collective-permute-done | bytes 131104 | tf_op jit(solution)/shard_map/ppermute | solution.py:405
  45.1 3.3 %products.6 = (bf16[16,256,128]{2,1,0:T(8,128)(2,1)}, f32[8,64,128]{2,1,0:T(8,128)}) custom-call(s32[128]{0:T(128)S(1)} %get-tuple-element.397.slot_ref, s32[128]{0:T(128)S(1)} %get-tuple-element.396.place_ref, s32[1]{0:T(128)} %bitcast.39.count_ref, bf16[128,128,128]{2,1,0:T(8,128)(2,1)S(1)} %copy-done.1, bf16[8,64,128]{2,1,0:T(8,128)(2,1)S(1)} %rounded.2.refs_0_, ...), custom_call_target="tpu_custom_call" | custom-call | tf_op jit(solution)/shard_map/products/pallas_call | solution.py:223
  48.4 4.7 %all-to-all-start.5 = ((bf16[16,256,128]{2,1,0:T(8,128)(2,1)}), bf16[16,256,128]{2,1,0:T(8,128)(2,1)S(1)}, u32[]{:S(2)}, u32[]{:S(2)}) async-start(bf16[16,256,128]{2,1,0:T(8,128)(2,1)} %get-tuple-element.335), calls=%async_computation.5 | async-start | bytes 2097152 | tf_op jit(solution)/shard_map/all_to_all | solution.py:426
  55.2 2.5 %collective-permute-start.9 = (bf16[8,64,128]{2,1,0:T(8,128)(2,1)S(1)}, bf16[8,64,128]{2,1,0:T(8,128)(2,1)S(1)}, u32[]{:S(2)}, u32[]{:S(2)}) collective-permute-start(bf16[8,64,128]{2,1,0:T(8,128)(2,1)S(1)} %rounded.3.refs_0_), channel_id=1, source_target_pairs={{0,96},{16,112},{32,0},{48,16},{64,32},{80,48},{96,64},{112,80},{1... | collective-permute-start | bytes 393224 | tf_op jit(solution)/shard_map/ppermute | solution.py:405
  58.7 3.4 %collective-permute-done.8.refs_2_ = bf16[8,64,128]{2,1,0:T(8,128)(2,1)S(1)} collective-permute-done((bf16[8,64,128]{2,1,0:T(8,128)(2,1)S(1)}, bf16[8,64,128]{2,1,0:T(8,128)(2,1)S(1)}, u32[]{:S(2)}, u32[]{:S(2)}) %collective-permute-start.8) | collective-permute-done | bytes 131104 | tf_op jit(solution)/shard_map/ppermute | solution.py:405
  64.7 3.3 %products.7 = (bf16[16,256,128]{2,1,0:T(8,128)(2,1)}, f32[8,64,128]{2,1,0:T(8,128)}) custom-call(s32[128]{0:T(128)S(1)} %get-tuple-element.397.slot_ref, s32[128]{0:T(128)S(1)} %get-tuple-element.396.place_ref, s32[1]{0:T(128)} %bitcast.40.count_ref, bf16[128,128,128]{2,1,0:T(8,128)(2,1)S(1)} %copy-done.2, bf16[8,64,128]{2,1,0:T(8,128)(2,1)S(1)} %rounded.3.refs_0_, ...), custom_call_target="tpu_custom_call" | custom-call | tf_op jit(solution)/shard_map/products/pallas_call | solution.py:223
  69.3 6.5 %all-to-all-start.2 = ((bf16[16,256,128]{2,1,0:T(8,128)(2,1)}), bf16[16,256,128]{2,1,0:T(8,128)(2,1)S(1)}, u32[]{:S(2)}, u32[]{:S(2)}) async-start(bf16[16,256,128]{2,1,0:T(8,128)(2,1)} %get-tuple-element.337), calls=%async_computation.2 | async-start | bytes 2097152 | tf_op jit(solution)/shard_map/all_to_all | solution.py:426
  78.8 2.5 %collective-permute-start.30 = (bf16[8,64,128]{2,1,0:T(8,128)(2,1)S(1)}, bf16[8,64,128]{2,1,0:T(8,128)(2,1)S(1)}, u32[]{:S(2)}, u32[]{:S(2)}) collective-permute-start(bf16[8,64,128]{2,1,0:T(8,128)(2,1)S(1)} %get-tuple-element.347.refs_0_), channel_id=1, source_target_pairs={{0,96},{16,112},{32,0},{48,16},{64,32},{80,48},{96,64},{112,80},{1... | collective-permute-start | bytes 393224 | tf_op jit(solution)/shard_map/ppermute | solution.py:405
  81.3 1.9 %collective-permute-done.28.refs_1_ = bf16[8,64,128]{2,1,0:T(8,128)(2,1)S(1)} collective-permute-done((bf16[8,64,128]{2,1,0:T(8,128)(2,1)S(1)}, bf16[8,64,128]{2,1,0:T(8,128)(2,1)S(1)}, u32[]{:S(2)}, u32[]{:S(2)}) %collective-permute-start.28) | collective-permute-done | bytes 131104 | tf_op jit(solution)/shard_map/ppermute | solution.py:405
  83.2 2.1 %collective-permute-done.29.refs_2_ = bf16[8,64,128]{2,1,0:T(8,128)(2,1)S(1)} collective-permute-done((bf16[8,64,128]{2,1,0:T(8,128)(2,1)S(1)}, bf16[8,64,128]{2,1,0:T(8,128)(2,1)S(1)}, u32[]{:S(2)}, u32[]{:S(2)}) %collective-permute-start.29) | collective-permute-done | bytes 131104 | tf_op jit(solution)/shard_map/ppermute | solution.py:405
  88.3 3.3 %products.10 = (bf16[16,256,128]{2,1,0:T(8,128)(2,1)}, f32[8,64,128]{2,1,0:T(8,128)}) custom-call(s32[128]{0:T(128)S(1)} %get-tuple-element.397.slot_ref, s32[128]{0:T(128)S(1)} %get-tuple-element.396.place_ref, s32[1]{0:T(128)} %bitcast.43.count_ref, bf16[128,128,128]{2,1,0:T(8,128)(2,1)S(1)} %copy-done.3, ...), custom_call_target="tpu_custom_call" | custom-call | tf_op jit(solution)/shard_map/products/pallas_call | solution.py:223
  92.0 7.4 %all-to-all-start.6 = ((bf16[16,256,128]{2,1,0:T(8,128)(2,1)}), bf16[16,256,128]{2,1,0:T(8,128)(2,1)S(1)}, u32[]{:S(2)}, u32[]{:S(2)}) async-start(bf16[16,256,128]{2,1,0:T(8,128)(2,1)} %get-tuple-element.350), calls=%async_computation.6 | async-start | bytes 2097152 | tf_op jit(solution)/shard_map/all_to_all | solution.py:426
  100.8 2.0 %collective-permute-start.15 = (bf16[8,64,128]{2,1,0:T(8,128)(2,1)S(1)}, bf16[8,64,128]{2,1,0:T(8,128)(2,1)S(1)}, u32[]{:S(2)}, u32[]{:S(2)}) collective-permute-start(bf16[8,64,128]{2,1,0:T(8,128)(2,1)S(1)} %get-tuple-element.338.refs_0_), channel_id=1, source_target_pairs={{0,64},{16,80},{32,96},{48,112},{64,0},{80,16},{96,32},{112,48},{1... | collective-permute-start | bytes 393224 | tf_op jit(solution)/shard_map/ppermute | solution.py:405
  102.7 2.5 %collective-permute-start.16 = (bf16[8,64,128]{2,1,0:T(8,128)(2,1)S(1)}, bf16[8,64,128]{2,1,0:T(8,128)(2,1)S(1)}, u32[]{:S(2)}, u32[]{:S(2)}) collective-permute-start(bf16[8,64,128]{2,1,0:T(8,128)(2,1)S(1)} %get-tuple-element.338.refs_0_), channel_id=1, source_target_pairs={{0,96},{16,112},{32,0},{48,16},{64,32},{80,48},{96,64},{112,80},{1... | collective-permute-start | bytes 393224 | tf_op jit(solution)/shard_map/ppermute | solution.py:405
  111.7 3.3 %products.8 = (bf16[16,256,128]{2,1,0:T(8,128)(2,1)}, f32[8,64,128]{2,1,0:T(8,128)}) custom-call(s32[128]{0:T(128)S(1)} %get-tuple-element.397.slot_ref, s32[128]{0:T(128)S(1)} %get-tuple-element.396.place_ref, s32[1]{0:T(128)} %bitcast.41.count_ref, bf16[128,128,128]{2,1,0:T(8,128)(2,1)S(1)} %copy-done.4, ...), custom_call_target="tpu_custom_call" | custom-call | tf_op jit(solution)/shard_map/products/pallas_call | solution.py:223
  115.7 7.2 %all-to-all-start.3 = ((bf16[16,256,128]{2,1,0:T(8,128)(2,1)}), bf16[16,256,128]{2,1,0:T(8,128)(2,1)S(1)}, u32[]{:S(2)}, u32[]{:S(2)}) async-start(bf16[16,256,128]{2,1,0:T(8,128)(2,1)} %get-tuple-element.341), calls=%async_computation.3 | async-start | bytes 2097152 | tf_op jit(solution)/shard_map/all_to_all | solution.py:426
  125.9 2.5 %collective-permute-start.37 = (bf16[8,64,128]{2,1,0:T(8,128)(2,1)S(1)}, bf16[8,64,128]{2,1,0:T(8,128)(2,1)S(1)}, u32[]{:S(2)}, u32[]{:S(2)}) collective-permute-start(bf16[8,64,128]{2,1,0:T(8,128)(2,1)S(1)} %get-tuple-element.351.refs_0_), channel_id=1, source_target_pairs={{0,96},{16,112},{32,0},{48,16},{64,32},{80,48},{96,64},{112,80},{1... | collective-permute-start | bytes 393224 | tf_op jit(solution)/shard_map/ppermute | solution.py:405
  135.0 3.3 %products.11 = (bf16[16,256,128]{2,1,0:T(8,128)(2,1)}, f32[8,64,128]{2,1,0:T(8,128)}) custom-call(s32[128]{0:T(128)S(1)} %get-tuple-element.397.slot_ref, s32[128]{0:T(128)S(1)} %get-tuple-element.396.place_ref, s32[1]{0:T(128)} %bitcast.44.count_ref, bf16[128,128,128]{2,1,0:T(8,128)(2,1)S(1)} %copy-done.5, ...), custom_call_target="tpu_custom_call" | custom-call | tf_op jit(solution)/shard_map/products/pallas_call | solution.py:223
  139.1 7.0 %all-to-all-start.7 = ((bf16[16,256,128]{2,1,0:T(8,128)(2,1)}), bf16[16,256,128]{2,1,0:T(8,128)(2,1)S(1)}, u32[]{:S(2)}, u32[]{:S(2)}) async-start(bf16[16,256,128]{2,1,0:T(8,128)(2,1)} %get-tuple-element.354), calls=%async_computation.7 | async-start | bytes 2097152 | tf_op jit(solution)/shard_map/all_to_all | solution.py:426
  149.1 2.5 %collective-permute-start.23 = (bf16[8,64,128]{2,1,0:T(8,128)(2,1)S(1)}, bf16[8,64,128]{2,1,0:T(8,128)(2,1)S(1)}, u32[]{:S(2)}, u32[]{:S(2)}) collective-permute-start(bf16[8,64,128]{2,1,0:T(8,128)(2,1)S(1)} %get-tuple-element.342.refs_0_), channel_id=1, source_target_pairs={{0,96},{16,112},{32,0},{48,16},{64,32},{80,48},{96,64},{112,80},{1... | collective-permute-start | bytes 393224 | tf_op jit(solution)/shard_map/ppermute | solution.py:405
  151.6 1.9 %collective-permute-done.21.refs_1_ = bf16[8,64,128]{2,1,0:T(8,128)(2,1)S(1)} collective-permute-done((bf16[8,64,128]{2,1,0:T(8,128)(2,1)S(1)}, bf16[8,64,128]{2,1,0:T(8,128)(2,1)S(1)}, u32[]{:S(2)}, u32[]{:S(2)}) %collective-permute-start.21) | collective-permute-done | bytes 131104 | tf_op jit(solution)/shard_map/ppermute | solution.py:405
  153.6 1.9 %collective-permute-done.22.refs_2_ = bf16[8,64,128]{2,1,0:T(8,128)(2,1)S(1)} collective-permute-done((bf16[8,64,128]{2,1,0:T(8,128)(2,1)S(1)}, bf16[8,64,128]{2,1,0:T(8,128)(2,1)S(1)}, u32[]{:S(2)}, u32[]{:S(2)}) %collective-permute-start.22) | collective-permute-done | bytes 131104 | tf_op jit(solution)/shard_map/ppermute | solution.py:405
  158.4 3.4 %products.9 = (bf16[16,256,128]{2,1,0:T(8,128)(2,1)}, f32[8,64,128]{2,1,0:T(8,128)}) custom-call(s32[128]{0:T(128)S(1)} %get-tuple-element.397.slot_ref, s32[128]{0:T(128)S(1)} %get-tuple-element.396.place_ref, s32[1]{0:T(128)} %bitcast.42.count_ref, bf16[128,128,128]{2,1,0:T(8,128)(2,1)S(1)} %copy-done.6, ...), custom_call_target="tpu_custom_call" | custom-call | tf_op jit(solution)/shard_map/products/pallas_call | solution.py:223
  162.4 7.2 %all-to-all-start.4 = ((bf16[16,256,128]{2,1,0:T(8,128)(2,1)}), bf16[16,256,128]{2,1,0:T(8,128)(2,1)S(1)}, u32[]{:S(2)}, u32[]{:S(2)}) async-start(bf16[16,256,128]{2,1,0:T(8,128)(2,1)} %get-tuple-element.345), calls=%async_computation.4 | async-start | bytes 2097152 | tf_op jit(solution)/shard_map/all_to_all | solution.py:426
  170.5 15.3 %all-to-all-done.4.got_ref = bf16[16,256,128]{2,1,0:T(8,128)(2,1)S(1)} async-done(((bf16[16,256,128]{2,1,0:T(8,128)(2,1)}), bf16[16,256,128]{2,1,0:T(8,128)(2,1)S(1)}, u32[]{:S(2)}, u32[]{:S(2)}) %all-to-all-start.4) | async-done | bytes 1048608 | tf_op jit(solution)/shard_map/all_to_all | solution.py:426
  (134 shorter events, 48.9 us)
Async XLA Ops:
  14.4 18.2 %all-to-all-start.1 = ((bf16[16,112,128]{2,1,0:T(8,128)(2,1)}), bf16[16,112,128]{2,1,0:T(8,128)(2,1)S(1)}, u32[]{:S(2)}, u32[]{:S(2)}) async-start(bf16[16,112,128]{2,1,0:T(8,128)(2,1)} %first_products.7), calls=%async_computation.1 | async-start | bytes 917504 | tf_op jit(solution)/shard_map/all_to_all | solution.py:426
  34.0 5.8 %collective-permute-start = (bf16[8,64,128]{2,1,0:T(8,128)(2,1)S(1)}, bf16[8,64,128]{2,1,0:T(8,128)(2,1)S(1)}, u32[]{:S(2)}, u32[]{:S(2)}) collective-permute-start(bf16[8,64,128]{2,1,0:T(8,128)(2,1)S(1)} %rounded.2.refs_0_), channel_id=1, source_target_pairs={{0,32},{16,48},{32,64},{48,80},{64,96},{80,112},{96,0},{112,16},{1... | collective-permute-start | bytes 393224 | tf_op jit(solution)/shard_map/ppermute | solution.py:405
  36.1 6.6 %collective-permute-start.1 = (bf16[8,64,128]{2,1,0:T(8,128)(2,1)S(1)}, bf16[8,64,128]{2,1,0:T(8,128)(2,1)S(1)}, u32[]{:S(2)}, u32[]{:S(2)}) collective-permute-start(bf16[8,64,128]{2,1,0:T(8,128)(2,1)S(1)} %rounded.2.refs_0_), channel_id=1, source_target_pairs={{0,64},{16,80},{32,96},{48,112},{64,0},{80,16},{96,32},{112,48},{1... | collective-permute-start | bytes 393224 | tf_op jit(solution)/shard_map/ppermute | solution.py:405
  36.3 7.4 %collective-permute-start.2 = (bf16[8,64,128]{2,1,0:T(8,128)(2,1)S(1)}, bf16[8,64,128]{2,1,0:T(8,128)(2,1)S(1)}, u32[]{:S(2)}, u32[]{:S(2)}) collective-permute-start(bf16[8,64,128]{2,1,0:T(8,128)(2,1)S(1)} %rounded.2.refs_0_), channel_id=1, source_target_pairs={{0,96},{16,112},{32,0},{48,16},{64,32},{80,48},{96,64},{112,80},{1... | collective-permute-start | bytes 393224 | tf_op jit(solution)/shard_map/ppermute | solution.py:405
  38.6 5.1 %collective-permute-start.3 = (bf16[8,64,128]{2,1,0:T(8,128)(2,1)S(1)}, bf16[8,64,128]{2,1,0:T(8,128)(2,1)S(1)}, u32[]{:S(2)}, u32[]{:S(2)}) collective-permute-start(bf16[8,64,128]{2,1,0:T(8,128)(2,1)S(1)} %rounded.2.refs_0_), channel_id=1, source_target_pairs={{0,16},{16,0},{32,48},{48,32},{64,80},{80,64},{96,112},{112,96},{1... | collective-permute-start | bytes 393224 | tf_op jit(solution)/shard_map/ppermute | solution.py:406
  48.4 20.9 %all-to-all-start.5 = ((bf16[16,256,128]{2,1,0:T(8,128)(2,1)}), bf16[16,256,128]{2,1,0:T(8,128)(2,1)S(1)}, u32[]{:S(2)}, u32[]{:S(2)}) async-start(bf16[16,256,128]{2,1,0:T(8,128)(2,1)} %get-tuple-element.335), calls=%async_computation.5 | async-start | bytes 2097152 | tf_op jit(solution)/shard_map/all_to_all | solution.py:426
  53.1 5.6 %collective-permute-start.7 = (bf16[8,64,128]{2,1,0:T(8,128)(2,1)S(1)}, bf16[8,64,128]{2,1,0:T(8,128)(2,1)S(1)}, u32[]{:S(2)}, u32[]{:S(2)}) collective-permute-start(bf16[8,64,128]{2,1,0:T(8,128)(2,1)S(1)} %rounded.3.refs_0_), channel_id=1, source_target_pairs={{0,32},{16,48},{32,64},{48,80},{64,96},{80,112},{96,0},{112,16},{1... | collective-permute-start | bytes 393224 | tf_op jit(solution)/shard_map/ppermute | solution.py:405
  54.7 7.4 %collective-permute-start.8 = (bf16[8,64,128]{2,1,0:T(8,128)(2,1)S(1)}, bf16[8,64,128]{2,1,0:T(8,128)(2,1)S(1)}, u32[]{:S(2)}, u32[]{:S(2)}) collective-permute-start(bf16[8,64,128]{2,1,0:T(8,128)(2,1)S(1)} %rounded.3.refs_0_), channel_id=1, source_target_pairs={{0,64},{16,80},{32,96},{48,112},{64,0},{80,16},{96,32},{112,48},{1... | collective-permute-start | bytes 393224 | tf_op jit(solution)/shard_map/ppermute | solution.py:405
  55.2 8.1 %collective-permute-start.9 = (bf16[8,64,128]{2,1,0:T(8,128)(2,1)S(1)}, bf16[8,64,128]{2,1,0:T(8,128)(2,1)S(1)}, u32[]{:S(2)}, u32[]{:S(2)}) collective-permute-start(bf16[8,64,128]{2,1,0:T(8,128)(2,1)S(1)} %rounded.3.refs_0_), channel_id=1, source_target_pairs={{0,96},{16,112},{32,0},{48,16},{64,32},{80,48},{96,64},{112,80},{1... | collective-permute-start | bytes 393224 | tf_op jit(solution)/shard_map/ppermute | solution.py:405
  57.8 5.5 %collective-permute-start.10 = (bf16[8,64,128]{2,1,0:T(8,128)(2,1)S(1)}, bf16[8,64,128]{2,1,0:T(8,128)(2,1)S(1)}, u32[]{:S(2)}, u32[]{:S(2)}) collective-permute-start(bf16[8,64,128]{2,1,0:T(8,128)(2,1)S(1)} %rounded.3.refs_0_), channel_id=1, source_target_pairs={{0,16},{16,0},{32,48},{48,32},{64,80},{80,64},{96,112},{112,96},{1... | collective-permute-start | bytes 393224 | tf_op jit(solution)/shard_map/ppermute | solution.py:406
  58.7 4.6 %collective-permute-start.11 = (bf16[8,64,128]{2,1,0:T(8,128)(2,1)S(1)}, bf16[8,64,128]{2,1,0:T(8,128)(2,1)S(1)}, u32[]{:S(2)}, u32[]{:S(2)}) collective-permute-start(bf16[8,64,128]{2,1,0:T(8,128)(2,1)S(1)} %collective-permute-done.7.refs_1_), channel_id=1, source_target_pairs={{0,16},{16,0},{32,48},{48,32},{64,80},{80,64},{96,112},{112,96},{1... | collective-permute-start | bytes 393224 | tf_op jit(solution)/shard_map/ppermute | solution.py:406
  69.3 22.7 %all-to-all-start.2 = ((bf16[16,256,128]{2,1,0:T(8,128)(2,1)}), bf16[16,256,128]{2,1,0:T(8,128)(2,1)S(1)}, u32[]{:S(2)}, u32[]{:S(2)}) async-start(bf16[16,256,128]{2,1,0:T(8,128)(2,1)} %get-tuple-element.337), calls=%async_computation.2 | async-start | bytes 2097152 | tf_op jit(solution)/shard_map/all_to_all | solution.py:426
  76.8 6.4 %collective-permute-start.28 = (bf16[8,64,128]{2,1,0:T(8,128)(2,1)S(1)}, bf16[8,64,128]{2,1,0:T(8,128)(2,1)S(1)}, u32[]{:S(2)}, u32[]{:S(2)}) collective-permute-start(bf16[8,64,128]{2,1,0:T(8,128)(2,1)S(1)} %get-tuple-element.347.refs_0_), channel_id=1, source_target_pairs={{0,32},{16,48},{32,64},{48,80},{64,96},{80,112},{96,0},{112,16},{1... | collective-permute-start | bytes 393224 | tf_op jit(solution)/shard_map/ppermute | solution.py:405
  77.4 7.9 %collective-permute-start.29 = (bf16[8,64,128]{2,1,0:T(8,128)(2,1)S(1)}, bf16[8,64,128]{2,1,0:T(8,128)(2,1)S(1)}, u32[]{:S(2)}, u32[]{:S(2)}) collective-permute-start(bf16[8,64,128]{2,1,0:T(8,128)(2,1)S(1)} %get-tuple-element.347.refs_0_), channel_id=1, source_target_pairs={{0,64},{16,80},{32,96},{48,112},{64,0},{80,16},{96,32},{112,48},{1... | collective-permute-start | bytes 393224 | tf_op jit(solution)/shard_map/ppermute | solution.py:405
  78.8 8.2 %collective-permute-start.30 = (bf16[8,64,128]{2,1,0:T(8,128)(2,1)S(1)}, bf16[8,64,128]{2,1,0:T(8,128)(2,1)S(1)}, u32[]{:S(2)}, u32[]{:S(2)}) collective-permute-start(bf16[8,64,128]{2,1,0:T(8,128)(2,1)S(1)} %get-tuple-element.347.refs_0_), channel_id=1, source_target_pairs={{0,96},{16,112},{32,0},{48,16},{64,32},{80,48},{96,64},{112,80},{1... | collective-permute-start | bytes 393224 | tf_op jit(solution)/shard_map/ppermute | solution.py:405
  81.3 5.8 %collective-permute-start.31 = (bf16[8,64,128]{2,1,0:T(8,128)(2,1)S(1)}, bf16[8,64,128]{2,1,0:T(8,128)(2,1)S(1)}, u32[]{:S(2)}, u32[]{:S(2)}) collective-permute-start(bf16[8,64,128]{2,1,0:T(8,128)(2,1)S(1)} %get-tuple-element.347.refs_0_), channel_id=1, source_target_pairs={{0,16},{16,0},{32,48},{48,32},{64,80},{80,64},{96,112},{112,96},{1... | collective-permute-start | bytes 393224 | tf_op jit(solution)/shard_map/ppermute | solution.py:406
  92.0 23.7 %all-to-all-start.6 = ((bf16[16,256,128]{2,1,0:T(8,128)(2,1)}), bf16[16,256,128]{2,1,0:T(8,128)(2,1)S(1)}, u32[]{:S(2)}, u32[]{:S(2)}) async-start(bf16[16,256,128]{2,1,0:T(8,128)(2,1)} %get-tuple-element.350), calls=%async_computation.6 | async-start | bytes 2097152 | tf_op jit(solution)/shard_map/all_to_all | solution.py:426
  100.4 6.4 %collective-permute-start.14 = (bf16[8,64,128]{2,1,0:T(8,128)(2,1)S(1)}, bf16[8,64,128]{2,1,0:T(8,128)(2,1)S(1)}, u32[]{:S(2)}, u32[]{:S(2)}) collective-permute-start(bf16[8,64,128]{2,1,0:T(8,128)(2,1)S(1)} %get-tuple-element.338.refs_0_), channel_id=1, source_target_pairs={{0,32},{16,48},{32,64},{48,80},{64,96},{80,112},{96,0},{112,16},{1... | collective-permute-start | bytes 393224 | tf_op jit(solution)/shard_map/ppermute | solution.py:405
  100.8 7.9 %collective-permute-start.15 = (bf16[8,64,128]{2,1,0:T(8,128)(2,1)S(1)}, bf16[8,64,128]{2,1,0:T(8,128)(2,1)S(1)}, u32[]{:S(2)}, u32[]{:S(2)}) collective-permute-start(bf16[8,64,128]{2,1,0:T(8,128)(2,1)S(1)} %get-tuple-element.338.refs_0_), channel_id=1, source_target_pairs={{0,64},{16,80},{32,96},{48,112},{64,0},{80,16},{96,32},{112,48},{1... | collective-permute-start | bytes 393224 | tf_op jit(solution)/shard_map/ppermute | solution.py:405
  102.7 7.6 %collective-permute-start.16 = (bf16[8,64,128]{2,1,0:T(8,128)(2,1)S(1)}, bf16[8,64,128]{2,1,0:T(8,128)(2,1)S(1)}, u32[]{:S(2)}, u32[]{:S(2)}) collective-permute-start(bf16[8,64,128]{2,1,0:T(8,128)(2,1)S(1)} %get-tuple-element.338.refs_0_), channel_id=1, source_target_pairs={{0,96},{16,112},{32,0},{48,16},{64,32},{80,48},{96,64},{112,80},{1... | collective-permute-start | bytes 393224 | tf_op jit(solution)/shard_map/ppermute | solution.py:405
  105.3 5.1 %collective-permute-start.17 = (bf16[8,64,128]{2,1,0:T(8,128)(2,1)S(1)}, bf16[8,64,128]{2,1,0:T(8,128)(2,1)S(1)}, u32[]{:S(2)}, u32[]{:S(2)}) collective-permute-start(bf16[8,64,128]{2,1,0:T(8,128)(2,1)S(1)} %get-tuple-element.338.refs_0_), channel_id=1, source_target_pairs={{0,16},{16,0},{32,48},{48,32},{64,80},{80,64},{96,112},{112,96},{1... | collective-permute-start | bytes 393224 | tf_op jit(solution)/shard_map/ppermute | solution.py:406
  115.7 23.4 %all-to-all-start.3 = ((bf16[16,256,128]{2,1,0:T(8,128)(2,1)}), bf16[16,256,128]{2,1,0:T(8,128)(2,1)S(1)}, u32[]{:S(2)}, u32[]{:S(2)}) async-start(bf16[16,256,128]{2,1,0:T(8,128)(2,1)} %get-tuple-element.341), calls=%async_computation.3 | async-start | bytes 2097152 | tf_op jit(solution)/shard_map/all_to_all | solution.py:426
  123.8 6.4 %collective-permute-start.35 = (bf16[8,64,128]{2,1,0:T(8,128)(2,1)S(1)}, bf16[8,64,128]{2,1,0:T(8,128)(2,1)S(1)}, u32[]{:S(2)}, u32[]{:S(2)}) collective-permute-start(bf16[8,64,128]{2,1,0:T(8,128)(2,1)S(1)} %get-tuple-element.351.refs_0_), channel_id=1, source_target_pairs={{0,32},{16,48},{32,64},{48,80},{64,96},{80,112},{96,0},{112,16},{1... | collective-permute-start | bytes 393224 | tf_op jit(solution)/shard_map/ppermute | solution.py:405
  124.2 7.9 %collective-permute-start.36 = (bf16[8,64,128]{2,1,0:T(8,128)(2,1)S(1)}, bf16[8,64,128]{2,1,0:T(8,128)(2,1)S(1)}, u32[]{:S(2)}, u32[]{:S(2)}) collective-permute-start(bf16[8,64,128]{2,1,0:T(8,128)(2,1)S(1)} %get-tuple-element.351.refs_0_), channel_id=1, source_target_pairs={{0,64},{16,80},{32,96},{48,112},{64,0},{80,16},{96,32},{112,48},{1... | collective-permute-start | bytes 393224 | tf_op jit(solution)/shard_map/ppermute | solution.py:405
  125.9 7.8 %collective-permute-start.37 = (bf16[8,64,128]{2,1,0:T(8,128)(2,1)S(1)}, bf16[8,64,128]{2,1,0:T(8,128)(2,1)S(1)}, u32[]{:S(2)}, u32[]{:S(2)}) collective-permute-start(bf16[8,64,128]{2,1,0:T(8,128)(2,1)S(1)} %get-tuple-element.351.refs_0_), channel_id=1, source_target_pairs={{0,96},{16,112},{32,0},{48,16},{64,32},{80,48},{96,64},{112,80},{1... | collective-permute-start | bytes 393224 | tf_op jit(solution)/shard_map/ppermute | solution.py:405
  128.4 5.3 %collective-permute-start.38 = (bf16[8,64,128]{2,1,0:T(8,128)(2,1)S(1)}, bf16[8,64,128]{2,1,0:T(8,128)(2,1)S(1)}, u32[]{:S(2)}, u32[]{:S(2)}) collective-permute-start(bf16[8,64,128]{2,1,0:T(8,128)(2,1)S(1)} %get-tuple-element.351.refs_0_), channel_id=1, source_target_pairs={{0,16},{16,0},{32,48},{48,32},{64,80},{80,64},{96,112},{112,96},{1... | collective-permute-start | bytes 393224 | tf_op jit(solution)/shard_map/ppermute | solution.py:406
  139.1 23.3 %all-to-all-start.7 = ((bf16[16,256,128]{2,1,0:T(8,128)(2,1)}), bf16[16,256,128]{2,1,0:T(8,128)(2,1)S(1)}, u32[]{:S(2)}, u32[]{:S(2)}) async-start(bf16[16,256,128]{2,1,0:T(8,128)(2,1)} %get-tuple-element.354), calls=%async_computation.7 | async-start | bytes 2097152 | tf_op jit(solution)/shard_map/all_to_all | solution.py:426
  147.1 6.4 %collective-permute-start.21 = (bf16[8,64,128]{2,1,0:T(8,128)(2,1)S(1)}, bf16[8,64,128]{2,1,0:T(8,128)(2,1)S(1)}, u32[]{:S(2)}, u32[]{:S(2)}) collective-permute-start(bf16[8,64,128]{2,1,0:T(8,128)(2,1)S(1)} %get-tuple-element.342.refs_0_), channel_id=1, source_target_pairs={{0,32},{16,48},{32,64},{48,80},{64,96},{80,112},{96,0},{112,16},{1... | collective-permute-start | bytes 393224 | tf_op jit(solution)/shard_map/ppermute | solution.py:405
  147.6 7.9 %collective-permute-start.22 = (bf16[8,64,128]{2,1,0:T(8,128)(2,1)S(1)}, bf16[8,64,128]{2,1,0:T(8,128)(2,1)S(1)}, u32[]{:S(2)}, u32[]{:S(2)}) collective-permute-start(bf16[8,64,128]{2,1,0:T(8,128)(2,1)S(1)} %get-tuple-element.342.refs_0_), channel_id=1, source_target_pairs={{0,64},{16,80},{32,96},{48,112},{64,0},{80,16},{96,32},{112,48},{1... | collective-permute-start | bytes 393224 | tf_op jit(solution)/shard_map/ppermute | solution.py:405
  149.1 8.0 %collective-permute-start.23 = (bf16[8,64,128]{2,1,0:T(8,128)(2,1)S(1)}, bf16[8,64,128]{2,1,0:T(8,128)(2,1)S(1)}, u32[]{:S(2)}, u32[]{:S(2)}) collective-permute-start(bf16[8,64,128]{2,1,0:T(8,128)(2,1)S(1)} %get-tuple-element.342.refs_0_), channel_id=1, source_target_pairs={{0,96},{16,112},{32,0},{48,16},{64,32},{80,48},{96,64},{112,80},{1... | collective-permute-start | bytes 393224 | tf_op jit(solution)/shard_map/ppermute | solution.py:405
  151.6 5.4 %collective-permute-start.24 = (bf16[8,64,128]{2,1,0:T(8,128)(2,1)S(1)}, bf16[8,64,128]{2,1,0:T(8,128)(2,1)S(1)}, u32[]{:S(2)}, u32[]{:S(2)}) collective-permute-start(bf16[8,64,128]{2,1,0:T(8,128)(2,1)S(1)} %get-tuple-element.342.refs_0_), channel_id=1, source_target_pairs={{0,16},{16,0},{32,48},{48,32},{64,80},{80,64},{96,112},{112,96},{1... | collective-permute-start | bytes 393224 | tf_op jit(solution)/shard_map/ppermute | solution.py:406
  162.4 23.4 %all-to-all-start.4 = ((bf16[16,256,128]{2,1,0:T(8,128)(2,1)}), bf16[16,256,128]{2,1,0:T(8,128)(2,1)S(1)}, u32[]{:S(2)}, u32[]{:S(2)}) async-start(bf16[16,256,128]{2,1,0:T(8,128)(2,1)} %get-tuple-element.345), calls=%async_computation.4 | async-start | bytes 2097152 | tf_op jit(solution)/shard_map/all_to_all | solution.py:426
  (30 other events, 170.4 us)

commit v4 on v3

--- a/solution.py
+++ b/solution.py
@@ -15,9 +15,9 @@
 STREAMS = 2
 PLACES = 24
 ID_ROWS = 16
-UNROLL = 8
+UNROLL = 16
 FIRST_UNROLL = 8
-CHUNK = 32
+CHUNK = 64
 VMEM_LIMIT = 14 * 1024 * 1024
 
 VMEM = pl.BlockSpec(memory_space=pltpu.VMEM)
@@ -374,20 +374,29 @@
     queries = sum(part.shape[1] for part in done) + width
 
     def body(id_ref, got_ref, damping_ref, score_ref, *refs):
-        done_refs, (out_ref, acc_ref) = refs[:-2], refs[-2:]
+        done_refs, (out_ref, acc_ref, block_ref, sems) = refs[:-4], refs[-4:]
         summed(id_ref, got_ref, acc_ref)
         coef = power(damping_ref, step)
+        leaving = []
         for block in range(BPD):
             mine = score_ref[block] + coef * acc_ref[block]
             rows = [part[block] for part in done_refs] + [mine]
-            out_ref[block] = jnp.transpose(jnp.concatenate(rows, axis=0))
-
-    return pl.pallas_call(
-        body,
-        out_shape=jax.ShapeDtypeStruct((BPD, tile, queries), F32),
+            block_ref[block] = jnp.transpose(jnp.concatenate(rows, axis=0))
+            leaving.append(pltpu.make_async_copy(block_ref.at[block], out_ref.at[block], sems.at[block]))
+            leaving[-1].start()
+        for copy in leaving:
+            copy.wait()
+
+    return pl.pallas_call(
+        body,
+        out_shape=pltpu.HBM((BPD, tile, queries), F32),
         in_specs=[SMEM] + [VMEM] * (3 + len(done)),
-        out_specs=VMEM,
-        scratch_shapes=[pltpu.VMEM((BPD + 1, width, tile), F32)],
+        out_specs=HBM,
+        scratch_shapes=[
+            pltpu.VMEM((BPD + 1, width, tile), F32),
+            pltpu.VMEM((BPD, tile, queries), F32),
+            pltpu.SemaphoreType.DMA((BPD,)),
+        ],
         compiler_params=PARAMS,
         name="last",
     )(ids, got, damping, scores, *done)

time: 190 us -> 188 us (0.989)
  no operation moved by 1% of the time
where the time goes in v4:
time: 188 us; the launch traced here: 187 us
  starting transfers between devices  75.6 us (40%)
  waiting for transfers between devices  67.8 us (36%)
  Pallas kernels  35.2 us (19%)
  local copies, waits for them, and re-layouts  3.72 us (2%)
  between operations  3.06 us (2%)
    all_to_all x7, starting transfers between devices, exchange(): lax.all_to_all(sent, 'col', split_axis=0, concat_axis=0, tiled=True, axis...  47 us
    ppermute x18, waiting for transfers between devices, column_parts(): lax.ppermute(mine, 'row', row_shift(dz, 0))  31.1 us
    all_to_all x7, waiting for transfers between devices, exchange(): lax.all_to_all(sent, 'col', split_axis=0, concat_axis=0, tiled=True, axis...  28.8 us
    ppermute x18, starting transfers between devices, column_parts(): lax.ppermute(mine, 'row', row_shift(dz, 0))  28.3 us
    pallas_call x6, Pallas kernels, products(): pl.pallas_call(body, out_shape=(jax.ShapeDtypeStruct((owners, rows, tile)...  19.4 us
    ppermute x24, waiting for transfers between devices, column_parts(): other = [lax.ppermute(part, 'row', row_shift(0, 1)) for part in same]  7.85 us
    pallas_call x1, Pallas kernels, first_products(): pl.pallas_call(body, out_shape=jax.ShapeDtypeStruct((n_col, sent_rows + I...  5.17 us
    pallas_call x4, Pallas kernels, owned_sum(): pl.pallas_call(body, out_shape=(jax.ShapeDtypeStruct((BPD, width, tile),...  3.87 us
  transfers between devices with their start and end apart: 49, of which 33 were waited for; matrix products, arithmetic and copies ran while one was open for 0% of the time, Pallas kernels for 11%

profile of v4, /device:TPU:32, one launch (start us, length us, event | category | flops | bytes accessed | tf_op | source)
XLA Modules:
  0.0 186.8 jit_solution(2266852534927214354)
XLA Ops:
  0.8 5.2 %first_products.7 = bf16[16,112,128]{2,1,0:T(8,128)(2,1)} custom-call(s32[3]{0:T(128)S(1)} %pad_add_fusion.1.info_ref, s32[128]{0:T(128)} %bitcast.52, s32[128]{0:T(128)} %bitcast.50, s32[128]{0:T(128)} %query_ref.1, bf16[128,128,128]{2,1,0:T(8,128)(2,1)} %bitcast.47), custom_call_target="tpu_custom_call" | custom-call | tf_op jit(solution)/shard_map/first_products/pallas_call | solution.py:176
  9.3 2.9 %turned.1.tiles_ref = bf16[128,128,128]{2,1,0:T(8,128)(2,1)S(1)} custom-call(s32[1]{0:T(128)} %bitcast.38.count_ref, bf16[128,128,128]{2,1,0:T(8,128)(2,1)} %bitcast.48), custom_call_target="tpu_custom_call" | custom-call | tf_op jit(solution)/shard_map/turned/pallas_call | solution.py:260
  12.2 2.0 %copy-done = bf16[128,128,128]{2,1,0:T(8,128)(2,1)} copy-done((bf16[128,128,128]{2,1,0:T(8,128)(2,1)}, bf16[128,128,128]{2,1,0:T(8,128)(2,1)S(1)}, u32[]{:S(2)}) %copy-start) | copy-done | bytes 4194328
  14.2 7.8 %all-to-all-start.1 = ((bf16[16,112,128]{2,1,0:T(8,128)(2,1)}), bf16[16,112,128]{2,1,0:T(8,128)(2,1)S(1)}, u32[]{:S(2)}, u32[]{:S(2)}) async-start(bf16[16,112,128]{2,1,0:T(8,128)(2,1)} %first_products.7), calls=%async_computation.1 | async-start | bytes 917504 | tf_op jit(solution)/shard_map/all_to_all | solution.py:435
  22.1 10.1 %all-to-all-done.1.got_ref = bf16[16,112,128]{2,1,0:T(8,128)(2,1)S(1)} async-done(((bf16[16,112,128]{2,1,0:T(8,128)(2,1)}), bf16[16,112,128]{2,1,0:T(8,128)(2,1)S(1)}, u32[]{:S(2)}, u32[]{:S(2)}) %all-to-all-start.1) | async-done | bytes 458784 | tf_op jit(solution)/shard_map/all_to_all | solution.py:435
  33.6 2.1 %collective-permute-start = (bf16[8,64,128]{2,1,0:T(8,128)(2,1)S(1)}, bf16[8,64,128]{2,1,0:T(8,128)(2,1)S(1)}, u32[]{:S(2)}, u32[]{:S(2)}) collective-permute-start(bf16[8,64,128]{2,1,0:T(8,128)(2,1)S(1)} %rounded.2.refs_0_), channel_id=1, source_target_pairs={{0,32},{16,48},{32,64},{48,80},{64,96},{80,112},{96,0},{112,16},{1... | collective-permute-start | bytes 393224 | tf_op jit(solution)/shard_map/ppermute | solution.py:414
  35.8 2.4 %collective-permute-start.2 = (bf16[8,64,128]{2,1,0:T(8,128)(2,1)S(1)}, bf16[8,64,128]{2,1,0:T(8,128)(2,1)S(1)}, u32[]{:S(2)}, u32[]{:S(2)}) collective-permute-start(bf16[8,64,128]{2,1,0:T(8,128)(2,1)S(1)} %rounded.2.refs_0_), channel_id=1, source_target_pairs={{0,96},{16,112},{32,0},{48,16},{64,32},{80,48},{96,64},{112,80},{1... | collective-permute-start | bytes 393224 | tf_op jit(solution)/shard_map/ppermute | solution.py:414
  39.4 2.8 %collective-permute-done.1.refs_2_ = bf16[8,64,128]{2,1,0:T(8,128)(2,1)S(1)} collective-permute-done((bf16[8,64,128]{2,1,0:T(8,128)(2,1)S(1)}, bf16[8,64,128]{2,1,0:T(8,128)(2,1)S(1)}, u32[]{:S(2)}, u32[]{:S(2)}) %collective-permute-start.1) | collective-permute-done | bytes 131104 | tf_op jit(solution)/shard_map/ppermute | solution.py:414
  44.1 3.2 %products.6 = (bf16[16,256,128]{2,1,0:T(8,128)(2,1)}, f32[8,64,128]{2,1,0:T(8,128)}) custom-call(s32[128]{0:T(128)S(1)} %get-tuple-element.397.slot_ref, s32[128]{0:T(128)S(1)} %get-tuple-element.396.place_ref, s32[1]{0:T(128)} %bitcast.39.count_ref, bf16[128,128,128]{2,1,0:T(8,128)(2,1)S(1)} %copy-done.1, bf16[8,64,128]{2,1,0:T(8,128)(2,1)S(1)} %rounded.2.refs_0_, ...), custom_call_target="tpu_custom_call" | custom-call | tf_op jit(solution)/shard_map/products/pallas_call | solution.py:223
  47.3 4.8 %all-to-all-start.5 = ((bf16[16,256,128]{2,1,0:T(8,128)(2,1)}), bf16[16,256,128]{2,1,0:T(8,128)(2,1)S(1)}, u32[]{:S(2)}, u32[]{:S(2)}) async-start(bf16[16,256,128]{2,1,0:T(8,128)(2,1)} %get-tuple-element.335), calls=%async_computation.5 | async-start | bytes 2097152 | tf_op jit(solution)/shard_map/all_to_all | solution.py:435
  52.1 1.9 %collective-permute-start.7 = (bf16[8,64,128]{2,1,0:T(8,128)(2,1)S(1)}, bf16[8,64,128]{2,1,0:T(8,128)(2,1)S(1)}, u32[]{:S(2)}, u32[]{:S(2)}) collective-permute-start(bf16[8,64,128]{2,1,0:T(8,128)(2,1)S(1)} %rounded.3.refs_0_), channel_id=1, source_target_pairs={{0,32},{16,48},{32,64},{48,80},{64,96},{80,112},{96,0},{112,16},{1... | collective-permute-start | bytes 393224 | tf_op jit(solution)/shard_map/ppermute | solution.py:414
  54.5 2.5 %collective-permute-start.9 = (bf16[8,64,128]{2,1,0:T(8,128)(2,1)S(1)}, bf16[8,64,128]{2,1,0:T(8,128)(2,1)S(1)}, u32[]{:S(2)}, u32[]{:S(2)}) collective-permute-start(bf16[8,64,128]{2,1,0:T(8,128)(2,1)S(1)} %rounded.3.refs_0_), channel_id=1, source_target_pairs={{0,96},{16,112},{32,0},{48,16},{64,32},{80,48},{96,64},{112,80},{1... | collective-permute-start | bytes 393224 | tf_op jit(solution)/shard_map/ppermute | solution.py:414
  57.6 3.8 %collective-permute-done.8.refs_2_ = bf16[8,64,128]{2,1,0:T(8,128)(2,1)S(1)} collective-permute-done((bf16[8,64,128]{2,1,0:T(8,128)(2,1)S(1)}, bf16[8,64,128]{2,1,0:T(8,128)(2,1)S(1)}, u32[]{:S(2)}, u32[]{:S(2)}) %collective-permute-start.8) | collective-permute-done | bytes 131104 | tf_op jit(solution)/shard_map/ppermute | solution.py:414
  64.0 3.2 %products.7 = (bf16[16,256,128]{2,1,0:T(8,128)(2,1)}, f32[8,64,128]{2,1,0:T(8,128)}) custom-call(s32[128]{0:T(128)S(1)} %get-tuple-element.397.slot_ref, s32[128]{0:T(128)S(1)} %get-tuple-element.396.place_ref, s32[1]{0:T(128)} %bitcast.40.count_ref, bf16[128,128,128]{2,1,0:T(8,128)(2,1)S(1)} %copy-done.2, bf16[8,64,128]{2,1,0:T(8,128)(2,1)S(1)} %rounded.3.refs_0_, ...), custom_call_target="tpu_custom_call" | custom-call | tf_op jit(solution)/shard_map/products/pallas_call | solution.py:223
  68.3 6.5 %all-to-all-start.2 = ((bf16[16,256,128]{2,1,0:T(8,128)(2,1)}), bf16[16,256,128]{2,1,0:T(8,128)(2,1)S(1)}, u32[]{:S(2)}, u32[]{:S(2)}) async-start(bf16[16,256,128]{2,1,0:T(8,128)(2,1)} %get-tuple-element.337), calls=%async_computation.2 | async-start | bytes 2097152 | tf_op jit(solution)/shard_map/all_to_all | solution.py:435
  78.4 2.0 %collective-permute-start.30 = (bf16[8,64,128]{2,1,0:T(8,128)(2,1)S(1)}, bf16[8,64,128]{2,1,0:T(8,128)(2,1)S(1)}, u32[]{:S(2)}, u32[]{:S(2)}) collective-permute-start(bf16[8,64,128]{2,1,0:T(8,128)(2,1)S(1)} %get-tuple-element.347.refs_0_), channel_id=1, source_target_pairs={{0,96},{16,112},{32,0},{48,16},{64,32},{80,48},{96,64},{112,80},{1... | collective-permute-start | bytes 393224 | tf_op jit(solution)/shard_map/ppermute | solution.py:414
  80.4 1.9 %collective-permute-done.28.refs_1_ = bf16[8,64,128]{2,1,0:T(8,128)(2,1)S(1)} collective-permute-done((bf16[8,64,128]{2,1,0:T(8,128)(2,1)S(1)}, bf16[8,64,128]{2,1,0:T(8,128)(2,1)S(1)}, u32[]{:S(2)}, u32[]{:S(2)}) %collective-permute-start.28) | collective-permute-done | bytes 131104 | tf_op jit(solution)/shard_map/ppermute | solution.py:414
  82.4 2.1 %collective-permute-done.29.refs_2_ = bf16[8,64,128]{2,1,0:T(8,128)(2,1)S(1)} collective-permute-done((bf16[8,64,128]{2,1,0:T(8,128)(2,1)S(1)}, bf16[8,64,128]{2,1,0:T(8,128)(2,1)S(1)}, u32[]{:S(2)}, u32[]{:S(2)}) %collective-permute-start.29) | collective-permute-done | bytes 131104 | tf_op jit(solution)/shard_map/ppermute | solution.py:414
  87.5 3.3 %products.10 = (bf16[16,256,128]{2,1,0:T(8,128)(2,1)}, f32[8,64,128]{2,1,0:T(8,128)}) custom-call(s32[128]{0:T(128)S(1)} %get-tuple-element.397.slot_ref, s32[128]{0:T(128)S(1)} %get-tuple-element.396.place_ref, s32[1]{0:T(128)} %bitcast.43.count_ref, bf16[128,128,128]{2,1,0:T(8,128)(2,1)S(1)} %copy-done.3, ...), custom_call_target="tpu_custom_call" | custom-call | tf_op jit(solution)/shard_map/products/pallas_call | solution.py:223
  91.0 7.3 %all-to-all-start.6 = ((bf16[16,256,128]{2,1,0:T(8,128)(2,1)}), bf16[16,256,128]{2,1,0:T(8,128)(2,1)S(1)}, u32[]{:S(2)}, u32[]{:S(2)}) async-start(bf16[16,256,128]{2,1,0:T(8,128)(2,1)} %get-tuple-element.350), calls=%async_computation.6 | async-start | bytes 2097152 | tf_op jit(solution)/shard_map/all_to_all | solution.py:435
  99.7 2.0 %collective-permute-start.15 = (bf16[8,64,128]{2,1,0:T(8,128)(2,1)S(1)}, bf16[8,64,128]{2,1,0:T(8,128)(2,1)S(1)}, u32[]{:S(2)}, u32[]{:S(2)}) collective-permute-start(bf16[8,64,128]{2,1,0:T(8,128)(2,1)S(1)} %get-tuple-element.338.refs_0_), channel_id=1, source_target_pairs={{0,64},{16,80},{32,96},{48,112},{64,0},{80,16},{96,32},{112,48},{1... | collective-permute-start | bytes 393224 | tf_op jit(solution)/shard_map/ppermute | solution.py:414
  101.6 2.5 %collective-permute-start.16 = (bf16[8,64,128]{2,1,0:T(8,128)(2,1)S(1)}, bf16[8,64,128]{2,1,0:T(8,128)(2,1)S(1)}, u32[]{:S(2)}, u32[]{:S(2)}) collective-permute-start(bf16[8,64,128]{2,1,0:T(8,128)(2,1)S(1)} %get-tuple-element.338.refs_0_), channel_id=1, source_target_pairs={{0,96},{16,112},{32,0},{48,16},{64,32},{80,48},{96,64},{112,80},{1... | collective-permute-start | bytes 393224 | tf_op jit(solution)/shard_map/ppermute | solution.py:414
  105.7 1.9 %collective-permute-done.15.refs_2_ = bf16[8,64,128]{2,1,0:T(8,128)(2,1)S(1)} collective-permute-done((bf16[8,64,128]{2,1,0:T(8,128)(2,1)S(1)}, bf16[8,64,128]{2,1,0:T(8,128)(2,1)S(1)}, u32[]{:S(2)}, u32[]{:S(2)}) %collective-permute-start.15) | collective-permute-done | bytes 131104 | tf_op jit(solution)/shard_map/ppermute | solution.py:414
  110.6 3.3 %products.8 = (bf16[16,256,128]{2,1,0:T(8,128)(2,1)}, f32[8,64,128]{2,1,0:T(8,128)}) custom-call(s32[128]{0:T(128)S(1)} %get-tuple-element.397.slot_ref, s32[128]{0:T(128)S(1)} %get-tuple-element.396.place_ref, s32[1]{0:T(128)} %bitcast.41.count_ref, bf16[128,128,128]{2,1,0:T(8,128)(2,1)S(1)} %copy-done.4, ...), custom_call_target="tpu_custom_call" | custom-call | tf_op jit(solution)/shard_map/products/pallas_call | solution.py:223
  114.6 6.9 %all-to-all-start.3 = ((bf16[16,256,128]{2,1,0:T(8,128)(2,1)}), bf16[16,256,128]{2,1,0:T(8,128)(2,1)S(1)}, u32[]{:S(2)}, u32[]{:S(2)}) async-start(bf16[16,256,128]{2,1,0:T(8,128)(2,1)} %get-tuple-element.341), calls=%async_computation.3 | async-start | bytes 2097152 | tf_op jit(solution)/shard_map/all_to_all | solution.py:435
  124.5 2.5 %collective-permute-start.37 = (bf16[8,64,128]{2,1,0:T(8,128)(2,1)S(1)}, bf16[8,64,128]{2,1,0:T(8,128)(2,1)S(1)}, u32[]{:S(2)}, u32[]{:S(2)}) collective-permute-start(bf16[8,64,128]{2,1,0:T(8,128)(2,1)S(1)} %get-tuple-element.351.refs_0_), channel_id=1, source_target_pairs={{0,96},{16,112},{32,0},{48,16},{64,32},{80,48},{96,64},{112,80},{1... | collective-permute-start | bytes 393224 | tf_op jit(solution)/shard_map/ppermute | solution.py:414
  133.7 3.3 %products.11 = (bf16[16,256,128]{2,1,0:T(8,128)(2,1)}, f32[8,64,128]{2,1,0:T(8,128)}) custom-call(s32[128]{0:T(128)S(1)} %get-tuple-element.397.slot_ref, s32[128]{0:T(128)S(1)} %get-tuple-element.396.place_ref, s32[1]{0:T(128)} %bitcast.44.count_ref, bf16[128,128,128]{2,1,0:T(8,128)(2,1)S(1)} %copy-done.5, ...), custom_call_target="tpu_custom_call" | custom-call | tf_op jit(solution)/shard_map/products/pallas_call | solution.py:223
  137.7 6.9 %all-to-all-start.7 = ((bf16[16,256,128]{2,1,0:T(8,128)(2,1)}), bf16[16,256,128]{2,1,0:T(8,128)(2,1)S(1)}, u32[]{:S(2)}, u32[]{:S(2)}) async-start(bf16[16,256,128]{2,1,0:T(8,128)(2,1)} %get-tuple-element.354), calls=%async_computation.7 | async-start | bytes 2097152 | tf_op jit(solution)/shard_map/all_to_all | solution.py:435
  147.7 2.5 %collective-permute-start.23 = (bf16[8,64,128]{2,1,0:T(8,128)(2,1)S(1)}, bf16[8,64,128]{2,1,0:T(8,128)(2,1)S(1)}, u32[]{:S(2)}, u32[]{:S(2)}) collective-permute-start(bf16[8,64,128]{2,1,0:T(8,128)(2,1)S(1)} %get-tuple-element.342.refs_0_), channel_id=1, source_target_pairs={{0,96},{16,112},{32,0},{48,16},{64,32},{80,48},{96,64},{112,80},{1... | collective-permute-start | bytes 393224 | tf_op jit(solution)/shard_map/ppermute | solution.py:414
  156.8 3.3 %products.9 = (bf16[16,256,128]{2,1,0:T(8,128)(2,1)}, f32[8,64,128]{2,1,0:T(8,128)}) custom-call(s32[128]{0:T(128)S(1)} %get-tuple-element.397.slot_ref, s32[128]{0:T(128)S(1)} %get-tuple-element.396.place_ref, s32[1]{0:T(128)} %bitcast.42.count_ref, bf16[128,128,128]{2,1,0:T(8,128)(2,1)S(1)} %copy-done.6, ...), custom_call_target="tpu_custom_call" | custom-call | tf_op jit(solution)/shard_map/products/pallas_call | solution.py:223
  160.8 6.8 %all-to-all-start.4 = ((bf16[16,256,128]{2,1,0:T(8,128)(2,1)}), bf16[16,256,128]{2,1,0:T(8,128)(2,1)S(1)}, u32[]{:S(2)}, u32[]{:S(2)}) async-start(bf16[16,256,128]{2,1,0:T(8,128)(2,1)} %get-tuple-element.345), calls=%async_computation.4 | async-start | bytes 2097152 | tf_op jit(solution)/shard_map/all_to_all | solution.py:435
  168.6 15.3 %all-to-all-done.4.got_ref = bf16[16,256,128]{2,1,0:T(8,128)(2,1)S(1)} async-done(((bf16[16,256,128]{2,1,0:T(8,128)(2,1)}), bf16[16,256,128]{2,1,0:T(8,128)(2,1)S(1)}, u32[]{:S(2)}, u32[]{:S(2)}) %all-to-all-start.4) | async-done | bytes 1048608 | tf_op jit(solution)/shard_map/all_to_all | solution.py:435
  (134 shorter events, 48.9 us)
Async XLA Ops:
  14.2 18.0 %all-to-all-start.1 = ((bf16[16,112,128]{2,1,0:T(8,128)(2,1)}), bf16[16,112,128]{2,1,0:T(8,128)(2,1)S(1)}, u32[]{:S(2)}, u32[]{:S(2)}) async-start(bf16[16,112,128]{2,1,0:T(8,128)(2,1)} %first_products.7), calls=%async_computation.1 | async-start | bytes 917504 | tf_op jit(solution)/shard_map/all_to_all | solution.py:435
  33.6 5.8 %collective-permute-start = (bf16[8,64,128]{2,1,0:T(8,128)(2,1)S(1)}, bf16[8,64,128]{2,1,0:T(8,128)(2,1)S(1)}, u32[]{:S(2)}, u32[]{:S(2)}) collective-permute-start(bf16[8,64,128]{2,1,0:T(8,128)(2,1)S(1)} %rounded.2.refs_0_), channel_id=1, source_target_pairs={{0,32},{16,48},{32,64},{48,80},{64,96},{80,112},{96,0},{112,16},{1... | collective-permute-start | bytes 393224 | tf_op jit(solution)/shard_map/ppermute | solution.py:414
  35.6 6.6 %collective-permute-start.1 = (bf16[8,64,128]{2,1,0:T(8,128)(2,1)S(1)}, bf16[8,64,128]{2,1,0:T(8,128)(2,1)S(1)}, u32[]{:S(2)}, u32[]{:S(2)}) collective-permute-start(bf16[8,64,128]{2,1,0:T(8,128)(2,1)S(1)} %rounded.2.refs_0_), channel_id=1, source_target_pairs={{0,64},{16,80},{32,96},{48,112},{64,0},{80,16},{96,32},{112,48},{1... | collective-permute-start | bytes 393224 | tf_op jit(solution)/shard_map/ppermute | solution.py:414
  35.8 6.8 %collective-permute-start.2 = (bf16[8,64,128]{2,1,0:T(8,128)(2,1)S(1)}, bf16[8,64,128]{2,1,0:T(8,128)(2,1)S(1)}, u32[]{:S(2)}, u32[]{:S(2)}) collective-permute-start(bf16[8,64,128]{2,1,0:T(8,128)(2,1)S(1)} %rounded.2.refs_0_), channel_id=1, source_target_pairs={{0,96},{16,112},{32,0},{48,16},{64,32},{80,48},{96,64},{112,80},{1... | collective-permute-start | bytes 393224 | tf_op jit(solution)/shard_map/ppermute | solution.py:414
  38.2 4.6 %collective-permute-start.3 = (bf16[8,64,128]{2,1,0:T(8,128)(2,1)S(1)}, bf16[8,64,128]{2,1,0:T(8,128)(2,1)S(1)}, u32[]{:S(2)}, u32[]{:S(2)}) collective-permute-start(bf16[8,64,128]{2,1,0:T(8,128)(2,1)S(1)} %rounded.2.refs_0_), channel_id=1, source_target_pairs={{0,16},{16,0},{32,48},{48,32},{64,80},{80,64},{96,112},{112,96},{1... | collective-permute-start | bytes 393224 | tf_op jit(solution)/shard_map/ppermute | solution.py:415
  47.3 21.0 %all-to-all-start.5 = ((bf16[16,256,128]{2,1,0:T(8,128)(2,1)}), bf16[16,256,128]{2,1,0:T(8,128)(2,1)S(1)}, u32[]{:S(2)}, u32[]{:S(2)}) async-start(bf16[16,256,128]{2,1,0:T(8,128)(2,1)} %get-tuple-element.335), calls=%async_computation.5 | async-start | bytes 2097152 | tf_op jit(solution)/shard_map/all_to_all | solution.py:435
  52.1 5.3 %collective-permute-start.7 = (bf16[8,64,128]{2,1,0:T(8,128)(2,1)S(1)}, bf16[8,64,128]{2,1,0:T(8,128)(2,1)S(1)}, u32[]{:S(2)}, u32[]{:S(2)}) collective-permute-start(bf16[8,64,128]{2,1,0:T(8,128)(2,1)S(1)} %rounded.3.refs_0_), channel_id=1, source_target_pairs={{0,32},{16,48},{32,64},{48,80},{64,96},{80,112},{96,0},{112,16},{1... | collective-permute-start | bytes 393224 | tf_op jit(solution)/shard_map/ppermute | solution.py:414
  54.0 7.4 %collective-permute-start.8 = (bf16[8,64,128]{2,1,0:T(8,128)(2,1)S(1)}, bf16[8,64,128]{2,1,0:T(8,128)(2,1)S(1)}, u32[]{:S(2)}, u32[]{:S(2)}) collective-permute-start(bf16[8,64,128]{2,1,0:T(8,128)(2,1)S(1)} %rounded.3.refs_0_), channel_id=1, source_target_pairs={{0,64},{16,80},{32,96},{48,112},{64,0},{80,16},{96,32},{112,48},{1... | collective-permute-start | bytes 393224 | tf_op jit(solution)/shard_map/ppermute | solution.py:414
  54.5 8.1 %collective-permute-start.9 = (bf16[8,64,128]{2,1,0:T(8,128)(2,1)S(1)}, bf16[8,64,128]{2,1,0:T(8,128)(2,1)S(1)}, u32[]{:S(2)}, u32[]{:S(2)}) collective-permute-start(bf16[8,64,128]{2,1,0:T(8,128)(2,1)S(1)} %rounded.3.refs_0_), channel_id=1, source_target_pairs={{0,96},{16,112},{32,0},{48,16},{64,32},{80,48},{96,64},{112,80},{1... | collective-permute-start | bytes 393224 | tf_op jit(solution)/shard_map/ppermute | solution.py:414
  57.0 5.5 %collective-permute-start.10 = (bf16[8,64,128]{2,1,0:T(8,128)(2,1)S(1)}, bf16[8,64,128]{2,1,0:T(8,128)(2,1)S(1)}, u32[]{:S(2)}, u32[]{:S(2)}) collective-permute-start(bf16[8,64,128]{2,1,0:T(8,128)(2,1)S(1)} %rounded.3.refs_0_), channel_id=1, source_target_pairs={{0,16},{16,0},{32,48},{48,32},{64,80},{80,64},{96,112},{112,96},{1... | collective-permute-start | bytes 393224 | tf_op jit(solution)/shard_map/ppermute | solution.py:415
  57.4 5.2 %collective-permute-start.11 = (bf16[8,64,128]{2,1,0:T(8,128)(2,1)S(1)}, bf16[8,64,128]{2,1,0:T(8,128)(2,1)S(1)}, u32[]{:S(2)}, u32[]{:S(2)}) collective-permute-start(bf16[8,64,128]{2,1,0:T(8,128)(2,1)S(1)} %collective-permute-done.7.refs_1_), channel_id=1, source_target_pairs={{0,16},{16,0},{32,48},{48,32},{64,80},{80,64},{96,112},{112,96},{1... | collective-permute-start | bytes 393224 | tf_op jit(solution)/shard_map/ppermute | solution.py:415
  68.3 22.7 %all-to-all-start.2 = ((bf16[16,256,128]{2,1,0:T(8,128)(2,1)}), bf16[16,256,128]{2,1,0:T(8,128)(2,1)S(1)}, u32[]{:S(2)}, u32[]{:S(2)}) async-start(bf16[16,256,128]{2,1,0:T(8,128)(2,1)} %get-tuple-element.337), calls=%async_computation.2 | async-start | bytes 2097152 | tf_op jit(solution)/shard_map/all_to_all | solution.py:435
  75.8 6.6 %collective-permute-start.28 = (bf16[8,64,128]{2,1,0:T(8,128)(2,1)S(1)}, bf16[8,64,128]{2,1,0:T(8,128)(2,1)S(1)}, u32[]{:S(2)}, u32[]{:S(2)}) collective-permute-start(bf16[8,64,128]{2,1,0:T(8,128)(2,1)S(1)} %get-tuple-element.347.refs_0_), channel_id=1, source_target_pairs={{0,32},{16,48},{32,64},{48,80},{64,96},{80,112},{96,0},{112,16},{1... | collective-permute-start | bytes 393224 | tf_op jit(solution)/shard_map/ppermute | solution.py:414
  76.6 7.9 %collective-permute-start.29 = (bf16[8,64,128]{2,1,0:T(8,128)(2,1)S(1)}, bf16[8,64,128]{2,1,0:T(8,128)(2,1)S(1)}, u32[]{:S(2)}, u32[]{:S(2)}) collective-permute-start(bf16[8,64,128]{2,1,0:T(8,128)(2,1)S(1)} %get-tuple-element.347.refs_0_), channel_id=1, source_target_pairs={{0,64},{16,80},{32,96},{48,112},{64,0},{80,16},{96,32},{112,48},{1... | collective-permute-start | bytes 393224 | tf_op jit(solution)/shard_map/ppermute | solution.py:414
  78.4 7.8 %collective-permute-start.30 = (bf16[8,64,128]{2,1,0:T(8,128)(2,1)S(1)}, bf16[8,64,128]{2,1,0:T(8,128)(2,1)S(1)}, u32[]{:S(2)}, u32[]{:S(2)}) collective-permute-start(bf16[8,64,128]{2,1,0:T(8,128)(2,1)S(1)} %get-tuple-element.347.refs_0_), channel_id=1, source_target_pairs={{0,96},{16,112},{32,0},{48,16},{64,32},{80,48},{96,64},{112,80},{1... | collective-permute-start | bytes 393224 | tf_op jit(solution)/shard_map/ppermute | solution.py:414
  80.4 5.7 %collective-permute-start.31 = (bf16[8,64,128]{2,1,0:T(8,128)(2,1)S(1)}, bf16[8,64,128]{2,1,0:T(8,128)(2,1)S(1)}, u32[]{:S(2)}, u32[]{:S(2)}) collective-permute-start(bf16[8,64,128]{2,1,0:T(8,128)(2,1)S(1)} %get-tuple-element.347.refs_0_), channel_id=1, source_target_pairs={{0,16},{16,0},{32,48},{48,32},{64,80},{80,64},{96,112},{112,96},{1... | collective-permute-start | bytes 393224 | tf_op jit(solution)/shard_map/ppermute | solution.py:415
  91.0 23.6 %all-to-all-start.6 = ((bf16[16,256,128]{2,1,0:T(8,128)(2,1)}), bf16[16,256,128]{2,1,0:T(8,128)(2,1)S(1)}, u32[]{:S(2)}, u32[]{:S(2)}) async-start(bf16[16,256,128]{2,1,0:T(8,128)(2,1)} %get-tuple-element.350), calls=%async_computation.6 | async-start | bytes 2097152 | tf_op jit(solution)/shard_map/all_to_all | solution.py:435
  99.3 6.3 %collective-permute-start.14 = (bf16[8,64,128]{2,1,0:T(8,128)(2,1)S(1)}, bf16[8,64,128]{2,1,0:T(8,128)(2,1)S(1)}, u32[]{:S(2)}, u32[]{:S(2)}) collective-permute-start(bf16[8,64,128]{2,1,0:T(8,128)(2,1)S(1)} %get-tuple-element.338.refs_0_), channel_id=1, source_target_pairs={{0,32},{16,48},{32,64},{48,80},{64,96},{80,112},{96,0},{112,16},{1... | collective-permute-start | bytes 393224 | tf_op jit(solution)/shard_map/ppermute | solution.py:414
  99.7 7.9 %collective-permute-start.15 = (bf16[8,64,128]{2,1,0:T(8,128)(2,1)S(1)}, bf16[8,64,128]{2,1,0:T(8,128)(2,1)S(1)}, u32[]{:S(2)}, u32[]{:S(2)}) collective-permute-start(bf16[8,64,128]{2,1,0:T(8,128)(2,1)S(1)} %get-tuple-element.338.refs_0_), channel_id=1, source_target_pairs={{0,64},{16,80},{32,96},{48,112},{64,0},{80,16},{96,32},{112,48},{1... | collective-permute-start | bytes 393224 | tf_op jit(solution)/shard_map/ppermute | solution.py:414
  101.6 7.6 %collective-permute-start.16 = (bf16[8,64,128]{2,1,0:T(8,128)(2,1)S(1)}, bf16[8,64,128]{2,1,0:T(8,128)(2,1)S(1)}, u32[]{:S(2)}, u32[]{:S(2)}) collective-permute-start(bf16[8,64,128]{2,1,0:T(8,128)(2,1)S(1)} %get-tuple-element.338.refs_0_), channel_id=1, source_target_pairs={{0,96},{16,112},{32,0},{48,16},{64,32},{80,48},{96,64},{112,80},{1... | collective-permute-start | bytes 393224 | tf_op jit(solution)/shard_map/ppermute | solution.py:414
  104.2 5.1 %collective-permute-start.17 = (bf16[8,64,128]{2,1,0:T(8,128)(2,1)S(1)}, bf16[8,64,128]{2,1,0:T(8,128)(2,1)S(1)}, u32[]{:S(2)}, u32[]{:S(2)}) collective-permute-start(bf16[8,64,128]{2,1,0:T(8,128)(2,1)S(1)} %get-tuple-element.338.refs_0_), channel_id=1, source_target_pairs={{0,16},{16,0},{32,48},{48,32},{64,80},{80,64},{96,112},{112,96},{1... | collective-permute-start | bytes 393224 | tf_op jit(solution)/shard_map/ppermute | solution.py:415
  114.6 23.1 %all-to-all-start.3 = ((bf16[16,256,128]{2,1,0:T(8,128)(2,1)}), bf16[16,256,128]{2,1,0:T(8,128)(2,1)S(1)}, u32[]{:S(2)}, u32[]{:S(2)}) async-start(bf16[16,256,128]{2,1,0:T(8,128)(2,1)} %get-tuple-element.341), calls=%async_computation.3 | async-start | bytes 2097152 | tf_op jit(solution)/shard_map/all_to_all | solution.py:435
  122.5 6.4 %collective-permute-start.35 = (bf16[8,64,128]{2,1,0:T(8,128)(2,1)S(1)}, bf16[8,64,128]{2,1,0:T(8,128)(2,1)S(1)}, u32[]{:S(2)}, u32[]{:S(2)}) collective-permute-start(bf16[8,64,128]{2,1,0:T(8,128)(2,1)S(1)} %get-tuple-element.351.refs_0_), channel_id=1, source_target_pairs={{0,32},{16,48},{32,64},{48,80},{64,96},{80,112},{96,0},{112,16},{1... | collective-permute-start | bytes 393224 | tf_op jit(solution)/shard_map/ppermute | solution.py:414
  122.8 7.9 %collective-permute-start.36 = (bf16[8,64,128]{2,1,0:T(8,128)(2,1)S(1)}, bf16[8,64,128]{2,1,0:T(8,128)(2,1)S(1)}, u32[]{:S(2)}, u32[]{:S(2)}) collective-permute-start(bf16[8,64,128]{2,1,0:T(8,128)(2,1)S(1)} %get-tuple-element.351.refs_0_), channel_id=1, source_target_pairs={{0,64},{16,80},{32,96},{48,112},{64,0},{80,16},{96,32},{112,48},{1... | collective-permute-start | bytes 393224 | tf_op jit(solution)/shard_map/ppermute | solution.py:414
  124.5 7.9 %collective-permute-start.37 = (bf16[8,64,128]{2,1,0:T(8,128)(2,1)S(1)}, bf16[8,64,128]{2,1,0:T(8,128)(2,1)S(1)}, u32[]{:S(2)}, u32[]{:S(2)}) collective-permute-start(bf16[8,64,128]{2,1,0:T(8,128)(2,1)S(1)} %get-tuple-element.351.refs_0_), channel_id=1, source_target_pairs={{0,96},{16,112},{32,0},{48,16},{64,32},{80,48},{96,64},{112,80},{1... | collective-permute-start | bytes 393224 | tf_op jit(solution)/shard_map/ppermute | solution.py:414
  127.0 5.4 %collective-permute-start.38 = (bf16[8,64,128]{2,1,0:T(8,128)(2,1)S(1)}, bf16[8,64,128]{2,1,0:T(8,128)(2,1)S(1)}, u32[]{:S(2)}, u32[]{:S(2)}) collective-permute-start(bf16[8,64,128]{2,1,0:T(8,128)(2,1)S(1)} %get-tuple-element.351.refs_0_), channel_id=1, source_target_pairs={{0,16},{16,0},{32,48},{48,32},{64,80},{80,64},{96,112},{112,96},{1... | collective-permute-start | bytes 393224 | tf_op jit(solution)/shard_map/ppermute | solution.py:415
  137.7 23.1 %all-to-all-start.7 = ((bf16[16,256,128]{2,1,0:T(8,128)(2,1)}), bf16[16,256,128]{2,1,0:T(8,128)(2,1)S(1)}, u32[]{:S(2)}, u32[]{:S(2)}) async-start(bf16[16,256,128]{2,1,0:T(8,128)(2,1)} %get-tuple-element.354), calls=%async_computation.7 | async-start | bytes 2097152 | tf_op jit(solution)/shard_map/all_to_all | solution.py:435
  145.6 6.4 %collective-permute-start.21 = (bf16[8,64,128]{2,1,0:T(8,128)(2,1)S(1)}, bf16[8,64,128]{2,1,0:T(8,128)(2,1)S(1)}, u32[]{:S(2)}, u32[]{:S(2)}) collective-permute-start(bf16[8,64,128]{2,1,0:T(8,128)(2,1)S(1)} %get-tuple-element.342.refs_0_), channel_id=1, source_target_pairs={{0,32},{16,48},{32,64},{48,80},{64,96},{80,112},{96,0},{112,16},{1... | collective-permute-start | bytes 393224 | tf_op jit(solution)/shard_map/ppermute | solution.py:414
  145.9 7.9 %collective-permute-start.22 = (bf16[8,64,128]{2,1,0:T(8,128)(2,1)S(1)}, bf16[8,64,128]{2,1,0:T(8,128)(2,1)S(1)}, u32[]{:S(2)}, u32[]{:S(2)}) collective-permute-start(bf16[8,64,128]{2,1,0:T(8,128)(2,1)S(1)} %get-tuple-element.342.refs_0_), channel_id=1, source_target_pairs={{0,64},{16,80},{32,96},{48,112},{64,0},{80,16},{96,32},{112,48},{1... | collective-permute-start | bytes 393224 | tf_op jit(solution)/shard_map/ppermute | solution.py:414
  147.7 7.7 %collective-permute-start.23 = (bf16[8,64,128]{2,1,0:T(8,128)(2,1)S(1)}, bf16[8,64,128]{2,1,0:T(8,128)(2,1)S(1)}, u32[]{:S(2)}, u32[]{:S(2)}) collective-permute-start(bf16[8,64,128]{2,1,0:T(8,128)(2,1)S(1)} %get-tuple-element.342.refs_0_), channel_id=1, source_target_pairs={{0,96},{16,112},{32,0},{48,16},{64,32},{80,48},{96,64},{112,80},{1... | collective-permute-start | bytes 393224 | tf_op jit(solution)/shard_map/ppermute | solution.py:414
  150.3 5.2 %collective-permute-start.24 = (bf16[8,64,128]{2,1,0:T(8,128)(2,1)S(1)}, bf16[8,64,128]{2,1,0:T(8,128)(2,1)S(1)}, u32[]{:S(2)}, u32[]{:S(2)}) collective-permute-start(bf16[8,64,128]{2,1,0:T(8,128)(2,1)S(1)} %get-tuple-element.342.refs_0_), channel_id=1, source_target_pairs={{0,16},{16,0},{32,48},{48,32},{64,80},{80,64},{96,112},{112,96},{1... | collective-permute-start | bytes 393224 | tf_op jit(solution)/shard_map/ppermute | solution.py:415
  160.8 23.1 %all-to-all-start.4 = ((bf16[16,256,128]{2,1,0:T(8,128)(2,1)}), bf16[16,256,128]{2,1,0:T(8,128)(2,1)S(1)}, u32[]{:S(2)}, u32[]{:S(2)}) async-start(bf16[16,256,128]{2,1,0:T(8,128)(2,1)} %get-tuple-element.345), calls=%async_computation.4 | async-start | bytes 2097152 | tf_op jit(solution)/shard_map/all_to_all | solution.py:435
  (30 other events, 168.8 us)

commit v5 on v4

--- a/solution.py
+++ b/solution.py
@@ -37,7 +37,7 @@
     return coef
 
 
-def multiply_tiles(slot_ref, place_ref, count, tile_ref, x_parts, acc_ref, x_ref):
+def multiply_tiles(slot_ref, place_ref, count, tile_ref, x_parts, acc_ref, x_ref, aside):
     each = x_ref.shape[0] // len(x_parts)
     for part, part_ref in enumerate(x_parts):
         x_ref[part * each : (part + 1) * each] = part_ref[...]
@@ -56,9 +56,10 @@
     def chunk_step(chunk, carry):
         for part in range(CHUNK // UNROLL):
             group(chunk * CHUNK + part * UNROLL)
+        pl.when(chunk == 0)(aside)
         return carry
 
-    lax.fori_loop(0, (count + CHUNK - 1) // CHUNK, chunk_step, 0)
+    lax.fori_loop(0, jnp.maximum((count + CHUNK - 1) // CHUNK, 1), chunk_step, 0)
 
 
 def first_products(round_index, rows, cols, query_ids, count, col, tiles, n_col, n_row):
@@ -208,15 +209,18 @@
         out_ref, score_out, score_ref, score_sems, acc_ref, *scratch = refs
         for ref in score_in:
             pltpu.make_async_copy(ref, score_ref, score_sems.at[0]).start()
-        multiply_tiles(slot_ref, place_ref, count_ref[0], tiles_ref, x_refs, acc_ref, *scratch)
-        for ref in score_in:
-            pltpu.make_async_copy(ref, score_ref, score_sems.at[0]).wait()
-        if score_in:
-            score_ref[...] = score_ref[...] + power(damping_ref, step - 1)[None] * owned_ref[...]
-        else:
-            score_ref[...] = owned_ref[...]
         leave = pltpu.make_async_copy(score_ref, score_out, score_sems.at[1])
-        leave.start()
+
+        def add_scores():
+            for ref in score_in:
+                pltpu.make_async_copy(ref, score_ref, score_sems.at[0]).wait()
+            if score_in:
+                score_ref[...] = score_ref[...] + power(damping_ref, step - 1)[None] * owned_ref[...]
+            else:
+                score_ref[...] = owned_ref[...]
+            leave.start()
+
+        multiply_tiles(slot_ref, place_ref, count_ref[0], tiles_ref, x_refs, acc_ref, *scratch, add_scores)
         out_ref[...] = acc_ref[: owners * TOUCH].astype(BF16).reshape(owners, rows, tile)
         leave.wait()
 

time: 188 us -> 187 us (level)
  starting transfers between devices: 75.6 us -> 73.5 us
    all_to_all x7, starting transfers between devices: 47 us -> 44.1 us  [exchange(): lax.all_to_all(sent, 'col', split_axis=0, concat_axis=0, tiled=True, axis...]
  transfers between devices with their start and end apart: 49 -> 49, of which waited for: 33 -> 32; matrix products, arithmetic and copies ran while one was open for 0% -> 0% of each run, Pallas kernels for 11% -> 11%
where the time goes in v5:
time: 187 us; the launch traced here: 184 us
  starting transfers between devices  73.5 us (39%)
  waiting for transfers between devices  67.1 us (36%)
  Pallas kernels  35.2 us (19%)
  local copies, waits for them, and re-layouts  3.72 us (2%)
  between operations  3.08 us (2%)
    all_to_all x7, starting transfers between devices, exchange(): lax.all_to_all(sent, 'col', split_axis=0, concat_axis=0, tiled=True, axis...  44.1 us
    ppermute x18, waiting for transfers between devices, column_parts(): lax.ppermute(mine, 'row', row_shift(dz, 0))  30.6 us
    ppermute x18, starting transfers between devices, column_parts(): lax.ppermute(mine, 'row', row_shift(dz, 0))  28.9 us
    all_to_all x7, waiting for transfers between devices, exchange(): lax.all_to_all(sent, 'col', split_axis=0, concat_axis=0, tiled=True, axis...  28.7 us
    pallas_call x6, Pallas kernels, products(): pl.pallas_call(body, out_shape=(jax.ShapeDtypeStruct((owners, rows, tile)...  19.4 us
    ppermute x24, waiting for transfers between devices, column_parts(): other = [lax.ppermute(part, 'row', row_shift(0, 1)) for part in same]  7.86 us
    pallas_call x1, Pallas kernels, first_products(): pl.pallas_call(body, out_shape=jax.ShapeDtypeStruct((n_col, sent_rows + I...  5.17 us
    pallas_call x4, Pallas kernels, owned_sum(): pl.pallas_call(body, out_shape=(jax.ShapeDtypeStruct((BPD, width, tile),...  3.87 us
  transfers between devices with their start and end apart: 49, of which 32 were waited for; matrix products, arithmetic and copies ran while one was open for 0% of the time, Pallas kernels for 11%

profile of v5, /device:TPU:32, one launch (start us, length us, event | category | flops | bytes accessed | tf_op | source)
XLA Modules:
  0.0 184.0 jit_solution(6699962816403544738)
XLA Ops:
  0.8 5.2 %first_products.7 = bf16[16,112,128]{2,1,0:T(8,128)(2,1)} custom-call(s32[3]{0:T(128)S(1)} %pad_add_fusion.1.info_ref, s32[128]{0:T(128)} %bitcast.52, s32[128]{0:T(128)} %bitcast.50, s32[128]{0:T(128)} %query_ref.1, bf16[128,128,128]{2,1,0:T(8,128)(2,1)} %bitcast.47), custom_call_target="tpu_custom_call" | custom-call | tf_op jit(solution)/shard_map/first_products/pallas_call | solution.py:177
  9.3 2.9 %turned.1.tiles_ref = bf16[128,128,128]{2,1,0:T(8,128)(2,1)S(1)} custom-call(s32[1]{0:T(128)} %bitcast.38.count_ref, bf16[128,128,128]{2,1,0:T(8,128)(2,1)} %bitcast.48), custom_call_target="tpu_custom_call" | custom-call | tf_op jit(solution)/shard_map/turned/pallas_call | solution.py:264
  12.2 2.0 %copy-done = bf16[128,128,128]{2,1,0:T(8,128)(2,1)} copy-done((bf16[128,128,128]{2,1,0:T(8,128)(2,1)}, bf16[128,128,128]{2,1,0:T(8,128)(2,1)S(1)}, u32[]{:S(2)}) %copy-start) | copy-done | bytes 4194328
  14.2 7.8 %all-to-all-start.1 = ((bf16[16,112,128]{2,1,0:T(8,128)(2,1)}), bf16[16,112,128]{2,1,0:T(8,128)(2,1)S(1)}, u32[]{:S(2)}, u32[]{:S(2)}) async-start(bf16[16,112,128]{2,1,0:T(8,128)(2,1)} %first_products.7), calls=%async_computation.1 | async-start | bytes 917504 | tf_op jit(solution)/shard_map/all_to_all | solution.py:439
  22.1 10.1 %all-to-all-done.1.got_ref = bf16[16,112,128]{2,1,0:T(8,128)(2,1)S(1)} async-done(((bf16[16,112,128]{2,1,0:T(8,128)(2,1)}), bf16[16,112,128]{2,1,0:T(8,128)(2,1)S(1)}, u32[]{:S(2)}, u32[]{:S(2)}) %all-to-all-start.1) | async-done | bytes 458784 | tf_op jit(solution)/shard_map/all_to_all | solution.py:439
  33.6 2.1 %collective-permute-start = (bf16[8,64,128]{2,1,0:T(8,128)(2,1)S(1)}, bf16[8,64,128]{2,1,0:T(8,128)(2,1)S(1)}, u32[]{:S(2)}, u32[]{:S(2)}) collective-permute-start(bf16[8,64,128]{2,1,0:T(8,128)(2,1)S(1)} %rounded.2.refs_0_), channel_id=1, source_target_pairs={{0,32},{16,48},{32,64},{48,80},{64,96},{80,112},{96,0},{112,16},{1... | collective-permute-start | bytes 393224 | tf_op jit(solution)/shard_map/ppermute | solution.py:418
  35.8 2.4 %collective-permute-start.2 = (bf16[8,64,128]{2,1,0:T(8,128)(2,1)S(1)}, bf16[8,64,128]{2,1,0:T(8,128)(2,1)S(1)}, u32[]{:S(2)}, u32[]{:S(2)}) collective-permute-start(bf16[8,64,128]{2,1,0:T(8,128)(2,1)S(1)} %rounded.2.refs_0_), channel_id=1, source_target_pairs={{0,96},{16,112},{32,0},{48,16},{64,32},{80,48},{96,64},{112,80},{1... | collective-permute-start | bytes 393224 | tf_op jit(solution)/shard_map/ppermute | solution.py:418
  39.4 2.8 %collective-permute-done.1.refs_2_ = bf16[8,64,128]{2,1,0:T(8,128)(2,1)S(1)} collective-permute-done((bf16[8,64,128]{2,1,0:T(8,128)(2,1)S(1)}, bf16[8,64,128]{2,1,0:T(8,128)(2,1)S(1)}, u32[]{:S(2)}, u32[]{:S(2)}) %collective-permute-start.1) | collective-permute-done | bytes 131104 | tf_op jit(solution)/shard_map/ppermute | solution.py:418
  44.1 3.2 %products.6 = (bf16[16,256,128]{2,1,0:T(8,128)(2,1)}, f32[8,64,128]{2,1,0:T(8,128)}) custom-call(s32[128]{0:T(128)S(1)} %get-tuple-element.397.slot_ref, s32[128]{0:T(128)S(1)} %get-tuple-element.396.place_ref, s32[1]{0:T(128)} %bitcast.39.count_ref, bf16[128,128,128]{2,1,0:T(8,128)(2,1)S(1)} %copy-done.1, bf16[8,64,128]{2,1,0:T(8,128)(2,1)S(1)} %rounded.2.refs_0_, ...), custom_call_target="tpu_custom_call" | custom-call | tf_op jit(solution)/shard_map/products/pallas_call | solution.py:227
  47.2 4.4 %all-to-all-start.5 = ((bf16[16,256,128]{2,1,0:T(8,128)(2,1)}), bf16[16,256,128]{2,1,0:T(8,128)(2,1)S(1)}, u32[]{:S(2)}, u32[]{:S(2)}) async-start(bf16[16,256,128]{2,1,0:T(8,128)(2,1)} %get-tuple-element.335), calls=%async_computation.5 | async-start | bytes 2097152 | tf_op jit(solution)/shard_map/all_to_all | solution.py:439
  54.2 2.5 %collective-permute-start.9 = (bf16[8,64,128]{2,1,0:T(8,128)(2,1)S(1)}, bf16[8,64,128]{2,1,0:T(8,128)(2,1)S(1)}, u32[]{:S(2)}, u32[]{:S(2)}) collective-permute-start(bf16[8,64,128]{2,1,0:T(8,128)(2,1)S(1)} %rounded.3.refs_0_), channel_id=1, source_target_pairs={{0,96},{16,112},{32,0},{48,16},{64,32},{80,48},{96,64},{112,80},{1... | collective-permute-start | bytes 393224 | tf_op jit(solution)/shard_map/ppermute | solution.py:418
  57.3 4.0 %collective-permute-done.8.refs_2_ = bf16[8,64,128]{2,1,0:T(8,128)(2,1)S(1)} collective-permute-done((bf16[8,64,128]{2,1,0:T(8,128)(2,1)S(1)}, bf16[8,64,128]{2,1,0:T(8,128)(2,1)S(1)}, u32[]{:S(2)}, u32[]{:S(2)}) %collective-permute-start.8) | collective-permute-done | bytes 131104 | tf_op jit(solution)/shard_map/ppermute | solution.py:418
  63.4 3.2 %products.7 = (bf16[16,256,128]{2,1,0:T(8,128)(2,1)}, f32[8,64,128]{2,1,0:T(8,128)}) custom-call(s32[128]{0:T(128)S(1)} %get-tuple-element.397.slot_ref, s32[128]{0:T(128)S(1)} %get-tuple-element.396.place_ref, s32[1]{0:T(128)} %bitcast.40.count_ref, bf16[128,128,128]{2,1,0:T(8,128)(2,1)S(1)} %copy-done.2, bf16[8,64,128]{2,1,0:T(8,128)(2,1)S(1)} %rounded.3.refs_0_, ...), custom_call_target="tpu_custom_call" | custom-call | tf_op jit(solution)/shard_map/products/pallas_call | solution.py:227
  67.9 5.8 %all-to-all-start.2 = ((bf16[16,256,128]{2,1,0:T(8,128)(2,1)}), bf16[16,256,128]{2,1,0:T(8,128)(2,1)S(1)}, u32[]{:S(2)}, u32[]{:S(2)}) async-start(bf16[16,256,128]{2,1,0:T(8,128)(2,1)} %get-tuple-element.337), calls=%async_computation.2 | async-start | bytes 2097152 | tf_op jit(solution)/shard_map/all_to_all | solution.py:439
  81.0 2.9 %collective-permute-done.29.refs_2_ = bf16[8,64,128]{2,1,0:T(8,128)(2,1)S(1)} collective-permute-done((bf16[8,64,128]{2,1,0:T(8,128)(2,1)S(1)}, bf16[8,64,128]{2,1,0:T(8,128)(2,1)S(1)}, u32[]{:S(2)}, u32[]{:S(2)}) %collective-permute-start.29) | collective-permute-done | bytes 131104 | tf_op jit(solution)/shard_map/ppermute | solution.py:418
  86.8 3.3 %products.10 = (bf16[16,256,128]{2,1,0:T(8,128)(2,1)}, f32[8,64,128]{2,1,0:T(8,128)}) custom-call(s32[128]{0:T(128)S(1)} %get-tuple-element.397.slot_ref, s32[128]{0:T(128)S(1)} %get-tuple-element.396.place_ref, s32[1]{0:T(128)} %bitcast.43.count_ref, bf16[128,128,128]{2,1,0:T(8,128)(2,1)S(1)} %copy-done.3, ...), custom_call_target="tpu_custom_call" | custom-call | tf_op jit(solution)/shard_map/products/pallas_call | solution.py:227
  90.0 7.0 %all-to-all-start.6 = ((bf16[16,256,128]{2,1,0:T(8,128)(2,1)}), bf16[16,256,128]{2,1,0:T(8,128)(2,1)S(1)}, u32[]{:S(2)}, u32[]{:S(2)}) async-start(bf16[16,256,128]{2,1,0:T(8,128)(2,1)} %get-tuple-element.350), calls=%async_computation.6 | async-start | bytes 2097152 | tf_op jit(solution)/shard_map/all_to_all | solution.py:439
  98.6 2.0 %collective-permute-start.15 = (bf16[8,64,128]{2,1,0:T(8,128)(2,1)S(1)}, bf16[8,64,128]{2,1,0:T(8,128)(2,1)S(1)}, u32[]{:S(2)}, u32[]{:S(2)}) collective-permute-start(bf16[8,64,128]{2,1,0:T(8,128)(2,1)S(1)} %get-tuple-element.338.refs_0_), channel_id=1, source_target_pairs={{0,64},{16,80},{32,96},{48,112},{64,0},{80,16},{96,32},{112,48},{1... | collective-permute-start | bytes 393224 | tf_op jit(solution)/shard_map/ppermute | solution.py:418
  100.6 2.2 %collective-permute-start.16 = (bf16[8,64,128]{2,1,0:T(8,128)(2,1)S(1)}, bf16[8,64,128]{2,1,0:T(8,128)(2,1)S(1)}, u32[]{:S(2)}, u32[]{:S(2)}) collective-permute-start(bf16[8,64,128]{2,1,0:T(8,128)(2,1)S(1)} %get-tuple-element.338.refs_0_), channel_id=1, source_target_pairs={{0,96},{16,112},{32,0},{48,16},{64,32},{80,48},{96,64},{112,80},{1... | collective-permute-start | bytes 393224 | tf_op jit(solution)/shard_map/ppermute | solution.py:418
  104.0 2.4 %collective-permute-done.15.refs_2_ = bf16[8,64,128]{2,1,0:T(8,128)(2,1)S(1)} collective-permute-done((bf16[8,64,128]{2,1,0:T(8,128)(2,1)S(1)}, bf16[8,64,128]{2,1,0:T(8,128)(2,1)S(1)}, u32[]{:S(2)}, u32[]{:S(2)}) %collective-permute-start.15) | collective-permute-done | bytes 131104 | tf_op jit(solution)/shard_map/ppermute | solution.py:418
  109.3 3.3 %products.8 = (bf16[16,256,128]{2,1,0:T(8,128)(2,1)}, f32[8,64,128]{2,1,0:T(8,128)}) custom-call(s32[128]{0:T(128)S(1)} %get-tuple-element.397.slot_ref, s32[128]{0:T(128)S(1)} %get-tuple-element.396.place_ref, s32[1]{0:T(128)} %bitcast.41.count_ref, bf16[128,128,128]{2,1,0:T(8,128)(2,1)S(1)} %copy-done.4, ...), custom_call_target="tpu_custom_call" | custom-call | tf_op jit(solution)/shard_map/products/pallas_call | solution.py:227
  113.3 6.3 %all-to-all-start.3 = ((bf16[16,256,128]{2,1,0:T(8,128)(2,1)}), bf16[16,256,128]{2,1,0:T(8,128)(2,1)S(1)}, u32[]{:S(2)}, u32[]{:S(2)}) async-start(bf16[16,256,128]{2,1,0:T(8,128)(2,1)} %get-tuple-element.341), calls=%async_computation.3 | async-start | bytes 2097152 | tf_op jit(solution)/shard_map/all_to_all | solution.py:439
  121.2 2.4 %collective-permute-start.36 = (bf16[8,64,128]{2,1,0:T(8,128)(2,1)S(1)}, bf16[8,64,128]{2,1,0:T(8,128)(2,1)S(1)}, u32[]{:S(2)}, u32[]{:S(2)}) collective-permute-start(bf16[8,64,128]{2,1,0:T(8,128)(2,1)S(1)} %get-tuple-element.351.refs_0_), channel_id=1, source_target_pairs={{0,64},{16,80},{32,96},{48,112},{64,0},{80,16},{96,32},{112,48},{1... | collective-permute-start | bytes 393224 | tf_op jit(solution)/shard_map/ppermute | solution.py:418
  126.7 2.4 %collective-permute-done.36.refs_2_ = bf16[8,64,128]{2,1,0:T(8,128)(2,1)S(1)} collective-permute-done((bf16[8,64,128]{2,1,0:T(8,128)(2,1)S(1)}, bf16[8,64,128]{2,1,0:T(8,128)(2,1)S(1)}, u32[]{:S(2)}, u32[]{:S(2)}) %collective-permute-start.36) | collective-permute-done | bytes 131104 | tf_op jit(solution)/shard_map/ppermute | solution.py:418
  131.9 3.3 %products.11 = (bf16[16,256,128]{2,1,0:T(8,128)(2,1)}, f32[8,64,128]{2,1,0:T(8,128)}) custom-call(s32[128]{0:T(128)S(1)} %get-tuple-element.397.slot_ref, s32[128]{0:T(128)S(1)} %get-tuple-element.396.place_ref, s32[1]{0:T(128)} %bitcast.44.count_ref, bf16[128,128,128]{2,1,0:T(8,128)(2,1)S(1)} %copy-done.5, ...), custom_call_target="tpu_custom_call" | custom-call | tf_op jit(solution)/shard_map/products/pallas_call | solution.py:227
  135.9 6.3 %all-to-all-start.7 = ((bf16[16,256,128]{2,1,0:T(8,128)(2,1)}), bf16[16,256,128]{2,1,0:T(8,128)(2,1)S(1)}, u32[]{:S(2)}, u32[]{:S(2)}) async-start(bf16[16,256,128]{2,1,0:T(8,128)(2,1)} %get-tuple-element.354), calls=%async_computation.7 | async-start | bytes 2097152 | tf_op jit(solution)/shard_map/all_to_all | solution.py:439
  143.8 2.5 %collective-permute-start.22 = (bf16[8,64,128]{2,1,0:T(8,128)(2,1)S(1)}, bf16[8,64,128]{2,1,0:T(8,128)(2,1)S(1)}, u32[]{:S(2)}, u32[]{:S(2)}) collective-permute-start(bf16[8,64,128]{2,1,0:T(8,128)(2,1)S(1)} %get-tuple-element.342.refs_0_), channel_id=1, source_target_pairs={{0,64},{16,80},{32,96},{48,112},{64,0},{80,16},{96,32},{112,48},{1... | collective-permute-start | bytes 393224 | tf_op jit(solution)/shard_map/ppermute | solution.py:418
  146.3 2.2 %collective-permute-start.23 = (bf16[8,64,128]{2,1,0:T(8,128)(2,1)S(1)}, bf16[8,64,128]{2,1,0:T(8,128)(2,1)S(1)}, u32[]{:S(2)}, u32[]{:S(2)}) collective-permute-start(bf16[8,64,128]{2,1,0:T(8,128)(2,1)S(1)} %get-tuple-element.342.refs_0_), channel_id=1, source_target_pairs={{0,96},{16,112},{32,0},{48,16},{64,32},{80,48},{96,64},{112,80},{1... | collective-permute-start | bytes 393224 | tf_op jit(solution)/shard_map/ppermute | solution.py:418
  149.0 2.7 %collective-permute-done.22.refs_2_ = bf16[8,64,128]{2,1,0:T(8,128)(2,1)S(1)} collective-permute-done((bf16[8,64,128]{2,1,0:T(8,128)(2,1)S(1)}, bf16[8,64,128]{2,1,0:T(8,128)(2,1)S(1)}, u32[]{:S(2)}, u32[]{:S(2)}) %collective-permute-start.22) | collective-permute-done | bytes 131104 | tf_op jit(solution)/shard_map/ppermute | solution.py:418
  154.5 3.3 %products.9 = (bf16[16,256,128]{2,1,0:T(8,128)(2,1)}, f32[8,64,128]{2,1,0:T(8,128)}) custom-call(s32[128]{0:T(128)S(1)} %get-tuple-element.397.slot_ref, s32[128]{0:T(128)S(1)} %get-tuple-element.396.place_ref, s32[1]{0:T(128)} %bitcast.42.count_ref, bf16[128,128,128]{2,1,0:T(8,128)(2,1)S(1)} %copy-done.6, ...), custom_call_target="tpu_custom_call" | custom-call | tf_op jit(solution)/shard_map/products/pallas_call | solution.py:227
  158.5 6.4 %all-to-all-start.4 = ((bf16[16,256,128]{2,1,0:T(8,128)(2,1)}), bf16[16,256,128]{2,1,0:T(8,128)(2,1)S(1)}, u32[]{:S(2)}, u32[]{:S(2)}) async-start(bf16[16,256,128]{2,1,0:T(8,128)(2,1)} %get-tuple-element.345), calls=%async_computation.4 | async-start | bytes 2097152 | tf_op jit(solution)/shard_map/all_to_all | solution.py:439
  165.8 15.3 %all-to-all-done.4.got_ref = bf16[16,256,128]{2,1,0:T(8,128)(2,1)S(1)} async-done(((bf16[16,256,128]{2,1,0:T(8,128)(2,1)}), bf16[16,256,128]{2,1,0:T(8,128)(2,1)S(1)}, u32[]{:S(2)}, u32[]{:S(2)}) %all-to-all-start.4) | async-done | bytes 1048608 | tf_op jit(solution)/shard_map/all_to_all | solution.py:439
  (134 shorter events, 46.6 us)
Async XLA Ops:
  14.2 18.0 %all-to-all-start.1 = ((bf16[16,112,128]{2,1,0:T(8,128)(2,1)}), bf16[16,112,128]{2,1,0:T(8,128)(2,1)S(1)}, u32[]{:S(2)}, u32[]{:S(2)}) async-start(bf16[16,112,128]{2,1,0:T(8,128)(2,1)} %first_products.7), calls=%async_computation.1 | async-start | bytes 917504 | tf_op jit(solution)/shard_map/all_to_all | solution.py:439
  33.6 5.8 %collective-permute-start = (bf16[8,64,128]{2,1,0:T(8,128)(2,1)S(1)}, bf16[8,64,128]{2,1,0:T(8,128)(2,1)S(1)}, u32[]{:S(2)}, u32[]{:S(2)}) collective-permute-start(bf16[8,64,128]{2,1,0:T(8,128)(2,1)S(1)} %rounded.2.refs_0_), channel_id=1, source_target_pairs={{0,32},{16,48},{32,64},{48,80},{64,96},{80,112},{96,0},{112,16},{1... | collective-permute-start | bytes 393224 | tf_op jit(solution)/shard_map/ppermute | solution.py:418
  35.6 6.6 %collective-permute-start.1 = (bf16[8,64,128]{2,1,0:T(8,128)(2,1)S(1)}, bf16[8,64,128]{2,1,0:T(8,128)(2,1)S(1)}, u32[]{:S(2)}, u32[]{:S(2)}) collective-permute-start(bf16[8,64,128]{2,1,0:T(8,128)(2,1)S(1)} %rounded.2.refs_0_), channel_id=1, source_target_pairs={{0,64},{16,80},{32,96},{48,112},{64,0},{80,16},{96,32},{112,48},{1... | collective-permute-start | bytes 393224 | tf_op jit(solution)/shard_map/ppermute | solution.py:418
  35.8 6.8 %collective-permute-start.2 = (bf16[8,64,128]{2,1,0:T(8,128)(2,1)S(1)}, bf16[8,64,128]{2,1,0:T(8,128)(2,1)S(1)}, u32[]{:S(2)}, u32[]{:S(2)}) collective-permute-start(bf16[8,64,128]{2,1,0:T(8,128)(2,1)S(1)} %rounded.2.refs_0_), channel_id=1, source_target_pairs={{0,96},{16,112},{32,0},{48,16},{64,32},{80,48},{96,64},{112,80},{1... | collective-permute-start | bytes 393224 | tf_op jit(solution)/shard_map/ppermute | solution.py:418
  38.2 4.6 %collective-permute-start.3 = (bf16[8,64,128]{2,1,0:T(8,128)(2,1)S(1)}, bf16[8,64,128]{2,1,0:T(8,128)(2,1)S(1)}, u32[]{:S(2)}, u32[]{:S(2)}) collective-permute-start(bf16[8,64,128]{2,1,0:T(8,128)(2,1)S(1)} %rounded.2.refs_0_), channel_id=1, source_target_pairs={{0,16},{16,0},{32,48},{48,32},{64,80},{80,64},{96,112},{112,96},{1... | collective-permute-start | bytes 393224 | tf_op jit(solution)/shard_map/ppermute | solution.py:419
  47.2 20.6 %all-to-all-start.5 = ((bf16[16,256,128]{2,1,0:T(8,128)(2,1)}), bf16[16,256,128]{2,1,0:T(8,128)(2,1)S(1)}, u32[]{:S(2)}, u32[]{:S(2)}) async-start(bf16[16,256,128]{2,1,0:T(8,128)(2,1)} %get-tuple-element.335), calls=%async_computation.5 | async-start | bytes 2097152 | tf_op jit(solution)/shard_map/all_to_all | solution.py:439
  51.7 5.5 %collective-permute-start.7 = (bf16[8,64,128]{2,1,0:T(8,128)(2,1)S(1)}, bf16[8,64,128]{2,1,0:T(8,128)(2,1)S(1)}, u32[]{:S(2)}, u32[]{:S(2)}) collective-permute-start(bf16[8,64,128]{2,1,0:T(8,128)(2,1)S(1)} %rounded.3.refs_0_), channel_id=1, source_target_pairs={{0,32},{16,48},{32,64},{48,80},{64,96},{80,112},{96,0},{112,16},{1... | collective-permute-start | bytes 393224 | tf_op jit(solution)/shard_map/ppermute | solution.py:418
  53.4 7.9 %collective-permute-start.8 = (bf16[8,64,128]{2,1,0:T(8,128)(2,1)S(1)}, bf16[8,64,128]{2,1,0:T(8,128)(2,1)S(1)}, u32[]{:S(2)}, u32[]{:S(2)}) collective-permute-start(bf16[8,64,128]{2,1,0:T(8,128)(2,1)S(1)} %rounded.3.refs_0_), channel_id=1, source_target_pairs={{0,64},{16,80},{32,96},{48,112},{64,0},{80,16},{96,32},{112,48},{1... | collective-permute-start | bytes 393224 | tf_op jit(solution)/shard_map/ppermute | solution.py:418
  54.2 7.8 %collective-permute-start.9 = (bf16[8,64,128]{2,1,0:T(8,128)(2,1)S(1)}, bf16[8,64,128]{2,1,0:T(8,128)(2,1)S(1)}, u32[]{:S(2)}, u32[]{:S(2)}) collective-permute-start(bf16[8,64,128]{2,1,0:T(8,128)(2,1)S(1)} %rounded.3.refs_0_), channel_id=1, source_target_pairs={{0,96},{16,112},{32,0},{48,16},{64,32},{80,48},{96,64},{112,80},{1... | collective-permute-start | bytes 393224 | tf_op jit(solution)/shard_map/ppermute | solution.py:418
  56.8 5.3 %collective-permute-start.10 = (bf16[8,64,128]{2,1,0:T(8,128)(2,1)S(1)}, bf16[8,64,128]{2,1,0:T(8,128)(2,1)S(1)}, u32[]{:S(2)}, u32[]{:S(2)}) collective-permute-start(bf16[8,64,128]{2,1,0:T(8,128)(2,1)S(1)} %rounded.3.refs_0_), channel_id=1, source_target_pairs={{0,16},{16,0},{32,48},{48,32},{64,80},{80,64},{96,112},{112,96},{1... | collective-permute-start | bytes 393224 | tf_op jit(solution)/shard_map/ppermute | solution.py:419
  57.2 4.8 %collective-permute-start.11 = (bf16[8,64,128]{2,1,0:T(8,128)(2,1)S(1)}, bf16[8,64,128]{2,1,0:T(8,128)(2,1)S(1)}, u32[]{:S(2)}, u32[]{:S(2)}) collective-permute-start(bf16[8,64,128]{2,1,0:T(8,128)(2,1)S(1)} %collective-permute-done.7.refs_1_), channel_id=1, source_target_pairs={{0,16},{16,0},{32,48},{48,32},{64,80},{80,64},{96,112},{112,96},{1... | collective-permute-start | bytes 393224 | tf_op jit(solution)/shard_map/ppermute | solution.py:419
  67.9 22.1 %all-to-all-start.2 = ((bf16[16,256,128]{2,1,0:T(8,128)(2,1)}), bf16[16,256,128]{2,1,0:T(8,128)(2,1)S(1)}, u32[]{:S(2)}, u32[]{:S(2)}) async-start(bf16[16,256,128]{2,1,0:T(8,128)(2,1)} %get-tuple-element.337), calls=%async_computation.2 | async-start | bytes 2097152 | tf_op jit(solution)/shard_map/all_to_all | solution.py:439
  74.7 6.3 %collective-permute-start.28 = (bf16[8,64,128]{2,1,0:T(8,128)(2,1)S(1)}, bf16[8,64,128]{2,1,0:T(8,128)(2,1)S(1)}, u32[]{:S(2)}, u32[]{:S(2)}) collective-permute-start(bf16[8,64,128]{2,1,0:T(8,128)(2,1)S(1)} %get-tuple-element.347.refs_0_), channel_id=1, source_target_pairs={{0,32},{16,48},{32,64},{48,80},{64,96},{80,112},{96,0},{112,16},{1... | collective-permute-start | bytes 393224 | tf_op jit(solution)/shard_map/ppermute | solution.py:418
  76.0 7.9 %collective-permute-start.29 = (bf16[8,64,128]{2,1,0:T(8,128)(2,1)S(1)}, bf16[8,64,128]{2,1,0:T(8,128)(2,1)S(1)}, u32[]{:S(2)}, u32[]{:S(2)}) collective-permute-start(bf16[8,64,128]{2,1,0:T(8,128)(2,1)S(1)} %get-tuple-element.347.refs_0_), channel_id=1, source_target_pairs={{0,64},{16,80},{32,96},{48,112},{64,0},{80,16},{96,32},{112,48},{1... | collective-permute-start | bytes 393224 | tf_op jit(solution)/shard_map/ppermute | solution.py:418
  77.9 7.5 %collective-permute-start.30 = (bf16[8,64,128]{2,1,0:T(8,128)(2,1)S(1)}, bf16[8,64,128]{2,1,0:T(8,128)(2,1)S(1)}, u32[]{:S(2)}, u32[]{:S(2)}) collective-permute-start(bf16[8,64,128]{2,1,0:T(8,128)(2,1)S(1)} %get-tuple-element.347.refs_0_), channel_id=1, source_target_pairs={{0,96},{16,112},{32,0},{48,16},{64,32},{80,48},{96,64},{112,80},{1... | collective-permute-start | bytes 393224 | tf_op jit(solution)/shard_map/ppermute | solution.py:418
  79.3 6.1 %collective-permute-start.31 = (bf16[8,64,128]{2,1,0:T(8,128)(2,1)S(1)}, bf16[8,64,128]{2,1,0:T(8,128)(2,1)S(1)}, u32[]{:S(2)}, u32[]{:S(2)}) collective-permute-start(bf16[8,64,128]{2,1,0:T(8,128)(2,1)S(1)} %get-tuple-element.347.refs_0_), channel_id=1, source_target_pairs={{0,16},{16,0},{32,48},{48,32},{64,80},{80,64},{96,112},{112,96},{1... | collective-permute-start | bytes 393224 | tf_op jit(solution)/shard_map/ppermute | solution.py:419
  90.0 23.3 %all-to-all-start.6 = ((bf16[16,256,128]{2,1,0:T(8,128)(2,1)}), bf16[16,256,128]{2,1,0:T(8,128)(2,1)S(1)}, u32[]{:S(2)}, u32[]{:S(2)}) async-start(bf16[16,256,128]{2,1,0:T(8,128)(2,1)} %get-tuple-element.350), calls=%async_computation.6 | async-start | bytes 2097152 | tf_op jit(solution)/shard_map/all_to_all | solution.py:439
  98.1 6.0 %collective-permute-start.14 = (bf16[8,64,128]{2,1,0:T(8,128)(2,1)S(1)}, bf16[8,64,128]{2,1,0:T(8,128)(2,1)S(1)}, u32[]{:S(2)}, u32[]{:S(2)}) collective-permute-start(bf16[8,64,128]{2,1,0:T(8,128)(2,1)S(1)} %get-tuple-element.338.refs_0_), channel_id=1, source_target_pairs={{0,32},{16,48},{32,64},{48,80},{64,96},{80,112},{96,0},{112,16},{1... | collective-permute-start | bytes 393224 | tf_op jit(solution)/shard_map/ppermute | solution.py:418
  98.6 7.9 %collective-permute-start.15 = (bf16[8,64,128]{2,1,0:T(8,128)(2,1)S(1)}, bf16[8,64,128]{2,1,0:T(8,128)(2,1)S(1)}, u32[]{:S(2)}, u32[]{:S(2)}) collective-permute-start(bf16[8,64,128]{2,1,0:T(8,128)(2,1)S(1)} %get-tuple-element.338.refs_0_), channel_id=1, source_target_pairs={{0,64},{16,80},{32,96},{48,112},{64,0},{80,16},{96,32},{112,48},{1... | collective-permute-start | bytes 393224 | tf_op jit(solution)/shard_map/ppermute | solution.py:418
  100.6 7.4 %collective-permute-start.16 = (bf16[8,64,128]{2,1,0:T(8,128)(2,1)S(1)}, bf16[8,64,128]{2,1,0:T(8,128)(2,1)S(1)}, u32[]{:S(2)}, u32[]{:S(2)}) collective-permute-start(bf16[8,64,128]{2,1,0:T(8,128)(2,1)S(1)} %get-tuple-element.338.refs_0_), channel_id=1, source_target_pairs={{0,96},{16,112},{32,0},{48,16},{64,32},{80,48},{96,64},{112,80},{1... | collective-permute-start | bytes 393224 | tf_op jit(solution)/shard_map/ppermute | solution.py:418
  102.7 5.3 %collective-permute-start.17 = (bf16[8,64,128]{2,1,0:T(8,128)(2,1)S(1)}, bf16[8,64,128]{2,1,0:T(8,128)(2,1)S(1)}, u32[]{:S(2)}, u32[]{:S(2)}) collective-permute-start(bf16[8,64,128]{2,1,0:T(8,128)(2,1)S(1)} %get-tuple-element.338.refs_0_), channel_id=1, source_target_pairs={{0,16},{16,0},{32,48},{48,32},{64,80},{80,64},{96,112},{112,96},{1... | collective-permute-start | bytes 393224 | tf_op jit(solution)/shard_map/ppermute | solution.py:419
  113.3 22.6 %all-to-all-start.3 = ((bf16[16,256,128]{2,1,0:T(8,128)(2,1)}), bf16[16,256,128]{2,1,0:T(8,128)(2,1)S(1)}, u32[]{:S(2)}, u32[]{:S(2)}) async-start(bf16[16,256,128]{2,1,0:T(8,128)(2,1)} %get-tuple-element.341), calls=%async_computation.3 | async-start | bytes 2097152 | tf_op jit(solution)/shard_map/all_to_all | solution.py:439
  120.6 6.0 %collective-permute-start.35 = (bf16[8,64,128]{2,1,0:T(8,128)(2,1)S(1)}, bf16[8,64,128]{2,1,0:T(8,128)(2,1)S(1)}, u32[]{:S(2)}, u32[]{:S(2)}) collective-permute-start(bf16[8,64,128]{2,1,0:T(8,128)(2,1)S(1)} %get-tuple-element.351.refs_0_), channel_id=1, source_target_pairs={{0,32},{16,48},{32,64},{48,80},{64,96},{80,112},{96,0},{112,16},{1... | collective-permute-start | bytes 393224 | tf_op jit(solution)/shard_map/ppermute | solution.py:418
  121.2 7.9 %collective-permute-start.36 = (bf16[8,64,128]{2,1,0:T(8,128)(2,1)S(1)}, bf16[8,64,128]{2,1,0:T(8,128)(2,1)S(1)}, u32[]{:S(2)}, u32[]{:S(2)}) collective-permute-start(bf16[8,64,128]{2,1,0:T(8,128)(2,1)S(1)} %get-tuple-element.351.refs_0_), channel_id=1, source_target_pairs={{0,64},{16,80},{32,96},{48,112},{64,0},{80,16},{96,32},{112,48},{1... | collective-permute-start | bytes 393224 | tf_op jit(solution)/shard_map/ppermute | solution.py:418
  123.6 7.0 %collective-permute-start.37 = (bf16[8,64,128]{2,1,0:T(8,128)(2,1)S(1)}, bf16[8,64,128]{2,1,0:T(8,128)(2,1)S(1)}, u32[]{:S(2)}, u32[]{:S(2)}) collective-permute-start(bf16[8,64,128]{2,1,0:T(8,128)(2,1)S(1)} %get-tuple-element.351.refs_0_), channel_id=1, source_target_pairs={{0,96},{16,112},{32,0},{48,16},{64,32},{80,48},{96,64},{112,80},{1... | collective-permute-start | bytes 393224 | tf_op jit(solution)/shard_map/ppermute | solution.py:418
  125.2 5.3 %collective-permute-start.38 = (bf16[8,64,128]{2,1,0:T(8,128)(2,1)S(1)}, bf16[8,64,128]{2,1,0:T(8,128)(2,1)S(1)}, u32[]{:S(2)}, u32[]{:S(2)}) collective-permute-start(bf16[8,64,128]{2,1,0:T(8,128)(2,1)S(1)} %get-tuple-element.351.refs_0_), channel_id=1, source_target_pairs={{0,16},{16,0},{32,48},{48,32},{64,80},{80,64},{96,112},{112,96},{1... | collective-permute-start | bytes 393224 | tf_op jit(solution)/shard_map/ppermute | solution.py:419
  135.9 22.6 %all-to-all-start.7 = ((bf16[16,256,128]{2,1,0:T(8,128)(2,1)}), bf16[16,256,128]{2,1,0:T(8,128)(2,1)S(1)}, u32[]{:S(2)}, u32[]{:S(2)}) async-start(bf16[16,256,128]{2,1,0:T(8,128)(2,1)} %get-tuple-element.354), calls=%async_computation.7 | async-start | bytes 2097152 | tf_op jit(solution)/shard_map/all_to_all | solution.py:439
  143.2 5.4 %collective-permute-start.21 = (bf16[8,64,128]{2,1,0:T(8,128)(2,1)S(1)}, bf16[8,64,128]{2,1,0:T(8,128)(2,1)S(1)}, u32[]{:S(2)}, u32[]{:S(2)}) collective-permute-start(bf16[8,64,128]{2,1,0:T(8,128)(2,1)S(1)} %get-tuple-element.342.refs_0_), channel_id=1, source_target_pairs={{0,32},{16,48},{32,64},{48,80},{64,96},{80,112},{96,0},{112,16},{1... | collective-permute-start | bytes 393224 | tf_op jit(solution)/shard_map/ppermute | solution.py:418
  143.8 7.9 %collective-permute-start.22 = (bf16[8,64,128]{2,1,0:T(8,128)(2,1)S(1)}, bf16[8,64,128]{2,1,0:T(8,128)(2,1)S(1)}, u32[]{:S(2)}, u32[]{:S(2)}) collective-permute-start(bf16[8,64,128]{2,1,0:T(8,128)(2,1)S(1)} %get-tuple-element.342.refs_0_), channel_id=1, source_target_pairs={{0,64},{16,80},{32,96},{48,112},{64,0},{80,16},{96,32},{112,48},{1... | collective-permute-start | bytes 393224 | tf_op jit(solution)/shard_map/ppermute | solution.py:418
  146.3 6.9 %collective-permute-start.23 = (bf16[8,64,128]{2,1,0:T(8,128)(2,1)S(1)}, bf16[8,64,128]{2,1,0:T(8,128)(2,1)S(1)}, u32[]{:S(2)}, u32[]{:S(2)}) collective-permute-start(bf16[8,64,128]{2,1,0:T(8,128)(2,1)S(1)} %get-tuple-element.342.refs_0_), channel_id=1, source_target_pairs={{0,96},{16,112},{32,0},{48,16},{64,32},{80,48},{96,64},{112,80},{1... | collective-permute-start | bytes 393224 | tf_op jit(solution)/shard_map/ppermute | solution.py:418
  148.5 4.7 %collective-permute-start.24 = (bf16[8,64,128]{2,1,0:T(8,128)(2,1)S(1)}, bf16[8,64,128]{2,1,0:T(8,128)(2,1)S(1)}, u32[]{:S(2)}, u32[]{:S(2)}) collective-permute-start(bf16[8,64,128]{2,1,0:T(8,128)(2,1)S(1)} %get-tuple-element.342.refs_0_), channel_id=1, source_target_pairs={{0,16},{16,0},{32,48},{48,32},{64,80},{80,64},{96,112},{112,96},{1... | collective-permute-start | bytes 393224 | tf_op jit(solution)/shard_map/ppermute | solution.py:419
  158.5 22.6 %all-to-all-start.4 = ((bf16[16,256,128]{2,1,0:T(8,128)(2,1)}), bf16[16,256,128]{2,1,0:T(8,128)(2,1)S(1)}, u32[]{:S(2)}, u32[]{:S(2)}) async-start(bf16[16,256,128]{2,1,0:T(8,128)(2,1)} %get-tuple-element.345), calls=%async_computation.4 | async-start | bytes 2097152 | tf_op jit(solution)/shard_map/all_to_all | solution.py:439
  (30 other events, 170.6 us)

commit v6 on v5

--- a/solution.py
+++ b/solution.py
@@ -16,7 +16,7 @@
 PLACES = 24
 ID_ROWS = 16
 UNROLL = 16
-FIRST_UNROLL = 8
+FIRST_UNROLL = 16
 CHUNK = 64
 VMEM_LIMIT = 14 * 1024 * 1024
 
@@ -75,7 +75,7 @@
         acc_ref, x_ref, tile_ref, id_rows_ref, asked_ref, has_ref, list_ref, mark_ref, slot_ref, id_ref, sems = scratch
         live, mine, first = info_ref[0], info_ref[1], info_ref[2] * PLACES
 
-        def repeat(times, step, start=0, unroll=8):
+        def repeat(times, step, start=0, unroll=32):
             return lax.fori_loop(0, times, step, start, unroll=unroll)
 
         def clear(ref, value):
@@ -83,7 +83,7 @@
                 ref[index] = value
                 return carry
 
-            repeat(ref.shape[0], step)
+            repeat(ref.shape[0], step, unroll=8)
 
         def copy(index, lane):
             return pltpu.make_async_copy(tiles_ref.at[index], tile_ref.at[lane], sems.at[lane])

time: 187 us -> 187 us (level)
  transfers between devices with their start and end apart: 49 -> 49, of which waited for: 32 -> 33; matrix products, arithmetic and copies ran while one was open for 0% -> 0% of each run, Pallas kernels for 11% -> 11%
where the time goes in v6:
time: 187 us; the launch traced here: 184 us
  starting transfers between devices  72.6 us (39%)
  waiting for transfers between devices  68.4 us (37%)
  Pallas kernels  35 us (19%)
  local copies, waits for them, and re-layouts  3.72 us (2%)
  between operations  3.06 us (2%)
    all_to_all x7, starting transfers between devices, exchange(): lax.all_to_all(sent, 'col', split_axis=0, concat_axis=0, tiled=True, axis...  43.9 us
    ppermute x18, waiting for transfers between devices, column_parts(): lax.ppermute(mine, 'row', row_shift(dz, 0))  31.6 us
    all_to_all x7, waiting for transfers between devices, exchange(): lax.all_to_all(sent, 'col', split_axis=0, concat_axis=0, tiled=True, axis...  28.9 us
    ppermute x18, starting transfers between devices, column_parts(): lax.ppermute(mine, 'row', row_shift(dz, 0))  28.5 us
    pallas_call x6, Pallas kernels, products(): pl.pallas_call(body, out_shape=(jax.ShapeDtypeStruct((owners, rows, tile)...  19.4 us
    ppermute x24, waiting for transfers between devices, column_parts(): other = [lax.ppermute(part, 'row', row_shift(0, 1)) for part in same]  7.93 us
    pallas_call x1, Pallas kernels, first_products(): pl.pallas_call(body, out_shape=jax.ShapeDtypeStruct((n_col, sent_rows + I...  4.91 us
    pallas_call x4, Pallas kernels, owned_sum(): pl.pallas_call(body, out_shape=(jax.ShapeDtypeStruct((BPD, width, tile),...  3.87 us
  transfers between devices with their start and end apart: 49, of which 33 were waited for; matrix products, arithmetic and copies ran while one was open for 0% of the time, Pallas kernels for 11%

profile of v6, /device:TPU:32, one launch (start us, length us, event | category | flops | bytes accessed | tf_op | source)
XLA Modules:
  0.0 184.2 jit_solution(8565143989246209443)
XLA Ops:
  0.8 4.9 %first_products.7 = bf16[16,112,128]{2,1,0:T(8,128)(2,1)} custom-call(s32[3]{0:T(128)S(1)} %pad_add_fusion.1.info_ref, s32[128]{0:T(128)} %bitcast.52, s32[128]{0:T(128)} %bitcast.50, s32[128]{0:T(128)} %query_ref.1, bf16[128,128,128]{2,1,0:T(8,128)(2,1)} %bitcast.47), custom_call_target="tpu_custom_call" | custom-call | tf_op jit(solution)/shard_map/first_products/pallas_call | solution.py:177
  9.0 2.9 %turned.1.tiles_ref = bf16[128,128,128]{2,1,0:T(8,128)(2,1)S(1)} custom-call(s32[1]{0:T(128)} %bitcast.38.count_ref, bf16[128,128,128]{2,1,0:T(8,128)(2,1)} %bitcast.48), custom_call_target="tpu_custom_call" | custom-call | tf_op jit(solution)/shard_map/turned/pallas_call | solution.py:264
  12.0 2.0 %copy-done = bf16[128,128,128]{2,1,0:T(8,128)(2,1)} copy-done((bf16[128,128,128]{2,1,0:T(8,128)(2,1)}, bf16[128,128,128]{2,1,0:T(8,128)(2,1)S(1)}, u32[]{:S(2)}) %copy-start) | copy-done | bytes 4194328
  14.0 7.8 %all-to-all-start.1 = ((bf16[16,112,128]{2,1,0:T(8,128)(2,1)}), bf16[16,112,128]{2,1,0:T(8,128)(2,1)S(1)}, u32[]{:S(2)}, u32[]{:S(2)}) async-start(bf16[16,112,128]{2,1,0:T(8,128)(2,1)} %first_products.7), calls=%async_computation.1 | async-start | bytes 917504 | tf_op jit(solution)/shard_map/all_to_all | solution.py:439
  21.9 10.1 %all-to-all-done.1.got_ref = bf16[16,112,128]{2,1,0:T(8,128)(2,1)S(1)} async-done(((bf16[16,112,128]{2,1,0:T(8,128)(2,1)}), bf16[16,112,128]{2,1,0:T(8,128)(2,1)S(1)}, u32[]{:S(2)}, u32[]{:S(2)}) %all-to-all-start.1) | async-done | bytes 458784 | tf_op jit(solution)/shard_map/all_to_all | solution.py:439
  33.3 2.3 %collective-permute-start = (bf16[8,64,128]{2,1,0:T(8,128)(2,1)S(1)}, bf16[8,64,128]{2,1,0:T(8,128)(2,1)S(1)}, u32[]{:S(2)}, u32[]{:S(2)}) collective-permute-start(bf16[8,64,128]{2,1,0:T(8,128)(2,1)S(1)} %rounded.2.refs_0_), channel_id=1, source_target_pairs={{0,32},{16,48},{32,64},{48,80},{64,96},{80,112},{96,0},{112,16},{1... | collective-permute-start | bytes 393224 | tf_op jit(solution)/shard_map/ppermute | solution.py:418
  35.8 2.2 %collective-permute-start.2 = (bf16[8,64,128]{2,1,0:T(8,128)(2,1)S(1)}, bf16[8,64,128]{2,1,0:T(8,128)(2,1)S(1)}, u32[]{:S(2)}, u32[]{:S(2)}) collective-permute-start(bf16[8,64,128]{2,1,0:T(8,128)(2,1)S(1)} %rounded.2.refs_0_), channel_id=1, source_target_pairs={{0,96},{16,112},{32,0},{48,16},{64,32},{80,48},{96,64},{112,80},{1... | collective-permute-start | bytes 393224 | tf_op jit(solution)/shard_map/ppermute | solution.py:418
  37.9 2.3 %collective-permute-done.refs_1_ = bf16[8,64,128]{2,1,0:T(8,128)(2,1)S(1)} collective-permute-done((bf16[8,64,128]{2,1,0:T(8,128)(2,1)S(1)}, bf16[8,64,128]{2,1,0:T(8,128)(2,1)S(1)}, u32[]{:S(2)}, u32[]{:S(2)}) %collective-permute-start) | collective-permute-done | bytes 131104 | tf_op jit(solution)/shard_map/ppermute | solution.py:418
  40.2 2.0 %collective-permute-done.1.refs_2_ = bf16[8,64,128]{2,1,0:T(8,128)(2,1)S(1)} collective-permute-done((bf16[8,64,128]{2,1,0:T(8,128)(2,1)S(1)}, bf16[8,64,128]{2,1,0:T(8,128)(2,1)S(1)}, u32[]{:S(2)}, u32[]{:S(2)}) %collective-permute-start.1) | collective-permute-done | bytes 131104 | tf_op jit(solution)/shard_map/ppermute | solution.py:418
  44.5 3.2 %products.6 = (bf16[16,256,128]{2,1,0:T(8,128)(2,1)}, f32[8,64,128]{2,1,0:T(8,128)}) custom-call(s32[128]{0:T(128)S(1)} %get-tuple-element.397.slot_ref, s32[128]{0:T(128)S(1)} %get-tuple-element.396.place_ref, s32[1]{0:T(128)} %bitcast.39.count_ref, bf16[128,128,128]{2,1,0:T(8,128)(2,1)S(1)} %copy-done.1, bf16[8,64,128]{2,1,0:T(8,128)(2,1)S(1)} %rounded.2.refs_0_, ...), custom_call_target="tpu_custom_call" | custom-call | tf_op jit(solution)/shard_map/products/pallas_call | solution.py:227
  47.7 4.4 %all-to-all-start.5 = ((bf16[16,256,128]{2,1,0:T(8,128)(2,1)}), bf16[16,256,128]{2,1,0:T(8,128)(2,1)S(1)}, u32[]{:S(2)}, u32[]{:S(2)}) async-start(bf16[16,256,128]{2,1,0:T(8,128)(2,1)} %get-tuple-element.335), calls=%async_computation.5 | async-start | bytes 2097152 | tf_op jit(solution)/shard_map/all_to_all | solution.py:439
  54.6 2.2 %collective-permute-start.9 = (bf16[8,64,128]{2,1,0:T(8,128)(2,1)S(1)}, bf16[8,64,128]{2,1,0:T(8,128)(2,1)S(1)}, u32[]{:S(2)}, u32[]{:S(2)}) collective-permute-start(bf16[8,64,128]{2,1,0:T(8,128)(2,1)S(1)} %rounded.3.refs_0_), channel_id=1, source_target_pairs={{0,96},{16,112},{32,0},{48,16},{64,32},{80,48},{96,64},{112,80},{1... | collective-permute-start | bytes 393224 | tf_op jit(solution)/shard_map/ppermute | solution.py:418
  58.0 3.3 %collective-permute-done.8.refs_2_ = bf16[8,64,128]{2,1,0:T(8,128)(2,1)S(1)} collective-permute-done((bf16[8,64,128]{2,1,0:T(8,128)(2,1)S(1)}, bf16[8,64,128]{2,1,0:T(8,128)(2,1)S(1)}, u32[]{:S(2)}, u32[]{:S(2)}) %collective-permute-start.8) | collective-permute-done | bytes 131104 | tf_op jit(solution)/shard_map/ppermute | solution.py:418
  63.5 3.2 %products.7 = (bf16[16,256,128]{2,1,0:T(8,128)(2,1)}, f32[8,64,128]{2,1,0:T(8,128)}) custom-call(s32[128]{0:T(128)S(1)} %get-tuple-element.397.slot_ref, s32[128]{0:T(128)S(1)} %get-tuple-element.396.place_ref, s32[1]{0:T(128)} %bitcast.40.count_ref, bf16[128,128,128]{2,1,0:T(8,128)(2,1)S(1)} %copy-done.2, bf16[8,64,128]{2,1,0:T(8,128)(2,1)S(1)} %rounded.3.refs_0_, ...), custom_call_target="tpu_custom_call" | custom-call | tf_op jit(solution)/shard_map/products/pallas_call | solution.py:227
  68.3 5.4 %all-to-all-start.2 = ((bf16[16,256,128]{2,1,0:T(8,128)(2,1)}), bf16[16,256,128]{2,1,0:T(8,128)(2,1)S(1)}, u32[]{:S(2)}, u32[]{:S(2)}) async-start(bf16[16,256,128]{2,1,0:T(8,128)(2,1)} %get-tuple-element.337), calls=%async_computation.2 | async-start | bytes 2097152 | tf_op jit(solution)/shard_map/all_to_all | solution.py:439
  80.6 3.2 %collective-permute-done.29.refs_2_ = bf16[8,64,128]{2,1,0:T(8,128)(2,1)S(1)} collective-permute-done((bf16[8,64,128]{2,1,0:T(8,128)(2,1)S(1)}, bf16[8,64,128]{2,1,0:T(8,128)(2,1)S(1)}, u32[]{:S(2)}, u32[]{:S(2)}) %collective-permute-start.29) | collective-permute-done | bytes 131104 | tf_op jit(solution)/shard_map/ppermute | solution.py:418
  86.7 3.3 %products.10 = (bf16[16,256,128]{2,1,0:T(8,128)(2,1)}, f32[8,64,128]{2,1,0:T(8,128)}) custom-call(s32[128]{0:T(128)S(1)} %get-tuple-element.397.slot_ref, s32[128]{0:T(128)S(1)} %get-tuple-element.396.place_ref, s32[1]{0:T(128)} %bitcast.43.count_ref, bf16[128,128,128]{2,1,0:T(8,128)(2,1)S(1)} %copy-done.3, ...), custom_call_target="tpu_custom_call" | custom-call | tf_op jit(solution)/shard_map/products/pallas_call | solution.py:227
  90.0 7.0 %all-to-all-start.6 = ((bf16[16,256,128]{2,1,0:T(8,128)(2,1)}), bf16[16,256,128]{2,1,0:T(8,128)(2,1)S(1)}, u32[]{:S(2)}, u32[]{:S(2)}) async-start(bf16[16,256,128]{2,1,0:T(8,128)(2,1)} %get-tuple-element.350), calls=%async_computation.6 | async-start | bytes 2097152 | tf_op jit(solution)/shard_map/all_to_all | solution.py:439
  100.4 2.2 %collective-permute-start.16 = (bf16[8,64,128]{2,1,0:T(8,128)(2,1)S(1)}, bf16[8,64,128]{2,1,0:T(8,128)(2,1)S(1)}, u32[]{:S(2)}, u32[]{:S(2)}) collective-permute-start(bf16[8,64,128]{2,1,0:T(8,128)(2,1)S(1)} %get-tuple-element.338.refs_0_), channel_id=1, source_target_pairs={{0,96},{16,112},{32,0},{48,16},{64,32},{80,48},{96,64},{112,80},{1... | collective-permute-start | bytes 393224 | tf_op jit(solution)/shard_map/ppermute | solution.py:418
  104.0 2.3 %collective-permute-done.15.refs_2_ = bf16[8,64,128]{2,1,0:T(8,128)(2,1)S(1)} collective-permute-done((bf16[8,64,128]{2,1,0:T(8,128)(2,1)S(1)}, bf16[8,64,128]{2,1,0:T(8,128)(2,1)S(1)}, u32[]{:S(2)}, u32[]{:S(2)}) %collective-permute-start.15) | collective-permute-done | bytes 131104 | tf_op jit(solution)/shard_map/ppermute | solution.py:418
  109.2 3.3 %products.8 = (bf16[16,256,128]{2,1,0:T(8,128)(2,1)}, f32[8,64,128]{2,1,0:T(8,128)}) custom-call(s32[128]{0:T(128)S(1)} %get-tuple-element.397.slot_ref, s32[128]{0:T(128)S(1)} %get-tuple-element.396.place_ref, s32[1]{0:T(128)} %bitcast.41.count_ref, bf16[128,128,128]{2,1,0:T(8,128)(2,1)S(1)} %copy-done.4, ...), custom_call_target="tpu_custom_call" | custom-call | tf_op jit(solution)/shard_map/products/pallas_call | solution.py:227
  113.2 6.3 %all-to-all-start.3 = ((bf16[16,256,128]{2,1,0:T(8,128)(2,1)}), bf16[16,256,128]{2,1,0:T(8,128)(2,1)S(1)}, u32[]{:S(2)}, u32[]{:S(2)}) async-start(bf16[16,256,128]{2,1,0:T(8,128)(2,1)} %get-tuple-element.341), calls=%async_computation.3 | async-start | bytes 2097152 | tf_op jit(solution)/shard_map/all_to_all | solution.py:439
  121.1 2.3 %collective-permute-start.36 = (bf16[8,64,128]{2,1,0:T(8,128)(2,1)S(1)}, bf16[8,64,128]{2,1,0:T(8,128)(2,1)S(1)}, u32[]{:S(2)}, u32[]{:S(2)}) collective-permute-start(bf16[8,64,128]{2,1,0:T(8,128)(2,1)S(1)} %get-tuple-element.351.refs_0_), channel_id=1, source_target_pairs={{0,64},{16,80},{32,96},{48,112},{64,0},{80,16},{96,32},{112,48},{1... | collective-permute-start | bytes 393224 | tf_op jit(solution)/shard_map/ppermute | solution.py:418
  126.5 2.4 %collective-permute-done.36.refs_2_ = bf16[8,64,128]{2,1,0:T(8,128)(2,1)S(1)} collective-permute-done((bf16[8,64,128]{2,1,0:T(8,128)(2,1)S(1)}, bf16[8,64,128]{2,1,0:T(8,128)(2,1)S(1)}, u32[]{:S(2)}, u32[]{:S(2)}) %collective-permute-start.36) | collective-permute-done | bytes 131104 | tf_op jit(solution)/shard_map/ppermute | solution.py:418
  131.8 3.3 %products.11 = (bf16[16,256,128]{2,1,0:T(8,128)(2,1)}, f32[8,64,128]{2,1,0:T(8,128)}) custom-call(s32[128]{0:T(128)S(1)} %get-tuple-element.397.slot_ref, s32[128]{0:T(128)S(1)} %get-tuple-element.396.place_ref, s32[1]{0:T(128)} %bitcast.44.count_ref, bf16[128,128,128]{2,1,0:T(8,128)(2,1)S(1)} %copy-done.5, ...), custom_call_target="tpu_custom_call" | custom-call | tf_op jit(solution)/shard_map/products/pallas_call | solution.py:227
  135.8 6.3 %all-to-all-start.7 = ((bf16[16,256,128]{2,1,0:T(8,128)(2,1)}), bf16[16,256,128]{2,1,0:T(8,128)(2,1)S(1)}, u32[]{:S(2)}, u32[]{:S(2)}) async-start(bf16[16,256,128]{2,1,0:T(8,128)(2,1)} %get-tuple-element.354), calls=%async_computation.7 | async-start | bytes 2097152 | tf_op jit(solution)/shard_map/all_to_all | solution.py:439
  143.9 2.4 %collective-permute-start.22 = (bf16[8,64,128]{2,1,0:T(8,128)(2,1)S(1)}, bf16[8,64,128]{2,1,0:T(8,128)(2,1)S(1)}, u32[]{:S(2)}, u32[]{:S(2)}) collective-permute-start(bf16[8,64,128]{2,1,0:T(8,128)(2,1)S(1)} %get-tuple-element.342.refs_0_), channel_id=1, source_target_pairs={{0,64},{16,80},{32,96},{48,112},{64,0},{80,16},{96,32},{112,48},{1... | collective-permute-start | bytes 393224 | tf_op jit(solution)/shard_map/ppermute | solution.py:418
  146.3 2.2 %collective-permute-start.23 = (bf16[8,64,128]{2,1,0:T(8,128)(2,1)S(1)}, bf16[8,64,128]{2,1,0:T(8,128)(2,1)S(1)}, u32[]{:S(2)}, u32[]{:S(2)}) collective-permute-start(bf16[8,64,128]{2,1,0:T(8,128)(2,1)S(1)} %get-tuple-element.342.refs_0_), channel_id=1, source_target_pairs={{0,96},{16,112},{32,0},{48,16},{64,32},{80,48},{96,64},{112,80},{1... | collective-permute-start | bytes 393224 | tf_op jit(solution)/shard_map/ppermute | solution.py:418
  149.0 2.8 %collective-permute-done.22.refs_2_ = bf16[8,64,128]{2,1,0:T(8,128)(2,1)S(1)} collective-permute-done((bf16[8,64,128]{2,1,0:T(8,128)(2,1)S(1)}, bf16[8,64,128]{2,1,0:T(8,128)(2,1)S(1)}, u32[]{:S(2)}, u32[]{:S(2)}) %collective-permute-start.22) | collective-permute-done | bytes 131104 | tf_op jit(solution)/shard_map/ppermute | solution.py:418
  154.6 3.3 %products.9 = (bf16[16,256,128]{2,1,0:T(8,128)(2,1)}, f32[8,64,128]{2,1,0:T(8,128)}) custom-call(s32[128]{0:T(128)S(1)} %get-tuple-element.397.slot_ref, s32[128]{0:T(128)S(1)} %get-tuple-element.396.place_ref, s32[1]{0:T(128)} %bitcast.42.count_ref, bf16[128,128,128]{2,1,0:T(8,128)(2,1)S(1)} %copy-done.6, ...), custom_call_target="tpu_custom_call" | custom-call | tf_op jit(solution)/shard_map/products/pallas_call | solution.py:227
  158.4 6.6 %all-to-all-start.4 = ((bf16[16,256,128]{2,1,0:T(8,128)(2,1)}), bf16[16,256,128]{2,1,0:T(8,128)(2,1)S(1)}, u32[]{:S(2)}, u32[]{:S(2)}) async-start(bf16[16,256,128]{2,1,0:T(8,128)(2,1)} %get-tuple-element.345), calls=%async_computation.4 | async-start | bytes 2097152 | tf_op jit(solution)/shard_map/all_to_all | solution.py:439
  165.9 15.3 %all-to-all-done.4.got_ref = bf16[16,256,128]{2,1,0:T(8,128)(2,1)S(1)} async-done(((bf16[16,256,128]{2,1,0:T(8,128)(2,1)}), bf16[16,256,128]{2,1,0:T(8,128)(2,1)S(1)}, u32[]{:S(2)}, u32[]{:S(2)}) %all-to-all-start.4) | async-done | bytes 1048608 | tf_op jit(solution)/shard_map/all_to_all | solution.py:439
  (134 shorter events, 48.6 us)
Async XLA Ops:
  14.0 18.0 %all-to-all-start.1 = ((bf16[16,112,128]{2,1,0:T(8,128)(2,1)}), bf16[16,112,128]{2,1,0:T(8,128)(2,1)S(1)}, u32[]{:S(2)}, u32[]{:S(2)}) async-start(bf16[16,112,128]{2,1,0:T(8,128)(2,1)} %first_products.7), calls=%async_computation.1 | async-start | bytes 917504 | tf_op jit(solution)/shard_map/all_to_all | solution.py:439
  33.3 6.9 %collective-permute-start = (bf16[8,64,128]{2,1,0:T(8,128)(2,1)S(1)}, bf16[8,64,128]{2,1,0:T(8,128)(2,1)S(1)}, u32[]{:S(2)}, u32[]{:S(2)}) collective-permute-start(bf16[8,64,128]{2,1,0:T(8,128)(2,1)S(1)} %rounded.2.refs_0_), channel_id=1, source_target_pairs={{0,32},{16,48},{32,64},{48,80},{64,96},{80,112},{96,0},{112,16},{1... | collective-permute-start | bytes 393224 | tf_op jit(solution)/shard_map/ppermute | solution.py:418
  35.6 6.6 %collective-permute-start.1 = (bf16[8,64,128]{2,1,0:T(8,128)(2,1)S(1)}, bf16[8,64,128]{2,1,0:T(8,128)(2,1)S(1)}, u32[]{:S(2)}, u32[]{:S(2)}) collective-permute-start(bf16[8,64,128]{2,1,0:T(8,128)(2,1)S(1)} %rounded.2.refs_0_), channel_id=1, source_target_pairs={{0,64},{16,80},{32,96},{48,112},{64,0},{80,16},{96,32},{112,48},{1... | collective-permute-start | bytes 393224 | tf_op jit(solution)/shard_map/ppermute | solution.py:418
  35.8 7.3 %collective-permute-start.2 = (bf16[8,64,128]{2,1,0:T(8,128)(2,1)S(1)}, bf16[8,64,128]{2,1,0:T(8,128)(2,1)S(1)}, u32[]{:S(2)}, u32[]{:S(2)}) collective-permute-start(bf16[8,64,128]{2,1,0:T(8,128)(2,1)S(1)} %rounded.2.refs_0_), channel_id=1, source_target_pairs={{0,96},{16,112},{32,0},{48,16},{64,32},{80,48},{96,64},{112,80},{1... | collective-permute-start | bytes 393224 | tf_op jit(solution)/shard_map/ppermute | solution.py:418
  37.9 5.2 %collective-permute-start.3 = (bf16[8,64,128]{2,1,0:T(8,128)(2,1)S(1)}, bf16[8,64,128]{2,1,0:T(8,128)(2,1)S(1)}, u32[]{:S(2)}, u32[]{:S(2)}) collective-permute-start(bf16[8,64,128]{2,1,0:T(8,128)(2,1)S(1)} %rounded.2.refs_0_), channel_id=1, source_target_pairs={{0,16},{16,0},{32,48},{48,32},{64,80},{80,64},{96,112},{112,96},{1... | collective-permute-start | bytes 393224 | tf_op jit(solution)/shard_map/ppermute | solution.py:419
  47.7 20.7 %all-to-all-start.5 = ((bf16[16,256,128]{2,1,0:T(8,128)(2,1)}), bf16[16,256,128]{2,1,0:T(8,128)(2,1)S(1)}, u32[]{:S(2)}, u32[]{:S(2)}) async-start(bf16[16,256,128]{2,1,0:T(8,128)(2,1)} %get-tuple-element.335), calls=%async_computation.5 | async-start | bytes 2097152 | tf_op jit(solution)/shard_map/all_to_all | solution.py:439
  52.1 5.9 %collective-permute-start.7 = (bf16[8,64,128]{2,1,0:T(8,128)(2,1)S(1)}, bf16[8,64,128]{2,1,0:T(8,128)(2,1)S(1)}, u32[]{:S(2)}, u32[]{:S(2)}) collective-permute-start(bf16[8,64,128]{2,1,0:T(8,128)(2,1)S(1)} %rounded.3.refs_0_), channel_id=1, source_target_pairs={{0,32},{16,48},{32,64},{48,80},{64,96},{80,112},{96,0},{112,16},{1... | collective-permute-start | bytes 393224 | tf_op jit(solution)/shard_map/ppermute | solution.py:418
  53.5 7.9 %collective-permute-start.8 = (bf16[8,64,128]{2,1,0:T(8,128)(2,1)S(1)}, bf16[8,64,128]{2,1,0:T(8,128)(2,1)S(1)}, u32[]{:S(2)}, u32[]{:S(2)}) collective-permute-start(bf16[8,64,128]{2,1,0:T(8,128)(2,1)S(1)} %rounded.3.refs_0_), channel_id=1, source_target_pairs={{0,64},{16,80},{32,96},{48,112},{64,0},{80,16},{96,32},{112,48},{1... | collective-permute-start | bytes 393224 | tf_op jit(solution)/shard_map/ppermute | solution.py:418
  54.6 7.5 %collective-permute-start.9 = (bf16[8,64,128]{2,1,0:T(8,128)(2,1)S(1)}, bf16[8,64,128]{2,1,0:T(8,128)(2,1)S(1)}, u32[]{:S(2)}, u32[]{:S(2)}) collective-permute-start(bf16[8,64,128]{2,1,0:T(8,128)(2,1)S(1)} %rounded.3.refs_0_), channel_id=1, source_target_pairs={{0,96},{16,112},{32,0},{48,16},{64,32},{80,48},{96,64},{112,80},{1... | collective-permute-start | bytes 393224 | tf_op jit(solution)/shard_map/ppermute | solution.py:418
  56.7 5.4 %collective-permute-start.10 = (bf16[8,64,128]{2,1,0:T(8,128)(2,1)S(1)}, bf16[8,64,128]{2,1,0:T(8,128)(2,1)S(1)}, u32[]{:S(2)}, u32[]{:S(2)}) collective-permute-start(bf16[8,64,128]{2,1,0:T(8,128)(2,1)S(1)} %rounded.3.refs_0_), channel_id=1, source_target_pairs={{0,16},{16,0},{32,48},{48,32},{64,80},{80,64},{96,112},{112,96},{1... | collective-permute-start | bytes 393224 | tf_op jit(solution)/shard_map/ppermute | solution.py:419
  68.3 21.6 %all-to-all-start.2 = ((bf16[16,256,128]{2,1,0:T(8,128)(2,1)}), bf16[16,256,128]{2,1,0:T(8,128)(2,1)S(1)}, u32[]{:S(2)}, u32[]{:S(2)}) async-start(bf16[16,256,128]{2,1,0:T(8,128)(2,1)} %get-tuple-element.337), calls=%async_computation.2 | async-start | bytes 2097152 | tf_op jit(solution)/shard_map/all_to_all | solution.py:439
  74.7 5.9 %collective-permute-start.28 = (bf16[8,64,128]{2,1,0:T(8,128)(2,1)S(1)}, bf16[8,64,128]{2,1,0:T(8,128)(2,1)S(1)}, u32[]{:S(2)}, u32[]{:S(2)}) collective-permute-start(bf16[8,64,128]{2,1,0:T(8,128)(2,1)S(1)} %get-tuple-element.347.refs_0_), channel_id=1, source_target_pairs={{0,32},{16,48},{32,64},{48,80},{64,96},{80,112},{96,0},{112,16},{1... | collective-permute-start | bytes 393224 | tf_op jit(solution)/shard_map/ppermute | solution.py:418
  75.9 7.9 %collective-permute-start.29 = (bf16[8,64,128]{2,1,0:T(8,128)(2,1)S(1)}, bf16[8,64,128]{2,1,0:T(8,128)(2,1)S(1)}, u32[]{:S(2)}, u32[]{:S(2)}) collective-permute-start(bf16[8,64,128]{2,1,0:T(8,128)(2,1)S(1)} %get-tuple-element.347.refs_0_), channel_id=1, source_target_pairs={{0,64},{16,80},{32,96},{48,112},{64,0},{80,16},{96,32},{112,48},{1... | collective-permute-start | bytes 393224 | tf_op jit(solution)/shard_map/ppermute | solution.py:418
  77.7 7.6 %collective-permute-start.30 = (bf16[8,64,128]{2,1,0:T(8,128)(2,1)S(1)}, bf16[8,64,128]{2,1,0:T(8,128)(2,1)S(1)}, u32[]{:S(2)}, u32[]{:S(2)}) collective-permute-start(bf16[8,64,128]{2,1,0:T(8,128)(2,1)S(1)} %get-tuple-element.347.refs_0_), channel_id=1, source_target_pairs={{0,96},{16,112},{32,0},{48,16},{64,32},{80,48},{96,64},{112,80},{1... | collective-permute-start | bytes 393224 | tf_op jit(solution)/shard_map/ppermute | solution.py:418
  79.5 5.8 %collective-permute-start.31 = (bf16[8,64,128]{2,1,0:T(8,128)(2,1)S(1)}, bf16[8,64,128]{2,1,0:T(8,128)(2,1)S(1)}, u32[]{:S(2)}, u32[]{:S(2)}) collective-permute-start(bf16[8,64,128]{2,1,0:T(8,128)(2,1)S(1)} %get-tuple-element.347.refs_0_), channel_id=1, source_target_pairs={{0,16},{16,0},{32,48},{48,32},{64,80},{80,64},{96,112},{112,96},{1... | collective-permute-start | bytes 393224 | tf_op jit(solution)/shard_map/ppermute | solution.py:419
  80.6 4.7 %collective-permute-start.32 = (bf16[8,64,128]{2,1,0:T(8,128)(2,1)S(1)}, bf16[8,64,128]{2,1,0:T(8,128)(2,1)S(1)}, u32[]{:S(2)}, u32[]{:S(2)}) collective-permute-start(bf16[8,64,128]{2,1,0:T(8,128)(2,1)S(1)} %collective-permute-done.28.refs_1_), channel_id=1, source_target_pairs={{0,16},{16,0},{32,48},{48,32},{64,80},{80,64},{96,112},{112,96},{1... | collective-permute-start | bytes 393224 | tf_op jit(solution)/shard_map/ppermute | solution.py:419
  90.0 23.2 %all-to-all-start.6 = ((bf16[16,256,128]{2,1,0:T(8,128)(2,1)}), bf16[16,256,128]{2,1,0:T(8,128)(2,1)S(1)}, u32[]{:S(2)}, u32[]{:S(2)}) async-start(bf16[16,256,128]{2,1,0:T(8,128)(2,1)} %get-tuple-element.350), calls=%async_computation.6 | async-start | bytes 2097152 | tf_op jit(solution)/shard_map/all_to_all | solution.py:439
  98.0 6.1 %collective-permute-start.14 = (bf16[8,64,128]{2,1,0:T(8,128)(2,1)S(1)}, bf16[8,64,128]{2,1,0:T(8,128)(2,1)S(1)}, u32[]{:S(2)}, u32[]{:S(2)}) collective-permute-start(bf16[8,64,128]{2,1,0:T(8,128)(2,1)S(1)} %get-tuple-element.338.refs_0_), channel_id=1, source_target_pairs={{0,32},{16,48},{32,64},{48,80},{64,96},{80,112},{96,0},{112,16},{1... | collective-permute-start | bytes 393224 | tf_op jit(solution)/shard_map/ppermute | solution.py:418
  98.5 7.9 %collective-permute-start.15 = (bf16[8,64,128]{2,1,0:T(8,128)(2,1)S(1)}, bf16[8,64,128]{2,1,0:T(8,128)(2,1)S(1)}, u32[]{:S(2)}, u32[]{:S(2)}) collective-permute-start(bf16[8,64,128]{2,1,0:T(8,128)(2,1)S(1)} %get-tuple-element.338.refs_0_), channel_id=1, source_target_pairs={{0,64},{16,80},{32,96},{48,112},{64,0},{80,16},{96,32},{112,48},{1... | collective-permute-start | bytes 393224 | tf_op jit(solution)/shard_map/ppermute | solution.py:418
  100.4 7.5 %collective-permute-start.16 = (bf16[8,64,128]{2,1,0:T(8,128)(2,1)S(1)}, bf16[8,64,128]{2,1,0:T(8,128)(2,1)S(1)}, u32[]{:S(2)}, u32[]{:S(2)}) collective-permute-start(bf16[8,64,128]{2,1,0:T(8,128)(2,1)S(1)} %get-tuple-element.338.refs_0_), channel_id=1, source_target_pairs={{0,96},{16,112},{32,0},{48,16},{64,32},{80,48},{96,64},{112,80},{1... | collective-permute-start | bytes 393224 | tf_op jit(solution)/shard_map/ppermute | solution.py:418
  102.5 5.4 %collective-permute-start.17 = (bf16[8,64,128]{2,1,0:T(8,128)(2,1)S(1)}, bf16[8,64,128]{2,1,0:T(8,128)(2,1)S(1)}, u32[]{:S(2)}, u32[]{:S(2)}) collective-permute-start(bf16[8,64,128]{2,1,0:T(8,128)(2,1)S(1)} %get-tuple-element.338.refs_0_), channel_id=1, source_target_pairs={{0,16},{16,0},{32,48},{48,32},{64,80},{80,64},{96,112},{112,96},{1... | collective-permute-start | bytes 393224 | tf_op jit(solution)/shard_map/ppermute | solution.py:419
  113.2 22.6 %all-to-all-start.3 = ((bf16[16,256,128]{2,1,0:T(8,128)(2,1)}), bf16[16,256,128]{2,1,0:T(8,128)(2,1)S(1)}, u32[]{:S(2)}, u32[]{:S(2)}) async-start(bf16[16,256,128]{2,1,0:T(8,128)(2,1)} %get-tuple-element.341), calls=%async_computation.3 | async-start | bytes 2097152 | tf_op jit(solution)/shard_map/all_to_all | solution.py:439
  120.5 6.0 %collective-permute-start.35 = (bf16[8,64,128]{2,1,0:T(8,128)(2,1)S(1)}, bf16[8,64,128]{2,1,0:T(8,128)(2,1)S(1)}, u32[]{:S(2)}, u32[]{:S(2)}) collective-permute-start(bf16[8,64,128]{2,1,0:T(8,128)(2,1)S(1)} %get-tuple-element.351.refs_0_), channel_id=1, source_target_pairs={{0,32},{16,48},{32,64},{48,80},{64,96},{80,112},{96,0},{112,16},{1... | collective-permute-start | bytes 393224 | tf_op jit(solution)/shard_map/ppermute | solution.py:418
  121.1 7.9 %collective-permute-start.36 = (bf16[8,64,128]{2,1,0:T(8,128)(2,1)S(1)}, bf16[8,64,128]{2,1,0:T(8,128)(2,1)S(1)}, u32[]{:S(2)}, u32[]{:S(2)}) collective-permute-start(bf16[8,64,128]{2,1,0:T(8,128)(2,1)S(1)} %get-tuple-element.351.refs_0_), channel_id=1, source_target_pairs={{0,64},{16,80},{32,96},{48,112},{64,0},{80,16},{96,32},{112,48},{1... | collective-permute-start | bytes 393224 | tf_op jit(solution)/shard_map/ppermute | solution.py:418
  123.4 7.1 %collective-permute-start.37 = (bf16[8,64,128]{2,1,0:T(8,128)(2,1)S(1)}, bf16[8,64,128]{2,1,0:T(8,128)(2,1)S(1)}, u32[]{:S(2)}, u32[]{:S(2)}) collective-permute-start(bf16[8,64,128]{2,1,0:T(8,128)(2,1)S(1)} %get-tuple-element.351.refs_0_), channel_id=1, source_target_pairs={{0,96},{16,112},{32,0},{48,16},{64,32},{80,48},{96,64},{112,80},{1... | collective-permute-start | bytes 393224 | tf_op jit(solution)/shard_map/ppermute | solution.py:418
  125.2 5.3 %collective-permute-start.38 = (bf16[8,64,128]{2,1,0:T(8,128)(2,1)S(1)}, bf16[8,64,128]{2,1,0:T(8,128)(2,1)S(1)}, u32[]{:S(2)}, u32[]{:S(2)}) collective-permute-start(bf16[8,64,128]{2,1,0:T(8,128)(2,1)S(1)} %get-tuple-element.351.refs_0_), channel_id=1, source_target_pairs={{0,16},{16,0},{32,48},{48,32},{64,80},{80,64},{96,112},{112,96},{1... | collective-permute-start | bytes 393224 | tf_op jit(solution)/shard_map/ppermute | solution.py:419
  135.8 22.6 %all-to-all-start.7 = ((bf16[16,256,128]{2,1,0:T(8,128)(2,1)}), bf16[16,256,128]{2,1,0:T(8,128)(2,1)S(1)}, u32[]{:S(2)}, u32[]{:S(2)}) async-start(bf16[16,256,128]{2,1,0:T(8,128)(2,1)} %get-tuple-element.354), calls=%async_computation.7 | async-start | bytes 2097152 | tf_op jit(solution)/shard_map/all_to_all | solution.py:439
  143.1 5.7 %collective-permute-start.21 = (bf16[8,64,128]{2,1,0:T(8,128)(2,1)S(1)}, bf16[8,64,128]{2,1,0:T(8,128)(2,1)S(1)}, u32[]{:S(2)}, u32[]{:S(2)}) collective-permute-start(bf16[8,64,128]{2,1,0:T(8,128)(2,1)S(1)} %get-tuple-element.342.refs_0_), channel_id=1, source_target_pairs={{0,32},{16,48},{32,64},{48,80},{64,96},{80,112},{96,0},{112,16},{1... | collective-permute-start | bytes 393224 | tf_op jit(solution)/shard_map/ppermute | solution.py:418
  143.9 7.9 %collective-permute-start.22 = (bf16[8,64,128]{2,1,0:T(8,128)(2,1)S(1)}, bf16[8,64,128]{2,1,0:T(8,128)(2,1)S(1)}, u32[]{:S(2)}, u32[]{:S(2)}) collective-permute-start(bf16[8,64,128]{2,1,0:T(8,128)(2,1)S(1)} %get-tuple-element.342.refs_0_), channel_id=1, source_target_pairs={{0,64},{16,80},{32,96},{48,112},{64,0},{80,16},{96,32},{112,48},{1... | collective-permute-start | bytes 393224 | tf_op jit(solution)/shard_map/ppermute | solution.py:418
  146.3 7.0 %collective-permute-start.23 = (bf16[8,64,128]{2,1,0:T(8,128)(2,1)S(1)}, bf16[8,64,128]{2,1,0:T(8,128)(2,1)S(1)}, u32[]{:S(2)}, u32[]{:S(2)}) collective-permute-start(bf16[8,64,128]{2,1,0:T(8,128)(2,1)S(1)} %get-tuple-element.342.refs_0_), channel_id=1, source_target_pairs={{0,96},{16,112},{32,0},{48,16},{64,32},{80,48},{96,64},{112,80},{1... | collective-permute-start | bytes 393224 | tf_op jit(solution)/shard_map/ppermute | solution.py:418
  148.5 4.8 %collective-permute-start.24 = (bf16[8,64,128]{2,1,0:T(8,128)(2,1)S(1)}, bf16[8,64,128]{2,1,0:T(8,128)(2,1)S(1)}, u32[]{:S(2)}, u32[]{:S(2)}) collective-permute-start(bf16[8,64,128]{2,1,0:T(8,128)(2,1)S(1)} %get-tuple-element.342.refs_0_), channel_id=1, source_target_pairs={{0,16},{16,0},{32,48},{48,32},{64,80},{80,64},{96,112},{112,96},{1... | collective-permute-start | bytes 393224 | tf_op jit(solution)/shard_map/ppermute | solution.py:419
  158.4 22.9 %all-to-all-start.4 = ((bf16[16,256,128]{2,1,0:T(8,128)(2,1)}), bf16[16,256,128]{2,1,0:T(8,128)(2,1)S(1)}, u32[]{:S(2)}, u32[]{:S(2)}) async-start(bf16[16,256,128]{2,1,0:T(8,128)(2,1)} %get-tuple-element.345), calls=%async_computation.4 | async-start | bytes 2097152 | tf_op jit(solution)/shard_map/all_to_all | solution.py:439
  (30 other events, 170.2 us)
